TPU v7x, 32 devices: a whole 2x2x4 slice. The times are simulated.
32 devices in a mesh: sub: 8 (over z, x), grp: 4 (over y, core).
Axes of the slice: x: 2, y: 2, z: 4, core: 2. Of those that a mesh axis runs over, the one named last changes fastest.
Arguments:
- solution: float32 [32, 128, 2048], P(('sub', 'grp')), may hold values from -6 to 6
- residual: float32 [32, 128, 2048], P(('sub', 'grp'))
- direction: float32 [32, 128, 2048], P(('sub', 'grp'))
- residual_product: float32 [128], replicated, may hold values from 65536 to 1310720
- neighbor_slots: int32 [32, 4], P(('sub', 'grp')), may hold values from 0 to 3, each once within a row
- coupling: bfloat16 [32, 96, 256, 128], P(('sub', 'grp')), may hold values from -0.375 to 0.375
- dirichlet_factor: bfloat16 [32, 96, 128, 128], P(('sub', 'grp')), may hold values from -0.5 to 0.5
- face_block: bfloat16 [32, 32, 128, 128], P(('sub', 'grp')), as said below
- neumann_factor: bfloat16 [32, 32, 128, 128], P(('sub', 'grp')), may hold values from -0.5 to 0.5
- primal_block: int32 [32, 128], P(('sub', 'grp')), may hold values from 0 to 31
- primal_basis: bfloat16 [32, 128, 128], P(('sub', 'grp')), may hold values from -1.5 to 1.5
- coarse_matrix: float32 [32, 9, 128, 128], P(('sub', 'grp')), may hold values from -0.17677669 to 0.17677669
- coarse_block_inverse: float32 [32, 128, 128], P(('sub', 'grp')), may hold values from -0.5 to 0.5
- coarse_pattern: int32 [32, 9], P(('sub', 'grp')), may hold values from 0 to 31, as said below
Outputs:
- new_solution: float32 [32, 128, 2048], P(('sub', 'grp'))
- new_residual: float32 [32, 128, 2048], P(('sub', 'grp'))
- new_direction: float32 [32, 128, 2048], P(('sub', 'grp'))
- new_product: float32 [128], replicated
Inputs may be any that keep to these rules, and one draw needn't show every extreme that they name: `neighbor_slots`: each row orders the four local face slots: entry d is the slot of the face toward direction d (sub lower, sub upper, grp lower, grp upper). `coarse_pattern`: row t names 9 different subdomains, the first of them t itself; subdomain s lies on the device of index s along sub+grp, and every entry lies within 2 positions of row t along sub, cyclically. `face_block`: each block is symmetric with every eigenvalue at least 0.5.
All inputs are finite; a program needn't handle non-finite values.
Results may differ from a plain program's by a relative error of at most 0.0003.
Values sent between devices are 32-bit elements; how exact they have to be, the bound alone decides.
No kernel may reach another device: no remote copies, remote signals or barrier semaphores. Data moves between devices by JAX's collectives and lax.ppermute only.
A program may use at most 128 MiB of HBM per device.

v0:
```python
import jax
import jax.numpy as jnp
from jax import lax
from jax.sharding import PartitionSpec as P

REACH_SUBS = 2


highest_precision = lax.Precision.HIGHEST


def shifted(value, axis, steps):
    count = lax.axis_size(axis)
    pairs = [(source, (source + steps) % count) for source in range(count)]
    return lax.ppermute(value, axis, pairs)


def slot_table(neighbor_slots):
    return (neighbor_slots[0][:, None] == jnp.arange(4, dtype=jnp.int32)[None, :]).astype(
        jnp.float32
    )


def place_faces(directed, slot_onehot, block_width):
    load_count = directed.shape[1]
    face_width = directed.shape[2]
    placed = jnp.einsum("dk,dlf->lkf", slot_onehot, directed, precision=highest_precision)
    return placed.reshape(load_count, 4 * face_width // block_width, block_width)


def spread(owned_part, slot_onehot, block_width):
    face_width = owned_part.shape[2] // 2
    own_sub = owned_part[:, :, :face_width]
    own_grp = owned_part[:, :, face_width:]
    from_sub = shifted(own_sub, "sub", 1)
    from_grp = shifted(own_grp, "grp", 1)
    directed = jnp.stack([from_sub[0], own_sub[0], from_grp[0], own_grp[0]], 0)
    return place_faces(directed, slot_onehot, block_width)


def collect(local_part, slot_onehot):
    load_count = local_part.shape[0]
    placed = local_part.reshape(load_count, 4, -1)
    directed = jnp.einsum("dk,lkf->dlf", slot_onehot, placed, precision=highest_precision)
    to_sub = shifted(directed[0][None], "sub", -1)
    to_grp = shifted(directed[2][None], "grp", -1)
    owned_sub = directed[1][None] + to_sub
    owned_grp = directed[3][None] + to_grp
    return jnp.concatenate([owned_sub, owned_grp], 2)


def condensed(vector, couple, dirichlet, face_matrix):
    count_of_blocks = vector.shape[1]
    block_width = vector.shape[2]
    paired = jnp.concatenate(
        [
            jnp.concatenate([vector, jnp.roll(vector, -(offset + 1), axis=1)], 2)
            for offset in range(3)
        ],
        1,
    )
    interior = jnp.einsum("lib,ibk->lik", paired, couple, precision=highest_precision)
    middle = jnp.einsum("lik,ikm->lim", interior, dirichlet, precision=highest_precision)
    solved = jnp.einsum("lim,ikm->lik", middle, dirichlet, precision=highest_precision)
    returned = jnp.einsum("lik,ibk->lib", solved, couple, precision=highest_precision)
    result = jnp.einsum("ljb,jbk->ljk", vector, face_matrix, precision=highest_precision)
    for offset in range(3):
        portion = returned[:, offset * count_of_blocks : (offset + 1) * count_of_blocks]
        result = (
            result
            + portion[:, :, :block_width]
            + jnp.roll(portion[:, :, block_width:], offset + 1, axis=1)
        )
    return result


def coarse_neighbors(initial_step, pattern, matrix):
    load_count, primal_count = initial_step.shape
    grp_count = lax.axis_size("grp")
    sub_count = lax.axis_size("sub")
    reach_count = 2 * REACH_SUBS + 1
    entry_sub = pattern // grp_count
    entry_grp = pattern % grp_count
    position = (entry_sub - lax.axis_index("sub") + REACH_SUBS) % sub_count
    column = lax.all_gather(initial_step[None], "grp", axis=0, tiled=True)
    pieces = []
    for place in range(reach_count):
        if place == REACH_SUBS:
            pieces.append(column)
        else:
            pieces.append(shifted(column, "sub", REACH_SUBS - place))
    window = jnp.stack(pieces, 0).reshape(-1, load_count, primal_count)
    slot_index = position * grp_count + entry_grp
    chooser = (slot_index[:, None] == jnp.arange(window.shape[0], dtype=jnp.int32)[None, :]).astype(
        jnp.float32
    )
    chosen = jnp.einsum("kj,jlc->klc", chooser, window, precision=highest_precision)
    return jnp.einsum("klc,kcd->ld", chosen, matrix, precision=highest_precision)


def precondition(
    local_copy, slot_onehot, neumann, block_ids, primal_rows, matrix, inverse, pattern
):
    halved = local_copy * 0.5
    neumann_step = jnp.einsum("ljb,jbk->ljk", halved, neumann, precision=highest_precision)
    local_solve = jnp.einsum("ljk,jmk->ljm", neumann_step, neumann, precision=highest_precision)
    selector = (block_ids[:, None] == jnp.arange(halved.shape[1], dtype=jnp.int32)[None, :]).astype(
        jnp.float32
    )
    picked = jnp.einsum("ljb,cj->lcb", halved, selector, precision=highest_precision)
    coarse_residual = jnp.einsum("lcb,cb->lc", picked, primal_rows, precision=highest_precision)
    initial_step = jnp.dot(coarse_residual, inverse, precision=highest_precision)
    adjacent_sum = coarse_neighbors(initial_step, pattern, matrix)
    coarse_correction = initial_step + jnp.dot(
        coarse_residual - adjacent_sum, inverse, precision=highest_precision
    )
    weighted = coarse_correction[:, :, None] * primal_rows[None]
    spread_back = jnp.einsum("lcb,cj->ljb", weighted, selector, precision=highest_precision)
    return collect(0.5 * (local_solve + spread_back), slot_onehot)


def shards(
    solution,
    residual,
    direction,
    residual_product,
    neighbor_slots,
    coupling,
    dirichlet_factor,
    face_block,
    neumann_factor,
    primal_block,
    primal_basis,
    coarse_matrix,
    coarse_block_inverse,
    coarse_pattern,
):
    slot_onehot = slot_table(neighbor_slots)
    block_width = face_block.shape[2]
    couple = coupling[0].astype(jnp.float32)
    dirichlet = dirichlet_factor[0].astype(jnp.float32)
    face_matrix = face_block[0].astype(jnp.float32)
    neumann = neumann_factor[0].astype(jnp.float32)
    primal_rows = primal_basis[0].astype(jnp.float32)
    direction_local = spread(direction, slot_onehot, block_width)
    image = collect(condensed(direction_local, couple, dirichlet, face_matrix), slot_onehot)
    curvature = lax.psum(jnp.sum(direction * image, axis=(0, 2)), ("sub", "grp"))
    step_length = residual_product / curvature
    new_residual = residual - step_length[None, :, None] * image
    new_local = spread(new_residual, slot_onehot, block_width)
    preconditioned = precondition(
        new_local,
        slot_onehot,
        neumann,
        primal_block[0],
        primal_rows,
        coarse_matrix[0],
        coarse_block_inverse[0],
        coarse_pattern[0],
    )
    new_product = lax.psum(jnp.sum(new_residual * preconditioned, axis=(0, 2)), ("sub", "grp"))
    new_solution = solution + step_length[None, :, None] * direction
    step_ratio = new_product / residual_product
    new_direction = preconditioned + step_ratio[None, :, None] * direction
    return (new_solution, new_residual, new_direction, new_product)


def solution(mesh):
    in_specs = (
        P(("sub", "grp"), None, None),
        P(("sub", "grp"), None, None),
        P(("sub", "grp"), None, None),
        P(),
        P(("sub", "grp"), None),
        P(("sub", "grp"), None, None, None),
        P(("sub", "grp"), None, None, None),
        P(("sub", "grp"), None, None, None),
        P(("sub", "grp"), None, None, None),
        P(("sub", "grp"), None),
        P(("sub", "grp"), None, None),
        P(("sub", "grp"), None, None, None),
        P(("sub", "grp"), None, None),
        P(("sub", "grp"), None),
    )
    out_specs = (
        P(("sub", "grp"), None, None),
        P(("sub", "grp"), None, None),
        P(("sub", "grp"), None, None),
        P(),
    )
    return jax.shard_map(shards, mesh=mesh, in_specs=in_specs, out_specs=out_specs, check_vma=False)
```

profile of v0, /device:TPU:0, one launch (start us, length us, event | category | flops | bytes accessed | tf_op | source)
XLA Modules:
  0.0 302.9 jit_solution(3611158063502701570)
XLA Ops:
  6.3 14.4 %collective-permute-done = f32[1,128,1024]{2,0,1:T(1,128)S(1)} collective-permute-done((f32[1,128,1024]{2,0,1:T(1,128)S(1)}, f32[1,128,1024]{2,0,1:T(1,128)S(1)}, u32[]{:S(2)}, u32[]{:S(2)}) %collective-permute-start) | collective-permute-done | bytes 524320 | tf_op jit(solution)/shard_map/ppermute | solution.py:15
  20.6 5.2 %fusion.45 = f32[128,4,1024]{2,1,0:T(4,128)} fusion(f32[1,128,1024]{2,0,1:T(1,128)S(1)} %copy.71, f32[1,128,1024]{2,0,1:T(1,128)S(1)} %collective-permute-done.1, f32[1,128,1024]{2,0,1:T(1,128)S(1)} %copy.70, f32[1,128,1024]{2,0,1:T(1,128)S(1)} %collective-permute-done, s32[4]{0:T(128)S(1)} %bitcast.127), kind=kOutput, calls=%fused_computation.46 | convolution fusion | flops 26738704 | bytes 4194320 | tf_op jit(solution)/shard_map/dk,dlf->lkf/dot_general | solution.py:27
  31.9 6.1 %maximum_maximum_fusion = f32[128,96,256]{2,1,0:T(8,128)} fusion(f32[128,3,128]{2,1,0:T(4,128)S(1)} %slice.143, f32[128,29,128]{2,1,0:T(8,128)S(1)} %slice.142, f32[128,32,128]{2,1,0:T(8,128)S(1)} %copy-done.2, f32[128,2,128]{2,1,0:T(2,128)S(1)} %slice.141, f32[128,30,128]{2,1,0:T(8,128)S(1)} %slice.140, f32[128,1,128]{2,1,0:T(1,128)S(1)} %slice.139, ...), kind=kLoop, calls=%fused_computation | loop fusion | flops 25165824 | bytes 20971520 | tf_op jit(solution)/shard_map/concatenate | solution.py:55
  38.0 21.7 %fusion = f32[96,128,128]{2,1,0:T(8,128)} fusion(f32[128,96,256]{2,1,0:T(8,128)} %maximum_maximum_fusion, bf16[1,96,256,128]{3,2,1,0:T(8,128)(2,1)} %param.19), kind=kOutput, calls=%fused_computation.1 | convolution fusion | flops 4831838208 | bytes 25165824 | tf_op jit(solution)/shard_map/lib,ibk->lik/dot_general | solution.py:62
  59.7 5.3 %fusion.11 = f32[96,128,128]{2,1,0:T(8,128)S(1)} fusion(f32[96,128,128]{2,1,0:T(8,128)} %fusion, bf16[1,96,128,128]{3,2,1,0:T(8,128)(2,1)S(1)} %copy-done), kind=kOutput, calls=%fused_computation.12 | convolution fusion | flops 2415919104 | bytes 15728640 | tf_op jit(solution)/shard_map/lik,ikm->lim/dot_general | solution.py:63
  65.0 8.5 %fusion.9 = f32[96,128,128]{2,1,0:T(8,128)} fusion(f32[96,128,128]{2,1,0:T(8,128)S(1)} %fusion.11, bf16[1,96,128,128]{3,2,1,0:T(8,128)(2,1)S(1)} %copy-done), kind=kOutput, calls=%fused_computation.10 | convolution fusion | flops 2415919104 | bytes 15728640 | tf_op jit(solution)/shard_map/lim,ikm->lik/dot_general | solution.py:64
  73.5 8.4 %fusion.15 = f32[128,96,256]{0,2,1:T(8,128)S(1)} fusion(bf16[1,96,256,128]{3,2,1,0:T(8,128)(2,1)} %param.19, f32[96,128,128]{2,1,0:T(8,128)} %fusion.9), kind=kOutput, calls=%fused_computation.16 | convolution fusion | flops 4831838208 | bytes 25165824 | tf_op jit(solution)/shard_map/lik,ibk->lib/dot_general | solution.py:65
  84.1 5.4 %fusion.24 = f32[128,32,128]{0,2,1:T(8,128)} fusion(f32[128,96,256]{0,2,1:T(8,128)S(1)} %fusion.15, f32[128,31,128]{0,2,1:T(8,128)S(1)} %slice.146, f32[128,1,128]{0,2,1:T(8,128)S(1)} %slice.145, f32[128,30,128]{0,2,1:T(8,128)S(1)} %slice.149, f32[128,2,128]{0,2,1:T(8,128)S(1)} %slice.148, f32[128,29,128]{0,2,1:T(8,128)S(1)} %slice.152, ...), kind=kOutput, calls=%fused_computation.22 | convolution fusion | flops 810024960 | bytes 17825792 | tf_op jit(solution)/shard_map/ljb,jbk->ljk/dot_general | solution.py:66
  92.8 3.7 %fusion.82 = f32[4,128,1024]{2,0,1:T(4,128)S(1)} fusion(f32[128,4,1024]{2,1,0:T(4,128)} %copy.44, s32[4]{0:T(128)S(1)} %bitcast.128), kind=kOutput, calls=%fused_computation.102 | convolution fusion | flops 25165840 | bytes 4194320 | tf_op jit(solution)/shard_map/dk,lkf->dlf/dot_general | solution.py:44
  100.1 11.2 %collective-permute-done.2 = f32[1,128,1024]{2,1,0:T(8,128)S(1)} collective-permute-done((f32[1,128,1024]{2,1,0:T(8,128)S(1)}, f32[1,128,1024]{2,1,0:T(8,128)S(1)}, u32[]{:S(2)}, u32[]{:S(2)}) %collective-permute-start.2) | collective-permute-done | bytes 524320 | tf_op jit(solution)/shard_map/ppermute | solution.py:15
  111.7 39.5 %psum.14 = f32[128]{0:T(128)S(1)} all-reduce(f32[128]{0:T(128)S(1)} %multiply_reduce_fusion.1), channel_id=1, replica_groups=mesh['sub'=8,'grp'=4] {'sub','grp'}, use_global_device_ids=true, to_apply=%region_1.2 | all-reduce | flops 128 | bytes 1024 | tf_op jit(solution)/shard_map/psum | solution.py:147
  155.2 13.2 %collective-permute-done.4 = f32[1,128,1024]{2,1,0:T(8,128)S(1)} collective-permute-done((f32[1,128,1024]{2,1,0:T(8,128)S(1)}, f32[1,128,1024]{2,1,0:T(8,128)S(1)}, u32[]{:S(2)}, u32[]{:S(2)}) %collective-permute-start.4) | collective-permute-done | bytes 524320 | tf_op jit(solution)/shard_map/ppermute | solution.py:15
  171.1 4.8 %multiply_bitcast_fusion = f32[128,4,1024]{2,1,0:T(4,128)} fusion(f32[4,128,1024]{2,1,0:T(8,128)S(1)} %pad_maximum_fusion, s32[4]{0:T(128)S(1)} %bitcast.129), kind=kOutput, calls=%fused_computation.45 | convolution fusion | flops 25690128 | bytes 4194320 | tf_op jit(solution)/shard_map/dk,dlf->lkf/dot_general | solution.py:27
  181.9 11.0 %fusion.2 = f32[128,1,128]{2,1,0:T(1,128)S(1)} fusion(f32[128,128,128]{2,0,1:T(8,128)S(1)} %fusion.66, bf16[128,128,1]{1,0,2:T(8,128)(2,1)S(1)} %bitcast.126), kind=kOutput, calls=%fused_computation.3 | convolution fusion | flops 25165824 | bytes 8486912 | tf_op jit(solution)/shard_map/lcb,cb->lc/dot_general | solution.py:111
  193.1 5.8 %all-gather = f32[512,128]{1,0:T(8,128)S(1)} all-gather(f32[128,128]{1,0:T(8,128)S(1)} %fusion.61), channel_id=2, replica_groups=mesh['sub'=8,'grp'=4] {'grp'}, dimensions={0}, use_global_device_ids=true | all-gather | bytes 327680 | tf_op jit(solution)/shard_map/all_gather | solution.py:85
  199.7 4.3 %collective-permute-start.8 = (f32[4,128,128]{2,1,0:T(8,128)S(1)}, f32[4,128,128]{2,1,0:T(8,128)S(1)}, u32[]{:S(2)}, u32[]{:S(2)}) collective-permute-start(f32[4,128,128]{2,1,0:T(8,128)S(1)} %bitcast.121), channel_id=1, source_target_pairs={{0,28},{4,0},{8,4},{12,8},{16,12},{20,16},{24,20},{28,24},{1,29},{... | collective-permute-start | bytes 786440 | tf_op jit(solution)/shard_map/ppermute | solution.py:15
  205.7 3.6 %fusion.37 = f32[32,128,128]{2,1,0:T(8,128)} fusion(f32[128,32,128]{2,1,0:T(8,128)S(1)} %mul.80, bf16[1,32,128,128]{3,2,1,0:T(8,128)(2,1)S(1)} %copy-done.9), kind=kOutput, calls=%fused_computation.38 | convolution fusion | flops 805306368 | bytes 5242880 | tf_op jit(solution)/shard_map/ljb,jbk->ljk/dot_general | solution.py:105
  210.0 3.6 %collective-permute-done.7 = f32[4,128,128]{2,1,0:T(8,128)S(1)} collective-permute-done((f32[4,128,128]{2,1,0:T(8,128)S(1)}, f32[4,128,128]{2,1,0:T(8,128)S(1)}, u32[]{:S(2)}, u32[]{:S(2)}) %collective-permute-start.7) | collective-permute-done | bytes 262176 | tf_op jit(solution)/shard_map/ppermute | solution.py:15
  214.0 6.6 %collective-permute-done.9 = f32[4,128,128]{2,1,0:T(8,128)S(1)} collective-permute-done((f32[4,128,128]{2,1,0:T(8,128)S(1)}, f32[4,128,128]{2,1,0:T(8,128)S(1)}, u32[]{:S(2)}, u32[]{:S(2)}) %collective-permute-start.9) | collective-permute-done | bytes 262176 | tf_op jit(solution)/shard_map/ppermute | solution.py:15
  223.5 5.3 %fusion.5 = f32[32,128,128]{2,0,1:T(8,128)} fusion(f32[128,128]{1,0:T(8,128)S(1)} %bitcast_convert_fusion, f32[128,128]{1,0:T(8,128)S(1)} %convolution_add_fusion, s32[128]{0:T(128)S(1)} %bitcast.132), kind=kOutput, calls=%fused_computation.6 | convolution fusion | flops 807407616 | bytes 2228736 | tf_op jit(solution)/shard_map/lcb,cj->ljb/dot_general | solution.py:118
  232.0 5.5 %add_multiply_fusion = f32[32,128,128]{1,2,0:T(8,128)} fusion(f32[32,128,128]{1,2,0:T(8,128)} %copy.51, f32[32,128,128]{2,1,0:T(8,128)S(1)} %copy-done.6, bf16[1,32,128,128]{3,2,1,0:T(8,128)(2,1)} %param.22), kind=kOutput, calls=%fused_computation.44 | convolution fusion | flops 806354944 | bytes 7340032 | tf_op jit(solution)/shard_map/ljk,jmk->ljm/dot_general | solution.py:106
  240.6 3.7 %fusion.80 = f32[4,128,1024]{2,0,1:T(4,128)S(1)} fusion(f32[128,4,1024]{2,1,0:T(4,128)} %copy.52, s32[4]{0:T(128)S(1)} %bitcast.130), kind=kOutput, calls=%fused_computation.101 | convolution fusion | flops 25165840 | bytes 4194320 | tf_op jit(solution)/shard_map/dk,lkf->dlf/dot_general | solution.py:44
  247.0 12.8 %collective-permute-done.10 = f32[1,128,1024]{2,1,0:T(8,128)S(1)} collective-permute-done((f32[1,128,1024]{2,1,0:T(8,128)S(1)}, f32[1,128,1024]{2,1,0:T(8,128)S(1)}, u32[]{:S(2)}, u32[]{:S(2)}) %collective-permute-start.10) | collective-permute-done | bytes 524320 | tf_op jit(solution)/shard_map/ppermute | solution.py:15
  261.0 38.0 %psum.15 = f32[128]{0:T(128)S(1)} all-reduce(f32[128]{0:T(128)S(1)} %multiply_reduce_fusion), channel_id=1, replica_groups=mesh['sub'=8,'grp'=4] {'sub','grp'}, use_global_device_ids=true, to_apply=%region_3.4 | all-reduce | flops 128 | bytes 1024 | tf_op jit(solution)/shard_map/psum | solution.py:161
  (111 shorter events, 53.9 us)
Async XLA Ops:
  0.6 59.0 %copy-start = (bf16[1,96,128,128]{3,2,1,0:T(8,128)(2,1)S(1)}, bf16[1,96,128,128]{3,2,1,0:T(8,128)(2,1)}, u32[]{:S(2)}) copy-start(bf16[1,96,128,128]{3,2,1,0:T(8,128)(2,1)} %param.20) | copy-start | bytes 9437188
  0.6 20.0 %copy-start.17 = (s32[1,4]{1,0:T(1,128)S(1)}, s32[1,4]{1,0:T(1,128)}, u32[]{:S(2)}) copy-start(s32[1,4]{1,0:T(1,128)} %param.18) | copy-start | bytes 52
  2.6 18.0 %collective-permute-start = (f32[1,128,1024]{2,0,1:T(1,128)S(1)}, f32[1,128,1024]{2,0,1:T(1,128)S(1)}, u32[]{:S(2)}, u32[]{:S(2)}) collective-permute-start(f32[1,128,1024]{2,0,1:T(1,128)S(1)} %copy.70), channel_id=1, source_target_pairs={{0,4},{4,8},{8,12},{12,16},{16,20},{20,24},{24,28},{28,0},{1,5},{5... | collective-permute-start | bytes 1572872 | tf_op jit(solution)/shard_map/ppermute | solution.py:15
  6.2 14.4 %collective-permute-start.1 = (f32[1,128,1024]{2,0,1:T(1,128)S(1)}, f32[1,128,1024]{2,0,1:T(1,128)S(1)}, u32[]{:S(2)}, u32[]{:S(2)}) collective-permute-start(f32[1,128,1024]{2,0,1:T(1,128)S(1)} %copy.71), channel_id=1, source_target_pairs={{0,1},{1,2},{2,3},{3,0},{4,5},{5,6},{6,7},{7,4},{8,9},{9,10},{10,1... | collective-permute-start | bytes 1572872 | tf_op jit(solution)/shard_map/ppermute | solution.py:15
  98.1 13.1 %collective-permute-start.2 = (f32[1,128,1024]{2,1,0:T(8,128)S(1)}, f32[1,128,1024]{2,1,0:T(8,128)S(1)}, u32[]{:S(2)}, u32[]{:S(2)}) collective-permute-start(f32[1,128,1024]{2,1,0:T(8,128)S(1)} %copy.73), channel_id=1, source_target_pairs={{0,28},{4,0},{8,4},{12,8},{16,12},{20,16},{24,20},{28,24},{1,29},{... | collective-permute-start | bytes 1572872 | tf_op jit(solution)/shard_map/ppermute | solution.py:15
  99.9 11.6 %copy-start.5 = (f32[1,128,2048]{2,1,0:T(8,128)S(1)}, f32[1,128,2048]{2,1,0:T(8,128)}, u32[]{:S(2)}) copy-start(f32[1,128,2048]{2,1,0:T(8,128)} %param.16) | copy-start | bytes 3145732
  100.0 11.4 %collective-permute-start.3 = (f32[1,128,1024]{2,1,0:T(8,128)S(1)}, f32[1,128,1024]{2,1,0:T(8,128)S(1)}, u32[]{:S(2)}, u32[]{:S(2)}) collective-permute-start(f32[1,128,1024]{2,1,0:T(8,128)S(1)} %copy.75), channel_id=1, source_target_pairs={{0,3},{1,0},{2,1},{3,2},{4,7},{5,4},{6,5},{7,6},{8,11},{9,8},{10,9... | collective-permute-start | bytes 1572872 | tf_op jit(solution)/shard_map/ppermute | solution.py:15
  111.4 39.9 %copy-start.20 = (f32[128]{0:T(128)S(1)}, f32[128]{0:T(128)}, u32[]{:S(2)}) copy-start(f32[128]{0:T(128)} %param.17) | copy-start | bytes 1540
  151.3 3.9 %copy-start.19 = (s32[1,9]{1,0:T(1,128)S(1)}, s32[1,9]{1,0:T(1,128)}, u32[]{:S(2)}) copy-start(s32[1,9]{1,0:T(1,128)} %param.27) | copy-start | bytes 112
  151.3 3.9 %copy-start.15 = (bf16[1,128,128]{2,1,0:T(8,128)(2,1)S(1)}, bf16[1,128,128]{2,1,0:T(8,128)(2,1)}, u32[]{:S(2)}) copy-start(bf16[1,128,128]{2,1,0:T(8,128)(2,1)} %param.24) | copy-start | bytes 98308
  152.7 107.4 %copy-start.4 = (f32[1,128,2048]{2,1,0:T(8,128)}, f32[1,128,2048]{2,1,0:T(8,128)S(1)}, u32[]{:S(2)}) copy-start(f32[1,128,2048]{2,1,0:T(8,128)S(1)} %multiply_subtract_fusion) | copy-start | bytes 3145732
  152.8 15.6 %copy-start.10 = (f32[1,128,1024]{2,1,0:T(8,128)}, f32[1,128,1024]{2,1,0:T(8,128)S(1)}, u32[]{:S(2)}) copy-start(f32[1,128,1024]{2,1,0:T(8,128)S(1)} %get-tuple-element.18) | copy-start | bytes 1572868
  152.9 15.6 %copy-start.11 = (f32[1,128,1024]{2,1,0:T(8,128)}, f32[1,128,1024]{2,1,0:T(8,128)S(1)}, u32[]{:S(2)}) copy-start(f32[1,128,1024]{2,1,0:T(8,128)S(1)} %get-tuple-element.19) | copy-start | bytes 1572868
  152.9 15.6 %collective-permute-start.4 = (f32[1,128,1024]{2,1,0:T(8,128)S(1)}, f32[1,128,1024]{2,1,0:T(8,128)S(1)}, u32[]{:S(2)}, u32[]{:S(2)}) collective-permute-start(f32[1,128,1024]{2,1,0:T(8,128)S(1)} %get-tuple-element.18), channel_id=1, source_target_pairs={{0,4},{4,8},{8,12},{12,16},{16,20},{20,24},{24,28},{28,0},{1,5},{5... | collective-permute-start | bytes 1572872 | tf_op jit(solution)/shard_map/ppermute | solution.py:15
  155.2 14.1 %collective-permute-start.5 = (f32[1,128,1024]{2,1,0:T(8,128)S(1)}, f32[1,128,1024]{2,1,0:T(8,128)}, u32[]{:S(2)}, u32[]{:S(2)}) collective-permute-start(f32[1,128,1024]{2,1,0:T(8,128)S(1)} %get-tuple-element.19), channel_id=1, source_target_pairs={{0,1},{1,2},{2,3},{3,0},{4,5},{5,6},{6,7},{7,4},{8,9},{9,10},{10,1... | collective-permute-start | bytes 1572872 | tf_op jit(solution)/shard_map/ppermute | solution.py:15
  181.8 11.0 %copy-start.16 = (f32[1,128,128]{2,1,0:T(8,128)S(1)}, f32[1,128,128]{2,1,0:T(8,128)}, u32[]{:S(2)}) copy-start(f32[1,128,128]{2,1,0:T(8,128)} %param.26) | copy-start | bytes 196612
  181.9 23.8 %copy-start.9 = (bf16[1,32,128,128]{3,2,1,0:T(8,128)(2,1)S(1)}, bf16[1,32,128,128]{3,2,1,0:T(8,128)(2,1)}, u32[]{:S(2)}) copy-start(bf16[1,32,128,128]{3,2,1,0:T(8,128)(2,1)} %param.22) | copy-start | bytes 3145732
  198.9 11.1 %collective-permute-start.6 = (f32[4,128,128]{2,1,0:T(8,128)S(1)}, f32[4,128,128]{2,1,0:T(8,128)S(1)}, u32[]{:S(2)}, u32[]{:S(2)}) collective-permute-start(f32[4,128,128]{2,1,0:T(8,128)S(1)} %bitcast.119), channel_id=1, source_target_pairs={{0,8},{4,12},{8,16},{12,20},{16,24},{20,28},{24,0},{28,4},{1,9},{5... | collective-permute-start | bytes 786440 | tf_op jit(solution)/shard_map/ppermute | solution.py:15
  199.2 14.4 %collective-permute-start.7 = (f32[4,128,128]{2,1,0:T(8,128)S(1)}, f32[4,128,128]{2,1,0:T(8,128)S(1)}, u32[]{:S(2)}, u32[]{:S(2)}) collective-permute-start(f32[4,128,128]{2,1,0:T(8,128)S(1)} %bitcast.120), channel_id=1, source_target_pairs={{0,4},{4,8},{8,12},{12,16},{16,20},{20,24},{24,28},{28,0},{1,5},{5... | collective-permute-start | bytes 786440 | tf_op jit(solution)/shard_map/ppermute | solution.py:15
  199.7 14.3 %collective-permute-start.8 = (f32[4,128,128]{2,1,0:T(8,128)S(1)}, f32[4,128,128]{2,1,0:T(8,128)S(1)}, u32[]{:S(2)}, u32[]{:S(2)}) collective-permute-start(f32[4,128,128]{2,1,0:T(8,128)S(1)} %bitcast.121), channel_id=1, source_target_pairs={{0,28},{4,0},{8,4},{12,8},{16,12},{20,16},{24,20},{28,24},{1,29},{... | collective-permute-start | bytes 786440 | tf_op jit(solution)/shard_map/ppermute | solution.py:15
  204.0 16.6 %collective-permute-start.9 = (f32[4,128,128]{2,1,0:T(8,128)S(1)}, f32[4,128,128]{2,1,0:T(8,128)S(1)}, u32[]{:S(2)}, u32[]{:S(2)}) collective-permute-start(f32[4,128,128]{2,1,0:T(8,128)S(1)} %bitcast.122), channel_id=1, source_target_pairs={{0,24},{4,28},{8,0},{12,4},{16,8},{20,12},{24,16},{28,20},{1,25},{... | collective-permute-start | bytes 786440 | tf_op jit(solution)/shard_map/ppermute | solution.py:15
  213.7 8.4 %copy-start.13 = (f32[1,9,128,128]{3,2,1,0:T(8,128)S(1)}, f32[1,9,128,128]{3,2,1,0:T(8,128)}, u32[]{:S(2)}) copy-start(f32[1,9,128,128]{3,2,1,0:T(8,128)} %param.25) | copy-start | bytes 1769476
  245.9 13.9 %collective-permute-start.10 = (f32[1,128,1024]{2,1,0:T(8,128)S(1)}, f32[1,128,1024]{2,1,0:T(8,128)S(1)}, u32[]{:S(2)}, u32[]{:S(2)}) collective-permute-start(f32[1,128,1024]{2,1,0:T(8,128)S(1)} %copy.77), channel_id=1, source_target_pairs={{0,28},{4,0},{8,4},{12,8},{16,12},{20,16},{24,20},{28,24},{1,29},{... | collective-permute-start | bytes 1572872 | tf_op jit(solution)/shard_map/ppermute | solution.py:15
  246.2 13.7 %collective-permute-start.11 = (f32[1,128,1024]{2,1,0:T(8,128)S(1)}, f32[1,128,1024]{2,1,0:T(8,128)S(1)}, u32[]{:S(2)}, u32[]{:S(2)}) collective-permute-start(f32[1,128,1024]{2,1,0:T(8,128)S(1)} %copy.79), channel_id=1, source_target_pairs={{0,3},{1,0},{2,1},{3,2},{4,7},{5,4},{6,5},{7,6},{8,11},{9,8},{10,9... | collective-permute-start | bytes 1572872 | tf_op jit(solution)/shard_map/ppermute | solution.py:15
  (10 other events, 20.9 us)
where the time goes:
time: 308 us; the launch traced here: 303 us
  matrix products  98.6 us (32%)
  blocking collectives  83.4 us (27%)
  waiting for transfers between devices  62.8 us (20%)
  local copies, waits for them, and re-layouts  27.9 us (9%)
  starting transfers between devices  15 us (5%)
  other arithmetic  13.8 us (4%)
    ppermute x12, waiting for transfers between devices, shifted(): return lax.ppermute(value, axis, pairs)  62.8 us
    psum x1, blocking collectives, shards(): lax.psum(jnp.sum(direction * image, axis=(0, 2)), ('sub', 'grp'))  39.5 us
    psum x1, blocking collectives, shards(): lax.psum(jnp.sum(new_residual * preconditioned, axis=(0, 2)), ('sub', 'gr...  38 us
    dot_general x1, matrix products, condensed(): jnp.einsum('lib,ibk->lik', paired, couple, precision=highest_precision)  21.7 us
    ppermute x12, starting transfers between devices, shifted(): return lax.ppermute(value, axis, pairs)  15 us
    dot_general x1, matrix products, precondition(): jnp.einsum('lcb,cb->lc', picked, primal_rows, precision=highest_precision)  11 us
    dot_general x2, matrix products, place_faces(): jnp.einsum('dk,dlf->lkf', slot_onehot, directed, precision=highest_precis...  9.93 us
    dot_general x1, matrix products, condensed(): jnp.einsum('lim,ikm->lik', middle, dirichlet, precision=highest_precision)  8.47 us
  transfers between devices with their start and end apart: 12, of which 8 were waited for; matrix products, arithmetic and copies ran while one was open for 2% of the time, Pallas kernels for 0%

commit v1 on v0

v1 whole, which is shorter than its diff:
```python
import functools

import jax
import jax.numpy as jnp
from jax import lax
from jax.experimental import pallas as pl
from jax.experimental.pallas import tpu as pltpu
from jax.sharding import PartitionSpec as P

REACH_SUBS = 2
F32 = jnp.float32
BF16 = jnp.bfloat16
VMEM = pl.BlockSpec(memory_space=pltpu.VMEM)
SMEM = pl.BlockSpec(memory_space=pltpu.SMEM)
NN = (((1,), (0,)), ((), ()))
NT = (((1,), (1,)), ((), ()))


def shifted(value, axis, steps):
    count = lax.axis_size(axis)
    pairs = [(source, (source + steps) % count) for source in range(count)]
    return lax.ppermute(value, axis, pairs)


def total(value, axis):
    count = lax.axis_size(axis)
    if count & (count - 1):
        return lax.psum(value, axis)
    bit = 1
    while bit < count:
        value = value + lax.ppermute(value, axis, [(i, i ^ bit) for i in range(count)])
        bit *= 2
    return value


def grand_total(value):
    return total(total(value, "grp"), "sub")


def split(value):
    high = value.astype(BF16)
    low = (value - high.astype(F32)).astype(BF16)
    return high, low


def mm(a, b, dims=NN):
    return lax.dot_general(a, b, dims, preferred_element_type=F32)


def mm3(a, b):
    a_high, a_low = split(a)
    b_high, b_low = split(b)
    return mm(a_high, b_high) + (mm(a_low, b_high) + mm(a_high, b_low))


def twice(value, axis):
    return jnp.concatenate([value, value], axis=axis)


def row_sums(partial):
    ones = jnp.ones((8, partial.shape[1]), F32)
    return lax.dot_general(ones, partial, NT, precision=lax.Precision.HIGHEST, preferred_element_type=F32)


def per_row(row, width):
    tall = jnp.broadcast_to(row[0:1], (width, row.shape[1]))
    return tall.T


def call(body, out_shapes, name, flops, moved, scratch=(), grid=None, in_specs=None, out_specs=None, limit=None):
    params = {}
    if limit is not None:
        params["vmem_limit_bytes"] = limit
    kwargs = {}
    if grid is not None:
        kwargs["grid"] = grid
    return pl.pallas_call(
        body,
        out_shape=out_shapes,
        in_specs=in_specs,
        out_specs=out_specs,
        scratch_shapes=scratch,
        compiler_params=pltpu.CompilerParams(**params),
        cost_estimate=pl.CostEstimate(flops=flops, bytes_accessed=moved, transcendentals=0),
        name=name,
        **kwargs,
    )


def assemble_body(blocks, couple_ref, dirichlet_ref, face_ref, high_ref, low_ref, diag_ref):
    step = pl.program_id(0)
    pairs = blocks // 2
    width = face_ref.shape[1]
    reach = couple_ref.shape[0]

    @pl.when(step == 0)
    def _():
        diag_ref[...] = face_ref[...].astype(F32)

    def put(pair, row, half, value):
        high, low = split(value)
        rows = pl.ds(row * width, width)
        cols = pl.ds(half * width, width)
        high_ref[pair, rows, cols] = high
        low_ref[pair, rows, cols] = low

    zero = jnp.zeros((width, width), BF16)
    for ref in (high_ref, low_ref):
        ref[step, pl.ds((2 * reach + 1) * width, width), pl.ds(0, width)] = zero
        ref[step, pl.ds(0, width), pl.ds(width, width)] = zero
    own = [0.0, 0.0]
    for side in range(2):
        own_sum = None
        for q in range(reach):
            couple = couple_ref[q, side]
            factor = dirichlet_ref[q, side]
            inner_high, inner_low = split(mm(factor, factor, NT))
            middle = mm(twice(couple, 1), jnp.concatenate([inner_high, inner_low], 0))
            middle_high, middle_low = split(middle)
            full = mm(jnp.concatenate([middle_high, middle_low], 1), twice(couple, 1), NT)
            near = full[:width, :width]
            far = full[width:, width:]
            own_sum = near if own_sum is None else own_sum + near
            reached = side + q + 1
            half = reached % 2
            pair = lax.rem(step + reached // 2, pairs)
            put(pair, reach - (q + 1) + half, half, full[:width, width:])
            put(step, reach + (q + 1) + side, side, full[width:, :width])
            other = lax.rem(2 * step + reached, blocks)
            diag_ref[other] += far
        diag_ref[2 * step + side] += own_sum

    def finish(pair):
        for side in range(2):
            put(pair, reach + side, side, diag_ref[2 * pair + side])

    first = (reach + 1) // 2

    @pl.when(step >= first)
    def _():
        finish(step)

    @pl.when(step == pairs - 1)
    def _():
        for pair in range(first):
            finish(pair)


def assemble(coupling, dirichlet, face):
    blocks, width, _ = face.shape
    reach = coupling.shape[0] // blocks
    pairs = blocks // 2
    couple = coupling.reshape(reach, blocks, 2 * width, width)
    factor = dirichlet.reshape(reach, blocks, width, width)
    depth = (2 * reach + 2) * width
    shape = jax.ShapeDtypeStruct((pairs, depth, 2 * width), BF16)
    whole = pl.BlockSpec((pairs, depth, 2 * width), lambda i: (0, 0, 0))
    return call(
        functools.partial(assemble_body, blocks),
        (shape, shape),
        "assemble",
        flops=reach * blocks * 2 * width**3 * 12,
        moved=coupling.size * 3,
        scratch=[pltpu.VMEM((blocks, width, width), F32)],
        grid=(pairs,),
        in_specs=[
            pl.BlockSpec((reach, 2, 2 * width, width), lambda i: (0, i, 0, 0)),
            pl.BlockSpec((reach, 2, width, width), lambda i: (0, i, 0, 0)),
            pl.BlockSpec((blocks, width, width), lambda i: (0, 0, 0)),
        ],
        out_specs=(whole, whole),
        limit=ASSEMBLE_LIMIT,
    )(couple, factor, face)


ASSEMBLE_LIMIT = 28 * 1024 * 1024


def apply_body(slots_ref, own_ref, from_sub_ref, from_grp_ref, high_ref, low_ref, out_ref, curve_ref, u_high, u_low):
    step = pl.program_id(0)
    pairs = pl.num_programs(0)
    width = u_high.shape[2]
    face_width = from_sub_ref.shape[1]
    per_face = face_width // width
    blocks = 4 * per_face
    reach = (high_ref.shape[1] // width - 2) // 2

    def faces():
        own = own_ref
        return (
            lambda lo, n: from_sub_ref[:, lo : lo + n],
            lambda lo, n: own[:, lo : lo + n],
            lambda lo, n: from_grp_ref[:, lo : lo + n],
            lambda lo, n: own[:, face_width + lo : face_width + lo + n],
        )

    @pl.when(step == 0)
    def _():
        for which, face in enumerate(faces()):
            slot = slots_ref[0, which]
            for b in range(per_face):
                high, low = split(face(b * width, width))
                place = slot * per_face + b + reach
                u_high[place] = high
                u_low[place] = low
        for ref in (u_high, u_low):
            for i in range(reach):
                ref[i] = ref[blocks + i]
            for i in range(reach + 1):
                ref[blocks + reach + i] = ref[reach + i]

    count = 2 * reach + 2
    high = jnp.concatenate([u_high[2 * step + i] for i in range(count)], 1)
    low = jnp.concatenate([u_low[2 * step + i] for i in range(count)], 1)
    weight = high_ref[0]
    result = mm(high, weight) + mm(low, weight) + mm(high, low_ref[0])
    pair_slot = step // (per_face // 2)
    lane = pl.multiple_of((step - pair_slot * (per_face // 2)) * 2 * width, 2 * width)
    which = jnp.int32(0)
    for d in range(1, 4):
        which = jnp.where(slots_ref[0, d] == pair_slot, d, which)
    out_ref[which, :, pl.ds(lane, 2 * width)] = result

    @pl.when(step == pairs - 1)
    def _():
        acc = jnp.zeros((out_ref.shape[1], width), F32)
        for which, face in enumerate(faces()):
            for b in range(per_face):
                acc += face(b * width, width) * out_ref[which, :, b * width : (b + 1) * width]
        curve_ref[...] = row_sums(acc)


def apply(slots, own, from_sub, from_grp, high, low):
    pairs, depth, double = high.shape
    width = double // 2
    loads, face_width = from_sub.shape
    blocks = 2 * pairs
    reach = depth // width // 2 - 1
    block = pl.BlockSpec((1, depth, double), lambda i: (i, 0, 0))
    return call(
        apply_body,
        (
            jax.ShapeDtypeStruct((4, loads, face_width), F32),
            jax.ShapeDtypeStruct((8, loads), F32),
        ),
        "apply",
        flops=pairs * depth * double * loads * 6,
        moved=high.size * 4,
        scratch=[pltpu.VMEM((blocks + 2 * reach + 1, loads, width), BF16)] * 2,
        grid=(pairs,),
        in_specs=[
            SMEM,
            pl.BlockSpec(own.shape, lambda i: (0, 0)),
            pl.BlockSpec(from_sub.shape, lambda i: (0, 0)),
            pl.BlockSpec(from_grp.shape, lambda i: (0, 0)),
            block,
            block,
        ],
        out_specs=(
            pl.BlockSpec((4, loads, face_width), lambda i: (0, 0, 0)),
            pl.BlockSpec((8, loads), lambda i: (0, 0)),
        ),
        limit=20 * 1024 * 1024,
    )(slots, own, from_sub, from_grp, high, low)


def pack_body(per_face, slots_ref, block_ref, basis_ref, factor_ref, sub_ref, grp_ref):
    width = basis_ref.shape[1]
    rows = per_face * width
    prims = basis_ref.shape[0]
    for out, which in ((sub_ref, 0), (grp_ref, 2)):
        first = slots_ref[0, which] * per_face
        for b in range(per_face):
            out[b * width : (b + 1) * width, :] = factor_ref[first + b].astype(F32)
        out[rows : rows + prims, :] = basis_ref[...].astype(F32)
        near = (block_ref[...] - first).astype(F32)
        out[rows + prims :, :] = jnp.broadcast_to(near, (8, width))


def pack(slots, blocks, basis, factor, per_face):
    prims, width = basis.shape
    shape = jax.ShapeDtypeStruct((per_face * width + prims + 8, width), F32)
    return call(
        functools.partial(pack_body, per_face),
        (shape, shape),
        "pack",
        flops=1000,
        moved=shape.size * 12,
        in_specs=[SMEM, VMEM, VMEM, VMEM],
        out_specs=(VMEM, VMEM),
        limit=8 * 1024 * 1024,
    )(slots, blocks, basis, factor)


def update_body(slots_ref, y_ref, back_sub_ref, back_grp_ref, residual_ref, curve_ref, product_ref, block_ref, basis_ref, aux_sub_ref, aux_grp_ref, residual_out, own_out, sub_out, grp_out):
    width = basis_ref.shape[1]
    prims = basis_ref.shape[0]
    face_width = back_sub_ref.shape[1]
    per_face = face_width // width
    rows = face_width
    scale = per_row(product_ref[...] / curve_ref[...], width)
    basis = basis_ref[...].astype(F32).T
    own_total = None
    for which, back, aux, out in (
        (1, back_sub_ref, aux_sub_ref, sub_out),
        (3, back_grp_ref, aux_grp_ref, grp_out),
    ):
        offset = (which // 2) * face_width
        other = aux[rows : rows + prims, :].T
        own_near = block_ref[...] - slots_ref[0, which] * per_face
        other_near = aux[rows + prims : rows + prims + 1, :]
        lefts = []
        rights = []
        for b in range(per_face):
            cols = slice(b * width, (b + 1) * width)
            image = y_ref[which, :, cols] + back[:, cols]
            fresh = residual_ref[:, offset + b * width : offset + (b + 1) * width] - scale * image
            residual_out[:, offset + b * width : offset + (b + 1) * width] = fresh
            lefts.append(fresh * 0.5)
            mine = jnp.where(own_near == b, basis, 0.0).astype(BF16)
            theirs = jnp.where(other_near == b, other, 0.0).astype(BF16)
            rights.append(jnp.concatenate([mine, theirs], 1))
        high, low = split(jnp.concatenate(lefts, 1))
        right = jnp.concatenate(rights, 0)
        both = mm(high, right) + mm(low, right)
        own = both[:, :prims]
        own_total = own if own_total is None else own_total + own
        out[...] = both[:, prims:]
    own_out[...] = own_total


def update(slots, y, back_sub, back_grp, residual, curve, product, blocks, basis, aux_sub, aux_grp):
    loads = residual.shape[0]
    prims = basis.shape[0]
    small = jax.ShapeDtypeStruct((loads, prims), F32)
    return call(
        update_body,
        (jax.ShapeDtypeStruct(residual.shape, F32), small, small, small),
        "update",
        flops=residual.size * prims * 8,
        moved=residual.size * 20,
        in_specs=[SMEM] + [VMEM] * 10,
        out_specs=(VMEM,) * 4,
        limit=16 * 1024 * 1024,
    )(slots, y, back_sub, back_grp, residual, curve, product, blocks, basis, aux_sub, aux_grp)


def first_body(own_ref, sub_ref, grp_ref, inverse_ref, coarse_out, first_out):
    coarse = own_ref[...] + sub_ref[...] + grp_ref[...]
    coarse_out[...] = coarse
    first_out[...] = mm3(coarse, inverse_ref[...])


def first_step(own, sub, grp, inverse):
    shape = jax.ShapeDtypeStruct(own.shape, F32)
    return call(
        first_body,
        (shape, shape),
        "first",
        flops=own.size * 128 * 6,
        moved=own.size * 24,
        in_specs=[VMEM] * 4,
        out_specs=(VMEM,) * 2,
        limit=4 * 1024 * 1024,
    )(own, sub, grp, inverse)


def correct_body(index_ref, window_ref, coarse_ref, first_ref, matrix_ref, inverse_ref, local_ref, out_ref, product_ref):
    acc = None
    for k in range(matrix_ref.shape[0]):
        term = mm3(window_ref[index_ref[0, k]], matrix_ref[k])
        acc = term if acc is None else acc + term
    coarse = coarse_ref[...]
    result = first_ref[...] + mm3(coarse - acc, inverse_ref[...])
    out_ref[...] = result
    product_ref[...] = row_sums(coarse * result) + local_ref[...]


def correct(index, window, coarse, first, matrix, inverse, local):
    shape = jax.ShapeDtypeStruct(first.shape, F32)
    return call(
        correct_body,
        (shape, jax.ShapeDtypeStruct((8, first.shape[0]), F32)),
        "correct",
        flops=matrix.size * 128 * 6,
        moved=window.size * 4,
        in_specs=[SMEM] + [VMEM] * 6,
        out_specs=(VMEM, VMEM),
        limit=8 * 1024 * 1024,
    )(index, window, coarse, first, matrix, inverse, local)


def local_body(slots_ref, fresh_ref, factor_ref, aux_sub_ref, aux_grp_ref, out_ref, product_ref):
    width = factor_ref.shape[1]
    half = fresh_ref.shape[1] // 2
    per_face = half // width
    acc = jnp.zeros((fresh_ref.shape[0], width), F32)
    for which, aux in ((1, aux_sub_ref), (3, aux_grp_ref)):
        base = (which // 2) * half
        first = slots_ref[0, which] * per_face
        for b in range(per_face):
            cols = slice(base + b * width, base + (b + 1) * width)
            fresh = fresh_ref[:, cols]
            high, low = split(fresh * 0.5)
            mine = factor_ref[first + b]
            theirs = aux[b * width : (b + 1) * width, :].astype(BF16)
            pair = jnp.concatenate([mine, theirs], 1)
            middle = mm(jnp.concatenate([high, low], 1), twice(pair, 0))
            middle_high, middle_low = split(middle)
            solved = mm(middle_high, pair, NT) + mm(middle_low, pair, NT)
            solved = solved * 0.5
            out_ref[:, cols] = solved
            acc += fresh * solved
    product_ref[...] = row_sums(acc)


def local_solve(slots, fresh, factor, aux_sub, aux_grp):
    return call(
        local_body,
        (jax.ShapeDtypeStruct(fresh.shape, F32), jax.ShapeDtypeStruct((8, fresh.shape[0]), F32)),
        "local",
        flops=fresh.size * 128 * 16,
        moved=fresh.size * 12,
        in_specs=[SMEM] + [VMEM] * 4,
        out_specs=(VMEM, VMEM),
        limit=10 * 1024 * 1024,
    )(slots, fresh, factor, aux_sub, aux_grp)


def spread_body(slots_ref, solved_ref, own_ref, from_sub_ref, from_grp_ref, block_ref, basis_ref, aux_sub_ref, aux_grp_ref, out_ref):
    width = basis_ref.shape[1]
    prims = basis_ref.shape[0]
    half = solved_ref.shape[1] // 2
    per_face = half // width
    rows = half
    own = own_ref[...] * 0.5
    basis = basis_ref[...]
    for which, aux, other_ref in ((1, aux_sub_ref, from_sub_ref), (3, aux_grp_ref, from_grp_ref)):
        base = (which // 2) * half
        both = jnp.concatenate([own, other_ref[...] * 0.5], 1)
        right = jnp.concatenate([basis, aux[rows : rows + prims, :].astype(BF16)], 0)
        own_near = (block_ref[...] - slots_ref[0, which] * per_face).astype(F32)
        near = jnp.concatenate([own_near, aux[rows + prims : rows + prims + 1, :]], 1)
        for b in range(per_face):
            cols = slice(base + b * width, base + (b + 1) * width)
            high, low = split(jnp.where(near == b, both, 0.0))
            out_ref[:, cols] = solved_ref[:, cols] + (mm(high, right) + mm(low, right))


def spread(slots, solved, own, from_sub, from_grp, blocks, basis, aux_sub, aux_grp):
    return call(
        spread_body,
        jax.ShapeDtypeStruct(solved.shape, F32),
        "spread",
        flops=solved.size * 128 * 8,
        moved=solved.size * 12,
        in_specs=[SMEM] + [VMEM] * 8,
        out_specs=VMEM,
        limit=10 * 1024 * 1024,
    )(slots, solved, own, from_sub, from_grp, blocks, basis, aux_sub, aux_grp)


def shards(
    solution,
    residual,
    direction,
    residual_product,
    neighbor_slots,
    coupling,
    dirichlet_factor,
    face_block,
    neumann_factor,
    primal_block,
    primal_basis,
    coarse_matrix,
    coarse_block_inverse,
    coarse_pattern,
):
    width = face_block.shape[2]
    per_face = face_block.shape[1] // 4
    face_width = per_face * width
    own = direction[0]
    basis = primal_basis[0]
    factor = neumann_factor[0]
    product = residual_product[None, :]
    grp_count = lax.axis_size("grp")
    sub_count = lax.axis_size("sub")

    from_sub = shifted(own[:, :face_width], "sub", 1)
    from_grp = shifted(own[:, face_width:], "grp", 1)
    high, low = assemble(coupling[0], dirichlet_factor[0], face_block[0])
    aux_sub, aux_grp = pack(neighbor_slots, primal_block, basis, factor, per_face)
    aux_sub = shifted(aux_sub, "sub", -1)
    aux_grp = shifted(aux_grp, "grp", -1)

    y, curve = apply(neighbor_slots, own, from_sub, from_grp, high, low)
    back_sub = shifted(y[0], "sub", -1)
    back_grp = shifted(y[2], "grp", -1)
    curve = grand_total(curve)
    fresh, part, part_sub, part_grp = update(
        neighbor_slots, y, back_sub, back_grp, residual[0], curve, product, primal_block, basis, aux_sub, aux_grp
    )
    part_sub = shifted(part_sub, "sub", 1)
    part_grp = shifted(part_grp, "grp", 1)
    coarse, first = first_step(part, part_sub, part_grp, coarse_block_inverse[0])

    entry_sub = coarse_pattern // grp_count
    entry_grp = coarse_pattern % grp_count
    position = (entry_sub - lax.axis_index("sub") + REACH_SUBS) % sub_count
    index = position * grp_count + entry_grp
    column = lax.all_gather(first[None], "grp", axis=0, tiled=True)
    pieces = []
    for place in range(2 * REACH_SUBS + 1):
        pieces.append(column if place == REACH_SUBS else shifted(column, "sub", REACH_SUBS - place))
    window = jnp.concatenate(pieces, 0)

    solved, local = local_solve(neighbor_slots, fresh, factor, aux_sub, aux_grp)
    correction, partial = correct(
        index, window, coarse, first, coarse_matrix[0], coarse_block_inverse[0], local
    )
    other_sub = shifted(correction, "sub", -1)
    other_grp = shifted(correction, "grp", -1)
    new_product = grand_total(partial)[0]
    preconditioned = spread(
        neighbor_slots, solved, correction, other_sub, other_grp, primal_block, basis, aux_sub, aux_grp
    )
    step_length = residual_product / curve[0]
    new_solution = solution + step_length[None, :, None] * direction
    step_ratio = new_product / residual_product
    new_direction = preconditioned[None] + step_ratio[None, :, None] * direction
    return (new_solution, fresh[None], new_direction, new_product)


def solution(mesh):
    in_specs = (
        P(("sub", "grp"), None, None),
        P(("sub", "grp"), None, None),
        P(("sub", "grp"), None, None),
        P(),
        P(("sub", "grp"), None),
        P(("sub", "grp"), None, None, None),
        P(("sub", "grp"), None, None, None),
        P(("sub", "grp"), None, None, None),
        P(("sub", "grp"), None, None, None),
        P(("sub", "grp"), None),
        P(("sub", "grp"), None, None),
        P(("sub", "grp"), None, None, None),
        P(("sub", "grp"), None, None),
        P(("sub", "grp"), None),
    )
    out_specs = (
        P(("sub", "grp"), None, None),
        P(("sub", "grp"), None, None),
        P(("sub", "grp"), None, None),
        P(),
    )
    return jax.shard_map(shards, mesh=mesh, in_specs=in_specs, out_specs=out_specs, check_vma=False)
```

time: 308 us -> 139 us (0.45); the launches traced: 303 us -> 139 us
  matrix products: 98.6 us -> 0 us
  blocking collectives: 83.4 us -> 5.78 us
  Pallas kernels: 0 us -> 47.1 us
  local copies, waits for them, and re-layouts: 27.9 us -> 11 us
  waiting for transfers between devices: 62.8 us -> 49.5 us
  other arithmetic: 13.8 us -> 2.15 us
  starting transfers between devices: 15 us -> 22.8 us
    dot_general x18 -> x0, matrix products: 98.6 us -> none  [the longest x1 21.7 us: condensed(): jnp.einsum('lib,ibk->lik', paired, couple, precision=highest_precision)]
    psum x2 -> x0, blocking collectives: 77.6 us -> none  [the longest x1 39.5 us: shards(): lax.psum(jnp.sum(direction * image, axis=(0, 2)), ('sub', 'grp'))]
    pallas_call x0 -> x8, Pallas kernels: none -> 47.1 us  [the longest x1 30.1 us: assemble(): call(functools.partial(assemble_body, blocks), (shape, shape), 'assemble'...]
    ppermute x12 -> x14, waiting for transfers between devices: 62.8 us -> 18.3 us  [shifted(): return lax.ppermute(value, axis, pairs)]
    ppermute x0 -> x10, waiting for transfers between devices: none -> 31.1 us  [total(): lax.ppermute(value, axis, [(i, i ^ bit) for i in range(count)])]
    reshape x3 -> x0, local copies, waits for them, and re-layouts: 9.42 us -> none  [the longest x2 6.38 us: collect(): placed = local_part.reshape(load_count, 4, -1)]
    slice x16 -> x1, local copies, waits for them, and re-layouts: 7.98 us -> 1.45 us  [shards(): from_grp = shifted(own[:, face_width:], 'grp', 1)]
    concatenate x1 -> x0, other arithmetic: 6.13 us -> none  [condensed(): jnp.concatenate([jnp.concatenate([vector, jnp.roll(vector, -(offset + 1),...]
  transfers between devices with their start and end apart: 12 -> 24, of which waited for: 8 -> 15; matrix products, arithmetic and copies ran while one was open for 2% -> 1% of each run, Pallas kernels for 0% -> 30%
where the time goes in v1:
time: 139 us
  waiting for transfers between devices  49.5 us (36%)
  Pallas kernels  47.1 us (34%)
  starting transfers between devices  22.8 us (16%)
  local copies, waits for them, and re-layouts  11 us (8%)
  blocking collectives  5.78 us (4%)
  other arithmetic  2.15 us (2%)
    ppermute x10, waiting for transfers between devices, total(): lax.ppermute(value, axis, [(i, i ^ bit) for i in range(count)])  31.1 us
    pallas_call x1, Pallas kernels, assemble(): call(functools.partial(assemble_body, blocks), (shape, shape), 'assemble'...  30.1 us
    ppermute x14, waiting for transfers between devices, shifted(): return lax.ppermute(value, axis, pairs)  18.3 us
    ppermute x14, starting transfers between devices, shifted(): return lax.ppermute(value, axis, pairs)  17.8 us
    unnamed x36, local copies, waits for them, and re-layouts  9.4 us
    pallas_call x1, Pallas kernels, apply(): call(apply_body, (jax.ShapeDtypeStruct((4, loads, face_width), F32), jax....  7.89 us
    all_gather x1, blocking collectives, shards(): column = lax.all_gather(first[None], 'grp', axis=0, tiled=True)  5.78 us
    ppermute x10, starting transfers between devices, total(): lax.ppermute(value, axis, [(i, i ^ bit) for i in range(count)])  4.94 us
  transfers between devices with their start and end apart: 24, of which 15 were waited for; matrix products, arithmetic and copies ran while one was open for 1% of the time, Pallas kernels for 30%

profile of v1, /device:TPU:0, one launch (start us, length us, event | category | flops | bytes accessed | tf_op | source)
XLA Modules:
  0.0 139.1 jit_solution(2040696335373285013)
XLA Ops:
  2.1 3.0 %collective-permute-start = (f32[128,1024]{1,0:T(8,128)S(1)}, f32[128,1024]{1,0:T(8,128)S(1)}, u32[]{:S(2)}, u32[]{:S(2)}) collective-permute-start(f32[128,1024]{1,0:T(8,128)S(1)} %get-tuple-element.43), channel_id=1, source_target_pairs={{0,4},{4,8},{8,12},{12,16},{16,20},{20,24},{24,28},{28,0},{1,5},{5... | collective-permute-start | bytes 1572872 | tf_op jit(solution)/shard_map/ppermute | solution.py:22
  7.6 3.1 %collective-permute-start.9 = (f32[1160,128]{1,0:T(8,128)S(1)}, f32[1160,128]{1,0:T(8,128)S(1)}, u32[]{:S(2)}, u32[]{:S(2)}) collective-permute-start(f32[1160,128]{1,0:T(8,128)S(1)} %get-tuple-element.24), channel_id=1, source_target_pairs={{0,28},{4,0},{8,4},{12,8},{16,12},{20,16},{24,20},{28,24},{1,29},{... | collective-permute-start | bytes 1781768 | tf_op jit(solution)/shard_map/ppermute | solution.py:22
  10.7 2.8 %copy-done.11 = bf16[1,96,256,128]{3,2,1,0:T(8,128)(2,1)S(1)} copy-done((bf16[1,96,256,128]{3,2,1,0:T(8,128)(2,1)S(1)}, bf16[1,96,256,128]{3,2,1,0:T(8,128)(2,1)}, u32[]{:S(2)}) %copy-start.11) | copy-done | bytes 6291480
  15.4 30.1 %assemble.1 = (bf16[16,1024,256]{2,1,0:T(8,128)(2,1)S(1)}, bf16[16,1024,256]{2,1,0:T(8,128)(2,1)}) custom-call(bf16[3,32,256,128]{3,2,1,0:T(8,128)(2,1)S(1)} %bitcast.36, bf16[3,32,128,128]{3,2,1,0:T(8,128)(2,1)S(1)} %bitcast.37, bf16[32,128,128]{2,1,0:T(8,128)(2,1)S(1)} %bitcast.38), custom_call_target="tpu_custom_call" | custom-call | flops 4831838208 | bytes 9437184 | tf_op jit(solution)/shard_map/assemble/pallas_call | solution.py:158
  45.5 3.4 %copy-done.1 = bf16[16,1024,256]{2,1,0:T(8,128)(2,1)S(1)} copy-done((bf16[16,1024,256]{2,1,0:T(8,128)(2,1)S(1)}, bf16[16,1024,256]{2,1,0:T(8,128)(2,1)}, u32[]{:S(2)}) %copy-start.1) | copy-done | bytes 8388632
  48.9 7.9 %apply.1 = (f32[4,128,1024]{2,1,0:T(8,128)S(1)}, f32[8,128]{1,0:T(8,128)S(1)}) custom-call(s32[1,4]{1,0:T(1,128)S(1)} %copy-done.8, f32[128,2048]{1,0:T(8,128)S(1)} %bitcast.24, f32[128,1024]{1,0:T(8,128)S(1)} %collective-permute-done.from_sub_ref, f32[128,1024]{1,0:T(8,128)S(1)} %collective-permute-done.1.from_grp_ref, ...), custom_call_target="tpu_custom_call" | custom-call | flops 3221225472 | bytes 16777216 | tf_op jit(solution)/shard_map/apply/pallas_call | solution.py:240
  56.9 2.0 %collective-permute-start.7 = (f32[128,1024]{1,0:T(8,128)S(1)}, f32[128,1024]{1,0:T(8,128)S(1)}, u32[]{:S(2)}, u32[]{:S(2)}) collective-permute-start(f32[128,1024]{1,0:T(8,128)S(1)} %get-tuple-element.39), channel_id=1, source_target_pairs={{0,28},{4,0},{8,4},{12,8},{16,12},{20,16},{24,20},{28,24},{1,29},{... | collective-permute-start | bytes 1572872 | tf_op jit(solution)/shard_map/ppermute | solution.py:22
  62.3 5.3 %collective-permute-done.3 = f32[8,128]{1,0:T(8,128)S(1)} collective-permute-done((f32[8,128]{1,0:T(8,128)S(1)}, f32[8,128]{1,0:T(8,128)S(1)}, u32[]{:S(2)}, u32[]{:S(2)}) %collective-permute-start.3) | collective-permute-done | bytes 4128 | tf_op jit(solution)/shard_map/ppermute | solution.py:31
  67.9 3.4 %collective-permute-done.4 = f32[8,128]{1,0:T(8,128)S(1)} collective-permute-done((f32[8,128]{1,0:T(8,128)S(1)}, f32[8,128]{1,0:T(8,128)S(1)}, u32[]{:S(2)}, u32[]{:S(2)}) %collective-permute-start.4) | collective-permute-done | bytes 4128 | tf_op jit(solution)/shard_map/ppermute | solution.py:31
  71.3 3.6 %collective-permute-done.5 = f32[8,128]{1,0:T(8,128)S(1)} collective-permute-done((f32[8,128]{1,0:T(8,128)S(1)}, f32[8,128]{1,0:T(8,128)S(1)}, u32[]{:S(2)}, u32[]{:S(2)}) %collective-permute-start.5) | collective-permute-done | bytes 4128 | tf_op jit(solution)/shard_map/ppermute | solution.py:31
  75.1 4.3 %collective-permute-done.6 = f32[8,128]{1,0:T(8,128)S(1)} collective-permute-done((f32[8,128]{1,0:T(8,128)S(1)}, f32[8,128]{1,0:T(8,128)S(1)}, u32[]{:S(2)}, u32[]{:S(2)}) %collective-permute-start.6) | collective-permute-done | bytes 4128 | tf_op jit(solution)/shard_map/ppermute | solution.py:31
  79.5 2.0 %update.1 = (f32[128,2048]{1,0:T(8,128)}, f32[128,128]{1,0:T(8,128)S(1)}, f32[128,128]{1,0:T(8,128)}, f32[128,128]{1,0:T(8,128)}) custom-call(s32[1,4]{1,0:T(1,128)S(1)} %copy-done.8, f32[4,128,1024]{2,1,0:T(8,128)S(1)} %get-tuple-element.23.y_ref, f32[128,1024]{1,0:T(8,128)S(1)} %collective-permute-done.7.back_sub_ref, ...), custom_call_target="tpu_custom_call" | custom-call | flops 268435456 | bytes 5242880 | tf_op jit(solution)/shard_map/update/pallas_call | solution.py:336
  81.6 7.0 %collective-permute-done.11.sub_ref = f32[128,128]{1,0:T(8,128)S(1)} collective-permute-done((f32[128,128]{1,0:T(8,128)}, f32[128,128]{1,0:T(8,128)S(1)}, u32[]{:S(2)}, u32[]{:S(2)}) %collective-permute-start.11) | collective-permute-done | bytes 65568 | tf_op jit(solution)/shard_map/ppermute | solution.py:22
  89.6 5.8 %all-gather = f32[512,128]{1,0:T(8,128)S(1)} all-gather(f32[128,128]{1,0:T(8,128)S(1)} %get-tuple-element.31.first_ref), channel_id=2, replica_groups=mesh['sub'=8,'grp'=4] {'grp'}, dimensions={0}, use_global_device_ids=true | all-gather | bytes 327680 | tf_op jit(solution)/shard_map/all_gather | solution.py:511
  96.7 2.8 %local.1 = (f32[128,2048]{1,0:T(8,128)S(1)}, f32[8,128]{1,0:T(8,128)S(1)}) custom-call(s32[1,4]{1,0:T(1,128)S(1)} %copy-done.8, f32[128,2048]{1,0:T(8,128)S(1)} %copy-done.3, bf16[32,128,128]{2,1,0:T(8,128)(2,1)S(1)} %bitcast.26, f32[1160,128]{1,0:T(8,128)S(1)} %collective-permute-done.9.aux_sub_ref, f32[1160,128]{1,0:T(8,128)S(1)} %collective-permute-done.10.aux_grp_ref), custom_call_target="tpu_custom_call" | custom-call | flops 536870912 | bytes 3145728 | tf_op jit(solution)/shard_map/local/pallas_call | solution.py:418
  99.5 4.7 %collective-permute-start.15 = (f32[4,128,128]{2,1,0:T(8,128)S(1)}, f32[4,128,128]{2,1,0:T(8,128)S(1)}, u32[]{:S(2)}, u32[]{:S(2)}) collective-permute-start(f32[4,128,128]{2,1,0:T(8,128)S(1)} %bitcast.41), channel_id=1, source_target_pairs={{0,28},{4,0},{8,4},{12,8},{16,12},{20,16},{24,20},{28,24},{1,29},{... | collective-permute-start | bytes 786440 | tf_op jit(solution)/shard_map/ppermute | solution.py:22
  104.2 2.0 %collective-permute-start.16 = (f32[4,128,128]{2,1,0:T(8,128)S(1)}, f32[4,128,128]{2,1,0:T(8,128)S(1)}, u32[]{:S(2)}, u32[]{:S(2)}) collective-permute-start(f32[4,128,128]{2,1,0:T(8,128)S(1)} %bitcast.42), channel_id=1, source_target_pairs={{0,24},{4,28},{8,0},{12,4},{16,8},{20,12},{24,16},{28,20},{1,25},{... | collective-permute-start | bytes 786440 | tf_op jit(solution)/shard_map/ppermute | solution.py:22
  106.3 3.6 %collective-permute-done.14 = f32[4,128,128]{2,1,0:T(8,128)S(1)} collective-permute-done((f32[4,128,128]{2,1,0:T(8,128)S(1)}, f32[4,128,128]{2,1,0:T(8,128)S(1)}, u32[]{:S(2)}, u32[]{:S(2)}) %collective-permute-start.14) | collective-permute-done | bytes 262176 | tf_op jit(solution)/shard_map/ppermute | solution.py:22
  109.9 3.8 %collective-permute-done.15 = f32[4,128,128]{2,1,0:T(8,128)S(1)} collective-permute-done((f32[4,128,128]{2,1,0:T(8,128)S(1)}, f32[4,128,128]{2,1,0:T(8,128)S(1)}, u32[]{:S(2)}, u32[]{:S(2)}) %collective-permute-start.15) | collective-permute-done | bytes 262176 | tf_op jit(solution)/shard_map/ppermute | solution.py:22
  113.7 3.3 %collective-permute-done.16 = f32[4,128,128]{2,1,0:T(8,128)S(1)} collective-permute-done((f32[4,128,128]{2,1,0:T(8,128)S(1)}, f32[4,128,128]{2,1,0:T(8,128)S(1)}, u32[]{:S(2)}, u32[]{:S(2)}) %collective-permute-start.16) | collective-permute-done | bytes 262176 | tf_op jit(solution)/shard_map/ppermute | solution.py:22
  120.2 3.1 %collective-permute-done.20 = f32[8,128]{1,0:T(8,128)S(1)} collective-permute-done((f32[8,128]{1,0:T(8,128)S(1)}, f32[8,128]{1,0:T(8,128)S(1)}, u32[]{:S(2)}, u32[]{:S(2)}) %collective-permute-start.20) | collective-permute-done | bytes 4128 | tf_op jit(solution)/shard_map/ppermute | solution.py:31
  123.3 3.6 %collective-permute-done.21 = f32[8,128]{1,0:T(8,128)S(1)} collective-permute-done((f32[8,128]{1,0:T(8,128)S(1)}, f32[8,128]{1,0:T(8,128)S(1)}, u32[]{:S(2)}, u32[]{:S(2)}) %collective-permute-start.21) | collective-permute-done | bytes 4128 | tf_op jit(solution)/shard_map/ppermute | solution.py:31
  127.5 3.0 %collective-permute-done.22 = f32[8,128]{1,0:T(8,128)S(1)} collective-permute-done((f32[8,128]{1,0:T(8,128)S(1)}, f32[8,128]{1,0:T(8,128)S(1)}, u32[]{:S(2)}, u32[]{:S(2)}) %collective-permute-start.22) | collective-permute-done | bytes 4128 | tf_op jit(solution)/shard_map/ppermute | solution.py:31
  132.9 2.1 %collective-permute-done.23 = f32[8,128]{1,0:T(8,128)S(1)} collective-permute-done((f32[8,128]{1,0:T(8,128)S(1)}, f32[8,128]{1,0:T(8,128)S(1)}, u32[]{:S(2)}, u32[]{:S(2)}) %collective-permute-start.23) | collective-permute-done | bytes 4128 | tf_op jit(solution)/shard_map/ppermute | solution.py:31
  (85 shorter events, 22.4 us)
Async XLA Ops:
  2.1 43.3 %collective-permute-start = (f32[128,1024]{1,0:T(8,128)S(1)}, f32[128,1024]{1,0:T(8,128)S(1)}, u32[]{:S(2)}, u32[]{:S(2)}) collective-permute-start(f32[128,1024]{1,0:T(8,128)S(1)} %get-tuple-element.43), channel_id=1, source_target_pairs={{0,4},{4,8},{8,12},{12,16},{16,20},{20,24},{24,28},{28,0},{1,5},{5... | collective-permute-start | bytes 1572872 | tf_op jit(solution)/shard_map/ppermute | solution.py:22
  5.2 40.3 %collective-permute-start.1 = (f32[128,1024]{1,0:T(8,128)S(1)}, f32[128,1024]{1,0:T(8,128)S(1)}, u32[]{:S(2)}, u32[]{:S(2)}) collective-permute-start(f32[128,1024]{1,0:T(8,128)S(1)} %get-tuple-element.42), channel_id=1, source_target_pairs={{0,1},{1,2},{2,3},{3,0},{4,5},{5,6},{6,7},{7,4},{8,9},{9,10},{10,1... | collective-permute-start | bytes 1572872 | tf_op jit(solution)/shard_map/ppermute | solution.py:22
  5.8 73.6 %collective-permute-start.10 = (f32[1160,128]{1,0:T(8,128)S(1)}, f32[1160,128]{1,0:T(8,128)S(1)}, u32[]{:S(2)}, u32[]{:S(2)}) collective-permute-start(f32[1160,128]{1,0:T(8,128)S(1)} %get-tuple-element.25), channel_id=1, source_target_pairs={{0,3},{1,0},{2,1},{3,2},{4,7},{5,4},{6,5},{7,6},{8,11},{9,8},{10,9... | collective-permute-start | bytes 1781768 | tf_op jit(solution)/shard_map/ppermute | solution.py:22
  7.6 71.8 %collective-permute-start.9 = (f32[1160,128]{1,0:T(8,128)S(1)}, f32[1160,128]{1,0:T(8,128)S(1)}, u32[]{:S(2)}, u32[]{:S(2)}) collective-permute-start(f32[1160,128]{1,0:T(8,128)S(1)} %get-tuple-element.24), channel_id=1, source_target_pairs={{0,28},{4,0},{8,4},{12,8},{16,12},{20,16},{24,20},{28,24},{1,29},{... | collective-permute-start | bytes 1781768 | tf_op jit(solution)/shard_map/ppermute | solution.py:22
  56.9 22.5 %collective-permute-start.7 = (f32[128,1024]{1,0:T(8,128)S(1)}, f32[128,1024]{1,0:T(8,128)S(1)}, u32[]{:S(2)}, u32[]{:S(2)}) collective-permute-start(f32[128,1024]{1,0:T(8,128)S(1)} %get-tuple-element.39), channel_id=1, source_target_pairs={{0,28},{4,0},{8,4},{12,8},{16,12},{20,16},{24,20},{28,24},{1,29},{... | collective-permute-start | bytes 1572872 | tf_op jit(solution)/shard_map/ppermute | solution.py:22
  58.9 20.5 %collective-permute-start.8 = (f32[128,1024]{1,0:T(8,128)S(1)}, f32[128,1024]{1,0:T(8,128)S(1)}, u32[]{:S(2)}, u32[]{:S(2)}) collective-permute-start(f32[128,1024]{1,0:T(8,128)S(1)} %get-tuple-element.38), channel_id=1, source_target_pairs={{0,3},{1,0},{2,1},{3,2},{4,7},{5,4},{6,5},{7,6},{8,11},{9,8},{10,9... | collective-permute-start | bytes 1572872 | tf_op jit(solution)/shard_map/ppermute | solution.py:22
  58.9 1.9 %collective-permute-start.2 = (f32[8,128]{1,0:T(8,128)S(1)}, f32[8,128]{1,0:T(8,128)S(1)}, u32[]{:S(2)}, u32[]{:S(2)}) collective-permute-start(f32[8,128]{1,0:T(8,128)S(1)} %get-tuple-element.22), channel_id=1, source_target_pairs={{0,1},{1,0},{2,3},{3,2},{4,5},{5,4},{6,7},{7,6},{8,9},{9,8},{10,11... | collective-permute-start | bytes 12296 | tf_op jit(solution)/shard_map/ppermute | solution.py:31
  60.8 6.8 %collective-permute-start.3 = (f32[8,128]{1,0:T(8,128)S(1)}, f32[8,128]{1,0:T(8,128)S(1)}, u32[]{:S(2)}, u32[]{:S(2)}) collective-permute-start(f32[8,128]{1,0:T(8,128)S(1)} %add.53), channel_id=1, source_target_pairs={{0,2},{1,3},{2,0},{3,1},{4,6},{5,7},{6,4},{7,5},{8,10},{9,11},{10,... | collective-permute-start | bytes 12296 | tf_op jit(solution)/shard_map/ppermute | solution.py:31
  67.7 3.6 %collective-permute-start.4 = (f32[8,128]{1,0:T(8,128)S(1)}, f32[8,128]{1,0:T(8,128)S(1)}, u32[]{:S(2)}, u32[]{:S(2)}) collective-permute-start(f32[8,128]{1,0:T(8,128)S(1)} %add.54), channel_id=1, source_target_pairs={{0,4},{4,0},{8,12},{12,8},{16,20},{20,16},{24,28},{28,24},{1,5},{5... | collective-permute-start | bytes 12296 | tf_op jit(solution)/shard_map/ppermute | solution.py:31
  71.3 3.6 %collective-permute-start.5 = (f32[8,128]{1,0:T(8,128)S(1)}, f32[8,128]{1,0:T(8,128)S(1)}, u32[]{:S(2)}, u32[]{:S(2)}) collective-permute-start(f32[8,128]{1,0:T(8,128)S(1)} %add.55), channel_id=1, source_target_pairs={{0,8},{4,12},{8,0},{12,4},{16,24},{20,28},{24,16},{28,20},{1,9},{5... | collective-permute-start | bytes 12296 | tf_op jit(solution)/shard_map/ppermute | solution.py:31
  74.9 4.5 %collective-permute-start.6 = (f32[8,128]{1,0:T(8,128)S(1)}, f32[8,128]{1,0:T(8,128)S(1)}, u32[]{:S(2)}, u32[]{:S(2)}) collective-permute-start(f32[8,128]{1,0:T(8,128)S(1)} %add.56), channel_id=1, source_target_pairs={{0,16},{4,20},{8,24},{12,28},{16,0},{20,4},{24,8},{28,12},{1,17},{... | collective-permute-start | bytes 12296 | tf_op jit(solution)/shard_map/ppermute | solution.py:31
  81.4 7.2 %collective-permute-start.11 = (f32[128,128]{1,0:T(8,128)}, f32[128,128]{1,0:T(8,128)S(1)}, u32[]{:S(2)}, u32[]{:S(2)}) collective-permute-start(f32[128,128]{1,0:T(8,128)} %get-tuple-element.29), channel_id=1, source_target_pairs={{0,4},{4,8},{8,12},{12,16},{16,20},{20,24},{24,28},{28,0},{1,5},{5... | collective-permute-start | bytes 196616 | tf_op jit(solution)/shard_map/ppermute | solution.py:22
  81.6 7.0 %collective-permute-start.12 = (f32[128,128]{1,0:T(8,128)}, f32[128,128]{1,0:T(8,128)}, u32[]{:S(2)}, u32[]{:S(2)}) collective-permute-start(f32[128,128]{1,0:T(8,128)} %get-tuple-element.30), channel_id=1, source_target_pairs={{0,1},{1,2},{2,3},{3,0},{4,5},{5,6},{6,7},{7,4},{8,9},{9,10},{10,1... | collective-permute-start | bytes 196616 | tf_op jit(solution)/shard_map/ppermute | solution.py:22
  95.4 10.8 %collective-permute-start.13 = (f32[4,128,128]{2,1,0:T(8,128)S(1)}, f32[4,128,128]{2,1,0:T(8,128)S(1)}, u32[]{:S(2)}, u32[]{:S(2)}) collective-permute-start(f32[4,128,128]{2,1,0:T(8,128)S(1)} %bitcast.39), channel_id=1, source_target_pairs={{0,8},{4,12},{8,16},{12,20},{16,24},{20,28},{24,0},{28,4},{1,9},{5... | collective-permute-start | bytes 786440 | tf_op jit(solution)/shard_map/ppermute | solution.py:22
  95.4 14.4 %collective-permute-start.14 = (f32[4,128,128]{2,1,0:T(8,128)S(1)}, f32[4,128,128]{2,1,0:T(8,128)S(1)}, u32[]{:S(2)}, u32[]{:S(2)}) collective-permute-start(f32[4,128,128]{2,1,0:T(8,128)S(1)} %bitcast.40), channel_id=1, source_target_pairs={{0,4},{4,8},{8,12},{12,16},{16,20},{20,24},{24,28},{28,0},{1,5},{5... | collective-permute-start | bytes 786440 | tf_op jit(solution)/shard_map/ppermute | solution.py:22
  99.5 14.2 %collective-permute-start.15 = (f32[4,128,128]{2,1,0:T(8,128)S(1)}, f32[4,128,128]{2,1,0:T(8,128)S(1)}, u32[]{:S(2)}, u32[]{:S(2)}) collective-permute-start(f32[4,128,128]{2,1,0:T(8,128)S(1)} %bitcast.41), channel_id=1, source_target_pairs={{0,28},{4,0},{8,4},{12,8},{16,12},{20,16},{24,20},{28,24},{1,29},{... | collective-permute-start | bytes 786440 | tf_op jit(solution)/shard_map/ppermute | solution.py:22
  104.2 12.8 %collective-permute-start.16 = (f32[4,128,128]{2,1,0:T(8,128)S(1)}, f32[4,128,128]{2,1,0:T(8,128)S(1)}, u32[]{:S(2)}, u32[]{:S(2)}) collective-permute-start(f32[4,128,128]{2,1,0:T(8,128)S(1)} %bitcast.42), channel_id=1, source_target_pairs={{0,24},{4,28},{8,0},{12,4},{16,8},{20,12},{24,16},{28,20},{1,25},{... | collective-permute-start | bytes 786440 | tf_op jit(solution)/shard_map/ppermute | solution.py:22
  118.5 1.2 collective-permute-start.19
  119.7 3.6 %collective-permute-start.20 = (f32[8,128]{1,0:T(8,128)S(1)}, f32[8,128]{1,0:T(8,128)S(1)}, u32[]{:S(2)}, u32[]{:S(2)}) collective-permute-start(f32[8,128]{1,0:T(8,128)S(1)} %add.63), channel_id=1, source_target_pairs={{0,2},{1,3},{2,0},{3,1},{4,6},{5,7},{6,4},{7,5},{8,10},{9,11},{10,... | collective-permute-start | bytes 12296 | tf_op jit(solution)/shard_map/ppermute | solution.py:31
  123.3 3.6 %collective-permute-start.21 = (f32[8,128]{1,0:T(8,128)S(1)}, f32[8,128]{1,0:T(8,128)S(1)}, u32[]{:S(2)}, u32[]{:S(2)}) collective-permute-start(f32[8,128]{1,0:T(8,128)S(1)} %add.64), channel_id=1, source_target_pairs={{0,4},{4,0},{8,12},{12,8},{16,20},{20,16},{24,28},{28,24},{1,5},{5... | collective-permute-start | bytes 12296 | tf_op jit(solution)/shard_map/ppermute | solution.py:31
  126.9 3.6 %collective-permute-start.22 = (f32[8,128]{1,0:T(8,128)S(1)}, f32[8,128]{1,0:T(8,128)S(1)}, u32[]{:S(2)}, u32[]{:S(2)}) collective-permute-start(f32[8,128]{1,0:T(8,128)S(1)} %add.65), channel_id=1, source_target_pairs={{0,8},{4,12},{8,0},{12,4},{16,24},{20,28},{24,16},{28,20},{1,9},{5... | collective-permute-start | bytes 12296 | tf_op jit(solution)/shard_map/ppermute | solution.py:31
  130.6 4.5 %collective-permute-start.23 = (f32[8,128]{1,0:T(8,128)S(1)}, f32[8,128]{1,0:T(8,128)S(1)}, u32[]{:S(2)}, u32[]{:S(2)}) collective-permute-start(f32[8,128]{1,0:T(8,128)S(1)} %add.66), channel_id=1, source_target_pairs={{0,16},{4,20},{8,24},{12,28},{16,0},{20,4},{24,8},{28,12},{1,17},{... | collective-permute-start | bytes 12296 | tf_op jit(solution)/shard_map/ppermute | solution.py:31
  132.0 4.3 %collective-permute-start.17 = (f32[128,128]{1,0:T(8,128)S(1)}, f32[128,128]{1,0:T(8,128)S(1)}, u32[]{:S(2)}, u32[]{:S(2)}) collective-permute-start(f32[128,128]{1,0:T(8,128)S(1)} %get-tuple-element.34.own_ref), channel_id=1, source_target_pairs={{0,28},{4,0},{8,4},{12,8},{16,12},{20,16},{24,20},{28,24},{1,29},{... | collective-permute-start | bytes 196616 | tf_op jit(solution)/shard_map/ppermute | solution.py:22
  132.9 3.3 %collective-permute-start.18 = (f32[128,128]{1,0:T(8,128)S(1)}, f32[128,128]{1,0:T(8,128)S(1)}, u32[]{:S(2)}, u32[]{:S(2)}) collective-permute-start(f32[128,128]{1,0:T(8,128)S(1)} %get-tuple-element.34.own_ref), channel_id=1, source_target_pairs={{0,3},{1,0},{2,1},{3,2},{4,7},{5,4},{6,5},{7,6},{8,11},{9,8},{10,9... | collective-permute-start | bytes 196616 | tf_op jit(solution)/shard_map/ppermute | solution.py:22
  (16 other events, 156.8 us)

commit v2 on v1

v2 whole, which is shorter than its diff:
```python
import functools

import jax
import jax.numpy as jnp
from jax import lax
from jax.experimental import pallas as pl
from jax.experimental.pallas import tpu as pltpu
from jax.sharding import PartitionSpec as P

REACH_SUBS = 2
F32 = jnp.float32
BF16 = jnp.bfloat16
VMEM = pl.BlockSpec(memory_space=pltpu.VMEM)
SMEM = pl.BlockSpec(memory_space=pltpu.SMEM)
NN = (((1,), (0,)), ((), ()))
NT = (((1,), (1,)), ((), ()))


def shifted(value, axis, steps):
    count = lax.axis_size(axis)
    pairs = [(source, (source + steps) % count) for source in range(count)]
    return lax.ppermute(value, axis, pairs)


def total(value, axis):
    count = lax.axis_size(axis)
    if count & (count - 1):
        return lax.psum(value, axis)
    bit = 1
    while bit < count:
        value = value + lax.ppermute(value, axis, [(i, i ^ bit) for i in range(count)])
        bit *= 2
    return value


def grand_total(value):
    return total(total(value, "grp"), "sub")


def split(value):
    high = value.astype(BF16)
    low = (value - high.astype(F32)).astype(BF16)
    return high, low


def mm(a, b, dims=NN):
    return lax.dot_general(a, b, dims, preferred_element_type=F32)


def mm3(a, b):
    a_high, a_low = split(a)
    b_high, b_low = split(b)
    return mm(a_high, b_high) + (mm(a_low, b_high) + mm(a_high, b_low))


def twice(value, axis):
    return jnp.concatenate([value, value], axis=axis)


def row_sums(partial):
    ones = jnp.ones((8, partial.shape[1]), F32)
    return lax.dot_general(ones, partial, NT, precision=lax.Precision.HIGHEST, preferred_element_type=F32)


def per_row(row, width):
    tall = jnp.broadcast_to(row[0:1], (width, row.shape[1]))
    return tall.T


def call(body, out_shapes, name, flops, moved, scratch=(), grid=None, in_specs=None, out_specs=None, limit=None):
    params = {}
    if limit is not None:
        params["vmem_limit_bytes"] = limit
    kwargs = {}
    if grid is not None:
        kwargs["grid"] = grid
    return pl.pallas_call(
        body,
        out_shape=out_shapes,
        in_specs=in_specs,
        out_specs=out_specs,
        scratch_shapes=scratch,
        compiler_params=pltpu.CompilerParams(**params),
        cost_estimate=pl.CostEstimate(flops=flops, bytes_accessed=moved, transcendentals=0),
        name=name,
        **kwargs,
    )


BATCH = 8


def assemble_body(blocks, kept, couple_hbm, factor_hbm, face_hbm, *refs):
    sources = refs[:kept]
    high_ref, low_ref = refs[kept : kept + 2]
    targets = refs[kept + 2 : 2 * kept + 2]
    couple_ref, factor_ref, face_ref, inner_ref, middle_ref, near_ref, far_ref, sems, keep_sems = refs[2 * kept + 2 :]
    width = face_ref.shape[1]
    count = couple_ref.shape[0]
    reach = count // blocks
    pairs = blocks // 2
    rounds = count // BATCH

    def copy_of(i, which):
        part = pl.ds(i * BATCH, BATCH)
        source, target = ((factor_hbm, factor_ref), (couple_hbm, couple_ref))[which]
        return pltpu.make_async_copy(source.at[part], target.at[part], sems.at[which, i])

    def begin(i, carry):
        for which in range(2):
            copy_of(i, which).start()
        return carry

    face_copy = pltpu.make_async_copy(face_hbm, face_ref, keep_sems.at[kept])
    face_copy.start()
    lax.fori_loop(0, rounds, begin, 0)
    keeping = [pltpu.make_async_copy(a, b, keep_sems.at[i]) for i, (a, b) in enumerate(zip(sources, targets))]
    for copy in keeping:
        copy.start()
    face_copy.wait()

    def convert(block, carry):
        near_ref[block] = face_ref[block].astype(F32)
        far_ref[block] = jnp.zeros((width, width), F32)
        return carry

    lax.fori_loop(0, blocks, convert, 0)
    for extra in range(reach):
        far_ref[blocks + extra] = jnp.zeros((width, width), F32)

    def inner(i):
        for k in range(BATCH):
            factor = factor_ref[i * BATCH + k]
            high, low = split(mm(factor, factor, NT))
            inner_ref[i % 2, k, :width] = high
            inner_ref[i % 2, k, width:] = low

    def middle(i):
        for k in range(BATCH):
            high, low = split(mm(twice(couple_ref[i * BATCH + k], 1), inner_ref[i % 2, k]))
            middle_ref[i % 2, k, :, :width] = high
            middle_ref[i % 2, k, :, width:] = low

    def put(pair, row, half, value):
        high, low = split(value)
        cols = pl.ds(pl.multiple_of(half * width, width), width)
        high_ref[pair, row, :, cols] = high
        low_ref[pair, row, :, cols] = low

    def outer(i):
        per = blocks // BATCH
        q = i // per
        base = (i - q * per) * BATCH
        for k in range(BATCH):
            full = mm(middle_ref[i % 2, k], twice(couple_ref[i * BATCH + k], 1), NT)
            place = base + k
            reached = place + q + 1
            near_ref[place] += full[:width, :width]
            far_ref[reached] += full[width:, width:]
            wrapped = lax.rem(reached, blocks)
            half = lax.rem(wrapped, 2)
            put(wrapped // 2, reach - 1 - q + half, half, full[:width, width:])
            side = k % 2
            put(place // 2, reach + q + 1 + side, side, full[width:, :width])

    def wait(i, which):
        copy_of(i, which).wait()

    wait(0, 0)
    inner(0)
    wait(1, 0)
    wait(0, 1)
    inner(1)
    middle(0)

    def steady(i, carry):
        wait(i, 0)
        wait(i - 1, 1)
        inner(i)
        middle(i - 1)
        outer(i - 2)
        return carry

    lax.fori_loop(2, rounds, steady, 0)
    wait(rounds - 1, 1)
    middle(rounds - 1)
    outer(rounds - 2)
    outer(rounds - 1)

    def close(pair, carry):
        zero = jnp.zeros((width, width), BF16)
        for ref in (high_ref, low_ref):
            ref[pair, 2 * reach + 1, :, pl.ds(0, width)] = zero
            ref[pair, 0, :, pl.ds(width, width)] = zero
        for side in range(2):
            put(pair, reach + side, side, near_ref[2 * pair + side] + far_ref[2 * pair + side])
        return carry

    for extra in range(reach):
        far_ref[extra] += far_ref[blocks + extra]
    lax.fori_loop(0, pairs, close, 0)
    for copy in keeping:
        copy.wait()


def in_hbm(value):
    return pltpu.with_memory_space_constraint(value, pltpu.HBM)


def assemble(coupling, dirichlet, face, keep):
    blocks, width, _ = face.shape
    count = coupling.shape[0]
    reach = count // blocks
    pairs = blocks // 2
    shape = jax.ShapeDtypeStruct((pairs, 2 * reach + 2, width, 2 * width), BF16)
    hbm = pl.BlockSpec(memory_space=pltpu.HBM)
    return call(
        functools.partial(assemble_body, blocks, len(keep)),
        (shape, shape) + tuple(jax.ShapeDtypeStruct(k.shape, k.dtype) for k in keep),
        "assemble",
        flops=count * 2 * width**3 * 12,
        moved=coupling.size * 3,
        scratch=[
            pltpu.VMEM((count, 2 * width, width), BF16),
            pltpu.VMEM((count, width, width), BF16),
            pltpu.VMEM((blocks, width, width), BF16),
            pltpu.VMEM((2, BATCH, 2 * width, width), BF16),
            pltpu.VMEM((2, BATCH, 2 * width, 2 * width), BF16),
            pltpu.VMEM((blocks, width, width), F32),
            pltpu.VMEM((blocks + reach, width, width), F32),
            pltpu.SemaphoreType.DMA((2, count // BATCH)),
            pltpu.SemaphoreType.DMA((len(keep) + 1,)),
        ],
        in_specs=[hbm] * (3 + len(keep)),
        out_specs=(VMEM,) * (2 + len(keep)),
        limit=ASSEMBLE_LIMIT,
    )(in_hbm(coupling), in_hbm(dirichlet), in_hbm(face), *(in_hbm(k) for k in keep))


ASSEMBLE_LIMIT = 22 * 1024 * 1024


def apply_body(slots_ref, own_ref, from_sub_ref, from_grp_ref, high_ref, low_ref, out_ref, curve_ref, u_high, u_low):
    pairs, count, width, _ = high_ref.shape
    reach = count // 2 - 1
    face_width = from_sub_ref.shape[1]
    per_face = face_width // width
    blocks = 2 * pairs
    loads = own_ref.shape[0]
    faces = ((from_sub_ref, 0), (own_ref, 0), (from_grp_ref, 0), (own_ref, face_width))
    for which, (ref, base) in enumerate(faces):
        slot = slots_ref[0, which]
        for b in range(per_face):
            high, low = split(ref[:, base + b * width : base + (b + 1) * width])
            place = slot * per_face + b + reach
            u_high[place] = high
            u_low[place] = low
    for ref in (u_high, u_low):
        for i in range(reach):
            ref[i] = ref[blocks + i]
        for i in range(reach + 1):
            ref[blocks + reach + i] = ref[reach + i]
    half_face = per_face // 2

    def one_face(which, carry):
        slot = slots_ref[0, which]
        for part in range(half_face):
            pair = slot * half_face + part
            high = jnp.concatenate([u_high[2 * pair + i] for i in range(count)], 1)
            low = jnp.concatenate([u_low[2 * pair + i] for i in range(count)], 1)
            weight = high_ref[pair].reshape(count * width, 2 * width)
            both = mm(jnp.concatenate([high, low], 0), weight)
            result = both[:loads] + both[loads:] + mm(high, low_ref[pair].reshape(count * width, 2 * width))
            out_ref[which, :, part * 2 * width : (part + 1) * 2 * width] = result
        return carry

    lax.fori_loop(0, 4, one_face, 0)
    acc = jnp.zeros((loads, width), F32)
    for which, (ref, base) in enumerate(faces):
        for b in range(per_face):
            acc += ref[:, base + b * width : base + (b + 1) * width] * out_ref[which, :, b * width : (b + 1) * width]
    curve_ref[...] = row_sums(acc)


def apply(slots, own, from_sub, from_grp, high, low):
    pairs, count, width, double = high.shape
    loads, face_width = from_sub.shape
    return call(
        apply_body,
        (
            jax.ShapeDtypeStruct((4, loads, face_width), F32),
            jax.ShapeDtypeStruct((8, loads), F32),
        ),
        "apply",
        flops=high.size * loads * 6,
        moved=high.size * 4,
        scratch=[pltpu.VMEM((2 * pairs + count - 1, loads, width), BF16)] * 2,
        in_specs=[SMEM] + [VMEM] * 5,
        out_specs=(VMEM, VMEM),
        limit=6 * 1024 * 1024,
    )(slots, own, from_sub, from_grp, high, low)


def pack_body(per_face, slots_ref, block_hbm, basis_hbm, factor_hbm, sub_ref, grp_ref, block_ref, basis_ref, factor_ref, sems):
    prims, width = basis_ref.shape
    rows = per_face * width
    copies = [
        pltpu.make_async_copy(basis_hbm, basis_ref, sems.at[2]),
        pltpu.make_async_copy(block_hbm, block_ref, sems.at[3]),
    ]
    for i, which in enumerate((0, 2)):
        part = pl.ds(slots_ref[0, which] * per_face, per_face)
        copies.append(pltpu.make_async_copy(factor_hbm.at[part], factor_ref.at[i], sems.at[i]))
    for copy in copies:
        copy.start()
    for copy in copies:
        copy.wait()
    for i, (out, which) in enumerate(((sub_ref, 0), (grp_ref, 2))):
        first = slots_ref[0, which] * per_face
        for b in range(per_face):
            out[b * width : (b + 1) * width, :] = factor_ref[i, b].astype(F32)
        out[rows : rows + prims, :] = basis_ref[...].astype(F32)
        near = (block_ref[...] - first).astype(F32)
        out[rows + prims :, :] = jnp.broadcast_to(near, (8, width))


def pack(slots, blocks, basis, factor, per_face):
    prims, width = basis.shape
    shape = jax.ShapeDtypeStruct((per_face * width + prims + 8, width), F32)
    hbm = pl.BlockSpec(memory_space=pltpu.HBM)
    return call(
        functools.partial(pack_body, per_face),
        (shape, shape),
        "pack",
        flops=1000,
        moved=shape.size * 12,
        scratch=[
            pltpu.VMEM(blocks.shape, jnp.int32),
            pltpu.VMEM((prims, width), BF16),
            pltpu.VMEM((2, per_face, width, width), BF16),
            pltpu.SemaphoreType.DMA((4,)),
        ],
        in_specs=[SMEM, hbm, hbm, hbm],
        out_specs=(VMEM, VMEM),
        limit=4 * 1024 * 1024,
    )(slots, in_hbm(blocks), in_hbm(basis), in_hbm(factor))


def update_body(slots_ref, y_ref, back_sub_ref, back_grp_ref, residual_ref, curve_ref, product_ref, block_ref, basis_ref, aux_sub_ref, aux_grp_ref, residual_out, half_out, own_out, sub_out, grp_out):
    width = basis_ref.shape[1]
    prims = basis_ref.shape[0]
    face_width = back_sub_ref.shape[1]
    per_face = face_width // width
    rows = face_width
    scale = per_row(product_ref[...] / curve_ref[...], width)
    basis = basis_ref[...].astype(F32).T
    own_total = None
    for which, back, aux, out in (
        (1, back_sub_ref, aux_sub_ref, sub_out),
        (3, back_grp_ref, aux_grp_ref, grp_out),
    ):
        offset = (which // 2) * face_width
        other = aux[rows : rows + prims, :].T
        own_near = block_ref[...] - slots_ref[0, which] * per_face
        other_near = aux[rows + prims : rows + prims + 1, :]
        lefts = []
        rights = []
        for b in range(per_face):
            cols = slice(b * width, (b + 1) * width)
            image = y_ref[which, :, cols] + back[:, cols]
            fresh = residual_ref[:, offset + b * width : offset + (b + 1) * width] - scale * image
            residual_out[:, offset + b * width : offset + (b + 1) * width] = fresh
            half = fresh * 0.5
            half_out[:, offset + b * width : offset + (b + 1) * width] = half
            lefts.append(half)
            mine = jnp.where(own_near == b, basis, 0.0).astype(BF16)
            theirs = jnp.where(other_near == b, other, 0.0).astype(BF16)
            rights.append(jnp.concatenate([mine, theirs], 1))
        high, low = split(jnp.concatenate(lefts, 1))
        right = jnp.concatenate(rights, 0)
        both = mm(high, right) + mm(low, right)
        own = both[:, :prims]
        own_total = own if own_total is None else own_total + own
        out[...] = both[:, prims:]
    own_out[...] = own_total


def update(slots, y, back_sub, back_grp, residual, curve, product, blocks, basis, aux_sub, aux_grp):
    loads = residual.shape[0]
    prims = basis.shape[0]
    small = jax.ShapeDtypeStruct((loads, prims), F32)
    return call(
        update_body,
        (jax.ShapeDtypeStruct(residual.shape, F32), jax.ShapeDtypeStruct(residual.shape, F32), small, small, small),
        "update",
        flops=residual.size * prims * 8,
        moved=residual.size * 20,
        in_specs=[SMEM] + [VMEM] * 10,
        out_specs=(VMEM,) * 5,
        limit=16 * 1024 * 1024,
    )(slots, y, back_sub, back_grp, residual, curve, product, blocks, basis, aux_sub, aux_grp)


def first_body(own_ref, sub_ref, grp_ref, inverse_ref, local_ref, coarse_out, first_out, local_out):
    coarse = own_ref[...] + sub_ref[...] + grp_ref[...]
    coarse_out[...] = coarse
    first_out[...] = mm3(coarse, inverse_ref[...])
    local_out[...] = local_ref[...]


def first_step(own, sub, grp, inverse, local):
    shape = jax.ShapeDtypeStruct(own.shape, F32)
    return call(
        first_body,
        (shape, shape, jax.ShapeDtypeStruct(local.shape, F32)),
        "first",
        flops=own.size * 128 * 6,
        moved=own.size * 24,
        in_specs=[VMEM] * 5,
        out_specs=(VMEM,) * 3,
        limit=4 * 1024 * 1024,
    )(own, sub, grp, inverse, local)


def merge_body(*refs):
    out_ref = refs[-1]
    for place, ref in enumerate(refs[:-1]):
        size = ref.shape[0]
        out_ref[place * size : (place + 1) * size] = ref[...]


def merge(pieces):
    size = pieces[0].shape[0]
    shape = jax.ShapeDtypeStruct((size * len(pieces),) + pieces[0].shape[1:], F32)
    return call(
        merge_body,
        shape,
        "merge",
        flops=1000,
        moved=shape.size * 8,
        in_specs=[VMEM] * len(pieces),
        out_specs=VMEM,
        limit=4 * 1024 * 1024,
    )(*pieces)


def correct_body(paired, pattern_ref, window_ref, beside_ref, coarse_ref, first_ref, matrix_ref, inverse_ref, local_ref, out_ref, product_ref, held_ref):
    size = window_ref.shape[0]
    held_ref[:size] = window_ref[...]
    held_ref[size:] = beside_ref[...]
    grp_count = lax.axis_size("grp")
    sub_count = lax.axis_size("sub")
    my_sub = lax.axis_index("sub")
    my_grp = lax.axis_index("grp")
    acc = None
    for k in range(matrix_ref.shape[0]):
        entry = pattern_ref[0, k]
        entry_sub = entry // grp_count
        entry_grp = entry - entry_sub * grp_count
        position = lax.rem(entry_sub - my_sub + REACH_SUBS + sub_count, sub_count)
        if paired:
            apart = entry_grp ^ my_grp
            index = ((apart & 1) * (2 * REACH_SUBS + 1) + position) * 2 + (apart >> 1)
        else:
            index = position * grp_count + entry_grp
        term = mm3(held_ref[index], matrix_ref[k])
        acc = term if acc is None else acc + term
    coarse = coarse_ref[...]
    result = first_ref[...] + mm3(coarse - acc, inverse_ref[...])
    out_ref[...] = result
    product_ref[...] = row_sums(coarse * result) + local_ref[...]


def correct(paired, pattern, window, beside, coarse, first, matrix, inverse, local):
    shape = jax.ShapeDtypeStruct(first.shape, F32)
    return call(
        functools.partial(correct_body, paired),
        (shape, jax.ShapeDtypeStruct((8, first.shape[0]), F32)),
        "correct",
        flops=matrix.size * 128 * 6,
        moved=window.size * 4,
        scratch=[pltpu.VMEM((window.shape[0] + beside.shape[0],) + window.shape[1:], F32)],
        in_specs=[SMEM] + [VMEM] * 7,
        out_specs=(VMEM, VMEM),
        limit=8 * 1024 * 1024,
    )(pattern, window, beside, coarse, first, matrix, inverse, local)


def local_body(slots_ref, halved_ref, factor_ref, aux_sub_ref, aux_grp_ref, out_ref, product_ref):
    width = factor_ref.shape[1]
    half = halved_ref.shape[1] // 2
    per_face = half // width
    acc = jnp.zeros((halved_ref.shape[0], width), F32)
    for which, aux in ((1, aux_sub_ref), (3, aux_grp_ref)):
        base = (which // 2) * half
        first = slots_ref[0, which] * per_face
        for b in range(per_face):
            cols = slice(base + b * width, base + (b + 1) * width)
            halved = halved_ref[:, cols]
            high, low = split(halved)
            mine = factor_ref[first + b]
            theirs = aux[b * width : (b + 1) * width, :].astype(BF16)
            pair = jnp.concatenate([mine, theirs], 1)
            middle = mm(jnp.concatenate([high, low], 1), twice(pair, 0))
            middle_high, middle_low = split(middle)
            solved = mm(middle_high, pair, NT) + mm(middle_low, pair, NT)
            out_ref[:, cols] = solved * 0.5
            acc += halved * solved
    product_ref[...] = row_sums(acc)


def local_solve(slots, fresh, factor, aux_sub, aux_grp):
    return call(
        local_body,
        (jax.ShapeDtypeStruct(fresh.shape, F32), jax.ShapeDtypeStruct((8, fresh.shape[0]), F32)),
        "local",
        flops=fresh.size * 128 * 16,
        moved=fresh.size * 12,
        in_specs=[SMEM] + [VMEM] * 4,
        out_specs=(VMEM, VMEM),
        limit=10 * 1024 * 1024,
    )(slots, fresh, factor, aux_sub, aux_grp)


def spread_body(slots_ref, solved_ref, own_ref, from_sub_ref, from_grp_ref, block_ref, basis_ref, aux_sub_ref, aux_grp_ref, iterate_ref, direction_ref, curve_ref, product_ref, out_ref, iterate_out):
    width = basis_ref.shape[1]
    prims = basis_ref.shape[0]
    half = solved_ref.shape[1] // 2
    per_face = half // width
    rows = half
    own = own_ref[...] * 0.5
    basis = basis_ref[...]
    scale = per_row(product_ref[...] / curve_ref[...], width)
    for which, aux, other_ref in ((1, aux_sub_ref, from_sub_ref), (3, aux_grp_ref, from_grp_ref)):
        base = (which // 2) * half
        both = jnp.concatenate([own, other_ref[...] * 0.5], 1)
        right = jnp.concatenate([basis, aux[rows : rows + prims, :].astype(BF16)], 0)
        own_near = (block_ref[...] - slots_ref[0, which] * per_face).astype(F32)
        near = jnp.concatenate([own_near, aux[rows + prims : rows + prims + 1, :]], 1)
        for b in range(per_face):
            cols = slice(base + b * width, base + (b + 1) * width)
            high, low = split(jnp.where(near == b, both, 0.0))
            out_ref[:, cols] = solved_ref[:, cols] + (mm(high, right) + mm(low, right))
            iterate_out[:, cols] = iterate_ref[:, cols] + scale * direction_ref[:, cols]


def spread(slots, solved, own, from_sub, from_grp, blocks, basis, aux_sub, aux_grp, iterate, direction, curve, product):
    return call(
        spread_body,
        (jax.ShapeDtypeStruct(solved.shape, F32),) * 2,
        "spread",
        flops=solved.size * 128 * 8,
        moved=solved.size * 12,
        in_specs=[SMEM] + [VMEM] * 12,
        out_specs=(VMEM, VMEM),
        limit=10 * 1024 * 1024,
    )(slots, solved, own, from_sub, from_grp, blocks, basis, aux_sub, aux_grp, iterate, direction, curve, product)


def shards(
    solution,
    residual,
    direction,
    residual_product,
    neighbor_slots,
    coupling,
    dirichlet_factor,
    face_block,
    neumann_factor,
    primal_block,
    primal_basis,
    coarse_matrix,
    coarse_block_inverse,
    coarse_pattern,
):
    width = face_block.shape[2]
    per_face = face_block.shape[1] // 4
    face_width = per_face * width
    own = direction[0]
    basis = primal_basis[0]
    factor = neumann_factor[0]
    product = residual_product[None, :]
    grp_count = lax.axis_size("grp")

    from_sub = shifted(own[:, :face_width], "sub", 1)
    from_grp = shifted(own[:, face_width:], "grp", 1)
    aux_sub, aux_grp = pack(neighbor_slots, primal_block, basis, factor, per_face)
    aux_sub = shifted(aux_sub, "sub", -1)
    aux_grp = shifted(aux_grp, "grp", -1)
    keep = (own, residual[0], factor, basis, coarse_matrix[0], coarse_block_inverse[0], primal_block, solution[0])
    high, low, own, old, factor, basis, matrix, inverse, blocks, iterate = assemble(
        coupling[0], dirichlet_factor[0], face_block[0], keep
    )

    y, curve = apply(neighbor_slots, own, from_sub, from_grp, high, low)
    back_sub = shifted(y[0], "sub", -1)
    back_grp = shifted(y[2], "grp", -1)
    curve = grand_total(curve)
    fresh, halved, part, part_sub, part_grp = update(
        neighbor_slots, y, back_sub, back_grp, old, curve, product, blocks, basis, aux_sub, aux_grp
    )
    part_sub = shifted(part_sub, "sub", 1)
    part_grp = shifted(part_grp, "grp", 1)
    solved, local = local_solve(neighbor_slots, halved, factor, aux_sub, aux_grp)
    coarse, first, local = first_step(part, part_sub, part_grp, inverse, local)

    if grp_count == 4:
        group = jnp.stack([first, shifted(first, "grp", 2)], 0)
    else:
        group = lax.all_gather(first[None], "grp", axis=0, tiled=True)
    pieces = []
    for place in range(2 * REACH_SUBS + 1):
        pieces.append(group if place == REACH_SUBS else shifted(group, "sub", REACH_SUBS - place))
    window = merge(pieces)
    beside = window[:1]
    if grp_count == 4:
        beside = lax.ppermute(window, "grp", [(i, i ^ 1) for i in range(grp_count)])

    correction, partial = correct(grp_count == 4, coarse_pattern, window, beside, coarse, first, matrix, inverse, local)
    other_sub = shifted(correction, "sub", -1)
    other_grp = shifted(correction, "grp", -1)
    partial = total(partial, "grp")
    partial, other_sub, other_grp = lax.optimization_barrier((partial, other_sub, other_grp))
    preconditioned, new_solution = spread(
        neighbor_slots, solved, correction, other_sub, other_grp, blocks, basis, aux_sub, aux_grp, iterate, own, curve, product
    )
    new_product = total(partial, "sub")[0]
    step_ratio = new_product / residual_product
    new_direction = preconditioned[None] + step_ratio[None, :, None] * own[None]
    return (new_solution[None], fresh[None], new_direction, new_product)


def solution(mesh):
    in_specs = (
        P(("sub", "grp"), None, None),
        P(("sub", "grp"), None, None),
        P(("sub", "grp"), None, None),
        P(),
        P(("sub", "grp"), None),
        P(("sub", "grp"), None, None, None),
        P(("sub", "grp"), None, None, None),
        P(("sub", "grp"), None, None, None),
        P(("sub", "grp"), None, None, None),
        P(("sub", "grp"), None),
        P(("sub", "grp"), None, None),
        P(("sub", "grp"), None, None, None),
        P(("sub", "grp"), None, None),
        P(("sub", "grp"), None),
    )
    out_specs = (
        P(("sub", "grp"), None, None),
        P(("sub", "grp"), None, None),
        P(("sub", "grp"), None, None),
        P(),
    )
    return jax.shard_map(shards, mesh=mesh, in_specs=in_specs, out_specs=out_specs, check_vma=False)
```

time: 139 us -> 109 us (0.78)
  Pallas kernels: 47.1 us -> 31.5 us
  local copies, waits for them, and re-layouts: 11 us -> 2.08 us
  blocking collectives: 5.78 us -> 0 us
  starting transfers between devices: 22.8 us -> 28.2 us
  waiting for transfers between devices: 49.5 us -> 44.3 us
    pallas_call x5 -> x6, Pallas kernels: 35.8 us -> 21.7 us  [the longest x1 15.7 us: assemble(): call(functools.partial(assemble_body, blocks, len(keep)), (shape, shape)...]
    unnamed x36 -> x8, local copies, waits for them, and re-layouts: 9.4 us -> 0.67 us
    ppermute x14 -> x15, waiting for transfers between devices: 18.3 us -> 11.9 us  [shifted(): return lax.ppermute(value, axis, pairs)]
    all_gather x1 -> x0, blocking collectives: 5.78 us -> none  [shards(): column = lax.all_gather(first[None], 'grp', axis=0, tiled=True)]
    ppermute x14 -> x15, starting transfers between devices: 17.8 us -> 23.6 us  [shifted(): return lax.ppermute(value, axis, pairs)]
    pallas_call x1, Pallas kernels: 7.89 us -> 5.31 us  [apply(): call(apply_body, (jax.ShapeDtypeStruct((4, loads, face_width), F32), jax....]
    ppermute x0 -> x1, waiting for transfers between devices: none -> 2.08 us  [shards(): beside = lax.ppermute(window, 'grp', [(i, i ^ 1) for i in range(grp_count)])]
  transfers between devices with their start and end apart: 24 -> 26, of which waited for: 15 -> 17; matrix products, arithmetic and copies ran while one was open for 1% -> 0% of each run, Pallas kernels for 30% -> 26%
where the time goes in v2:
time: 109 us
  waiting for transfers between devices  44.3 us (41%)
  Pallas kernels  31.5 us (29%)
  starting transfers between devices  28.2 us (26%)
  local copies, waits for them, and re-layouts  2.08 us (2%)
  other arithmetic  1.7 us (2%)
    ppermute x10, waiting for transfers between devices, total(): lax.ppermute(value, axis, [(i, i ^ bit) for i in range(count)])  30.3 us
    ppermute x15, starting transfers between devices, shifted(): return lax.ppermute(value, axis, pairs)  23.6 us
    pallas_call x1, Pallas kernels, assemble(): call(functools.partial(assemble_body, blocks, len(keep)), (shape, shape)...  15.7 us
    ppermute x15, waiting for transfers between devices, shifted(): return lax.ppermute(value, axis, pairs)  11.9 us
    pallas_call x1, Pallas kernels, apply(): call(apply_body, (jax.ShapeDtypeStruct((4, loads, face_width), F32), jax....  5.31 us
    ppermute x10, starting transfers between devices, total(): lax.ppermute(value, axis, [(i, i ^ bit) for i in range(count)])  4.56 us
    pallas_call x1, Pallas kernels, local_solve(): call(local_body, (jax.ShapeDtypeStruct(fresh.shape, F32), jax.ShapeDtypeS...  2.77 us
    pallas_call x1, Pallas kernels, spread(): call(spread_body, (jax.ShapeDtypeStruct(solved.shape, F32),) * 2, 'spread...  2.29 us
  transfers between devices with their start and end apart: 26, of which 17 were waited for; matrix products, arithmetic and copies ran while one was open for 0% of the time, Pallas kernels for 26%

profile of v2, /device:TPU:0, one launch (start us, length us, event | category | flops | bytes accessed | tf_op | source)
XLA Modules:
  0.0 108.6 jit_solution(14438476485227490410)
XLA Ops:
  1.9 3.0 %collective-permute-start = (f32[128,1024]{1,0:T(8,128)S(1)}, f32[128,1024]{1,0:T(8,128)S(1)}, u32[]{:S(2)}, u32[]{:S(2)}) collective-permute-start(f32[128,1024]{1,0:T(8,128)S(1)} %get-tuple-element.71), channel_id=1, source_target_pairs={{0,4},{4,8},{8,12},{12,16},{16,20},{20,24},{24,28},{28,0},{1,5},{5... | collective-permute-start | bytes 1572872 | tf_op jit(solution)/shard_map/ppermute | solution.py:22
  5.6 1.7 %pack.1 = (f32[1160,128]{1,0:T(8,128)S(1)}, f32[1160,128]{1,0:T(8,128)S(1)}) custom-call(s32[1,4]{1,0:T(1,128)S(1)} %copy-done, s32[1,128]{1,0:T(1,128)} %block_hbm.1, bf16[128,128]{1,0:T(8,128)(2,1)} %bitcast.32, bf16[32,128,128]{2,1,0:T(8,128)(2,1)} %bitcast.27), custom_call_target="tpu_custom_call" | custom-call | flops 1000 | bytes 1781760 | tf_op jit(solution)/shard_map/pack/pallas_call | solution.py:331
  7.3 1.8 %collective-permute-start.10 = (f32[1160,128]{1,0:T(8,128)S(1)}, f32[1160,128]{1,0:T(8,128)S(1)}, u32[]{:S(2)}, u32[]{:S(2)}) collective-permute-start(f32[1160,128]{1,0:T(8,128)S(1)} %get-tuple-element.44), channel_id=1, source_target_pairs={{0,3},{1,0},{2,1},{3,2},{4,7},{5,4},{6,5},{7,6},{8,11},{9,8},{10,9... | collective-permute-start | bytes 1781768 | tf_op jit(solution)/shard_map/ppermute | solution.py:22
  9.1 3.1 %collective-permute-start.9 = (f32[1160,128]{1,0:T(8,128)S(1)}, f32[1160,128]{1,0:T(8,128)S(1)}, u32[]{:S(2)}, u32[]{:S(2)}) collective-permute-start(f32[1160,128]{1,0:T(8,128)S(1)} %get-tuple-element.43), channel_id=1, source_target_pairs={{0,28},{4,0},{8,4},{12,8},{16,12},{20,16},{24,20},{28,24},{1,29},{... | collective-permute-start | bytes 1781768 | tf_op jit(solution)/shard_map/ppermute | solution.py:22
  12.2 15.7 %assemble.1 = (bf16[16,8,128,256]{3,2,1,0:T(8,128)(2,1)S(1)}, bf16[16,8,128,256]{3,2,1,0:T(8,128)(2,1)S(1)}, f32[128,2048]{1,0:T(8,128)S(1)}, f32[128,2048]{1,0:...) custom-call(bf16[96,256,128]{2,1,0:T(8,128)(2,1)} %bitcast.34, ...), custom_call_target="tpu_custom_call" | custom-call | flops 4831838208 | bytes 9437184 | tf_op jit(solution)/shard_map/assemble/pallas_call | solution.py:217
  28.9 5.3 %apply.1 = (f32[4,128,1024]{2,1,0:T(8,128)S(1)}, f32[8,128]{1,0:T(8,128)S(1)}) custom-call(s32[1,4]{1,0:T(1,128)S(1)} %copy-done.1, f32[128,2048]{1,0:T(8,128)S(1)} %get-tuple-element.35.own_ref.direction_ref, f32[128,1024]{1,0:T(8,128)S(1)} %collective-permute-done.from_sub_ref, f32[128,1024]{1,0:T(8,128)S(1)} %collective-permute-done.1.from_grp_ref, ...), custom_call_target="tpu_custom_call" | custom-call | flops 3221225472 | bytes 16777216 | tf_op jit(solution)/shard_map/apply/pallas_call | solution.py:288
  34.3 5.6 %collective-permute-start.2 = (f32[128,1024]{1,0:T(8,128)S(1)}, f32[128,1024]{1,0:T(8,128)S(1)}, u32[]{:S(2)}, u32[]{:S(2)}) collective-permute-start(f32[128,1024]{1,0:T(8,128)S(1)} %get-tuple-element.69), channel_id=1, source_target_pairs={{0,28},{4,0},{8,4},{12,8},{16,12},{20,16},{24,20},{28,24},{1,29},{... | collective-permute-start | bytes 1572872 | tf_op jit(solution)/shard_map/ppermute | solution.py:22
  43.3 5.3 %collective-permute-done.5 = f32[8,128]{1,0:T(8,128)S(1)} collective-permute-done((f32[8,128]{1,0:T(8,128)S(1)}, f32[8,128]{1,0:T(8,128)S(1)}, u32[]{:S(2)}, u32[]{:S(2)}) %collective-permute-start.5) | collective-permute-done | bytes 4128 | tf_op jit(solution)/shard_map/ppermute | solution.py:31
  48.7 3.6 %collective-permute-done.6 = f32[8,128]{1,0:T(8,128)S(1)} collective-permute-done((f32[8,128]{1,0:T(8,128)S(1)}, f32[8,128]{1,0:T(8,128)S(1)}, u32[]{:S(2)}, u32[]{:S(2)}) %collective-permute-start.6) | collective-permute-done | bytes 4128 | tf_op jit(solution)/shard_map/ppermute | solution.py:31
  52.3 3.6 %collective-permute-done.7 = f32[8,128]{1,0:T(8,128)S(1)} collective-permute-done((f32[8,128]{1,0:T(8,128)S(1)}, f32[8,128]{1,0:T(8,128)S(1)}, u32[]{:S(2)}, u32[]{:S(2)}) %collective-permute-start.7) | collective-permute-done | bytes 4128 | tf_op jit(solution)/shard_map/ppermute | solution.py:31
  55.9 4.5 %collective-permute-done.8 = f32[8,128]{1,0:T(8,128)S(1)} collective-permute-done((f32[8,128]{1,0:T(8,128)S(1)}, f32[8,128]{1,0:T(8,128)S(1)}, u32[]{:S(2)}, u32[]{:S(2)}) %collective-permute-start.8) | collective-permute-done | bytes 4128 | tf_op jit(solution)/shard_map/ppermute | solution.py:31
  60.4 2.0 %update.1 = (f32[128,2048]{1,0:T(8,128)}, f32[128,2048]{1,0:T(8,128)S(1)}, f32[128,128]{1,0:T(8,128)S(1)}, f32[128,128]{1,0:T(8,128)S(1)}, f32[128,128]{1,0:T(8,128)S(1)}) custom-call(s32[1,4]{1,0:T(1,128)S(1)} %copy-done.1, f32[4,128,1024]{2,1,0:T(8,128)S(1)} %get-tuple-element.38.y_ref, f32[128,1024]{1,0:T(8,128)S(1)} %collective-permute-done.2.back_sub_ref, ...), custom_call_target="tpu_custom_call" | custom-call | flops 268435456 | bytes 5242880 | tf_op jit(solution)/shard_map/update/pallas_call | solution.py:392
  62.4 2.8 %local.1 = (f32[128,2048]{1,0:T(8,128)S(1)}, f32[8,128]{1,0:T(8,128)S(1)}) custom-call(s32[1,4]{1,0:T(1,128)S(1)} %copy-done.1, f32[128,2048]{1,0:T(8,128)S(1)} %get-tuple-element.45.halved_ref, bf16[32,128,128]{2,1,0:T(8,128)(2,1)S(1)} %get-tuple-element.46.factor_ref, f32[1160,128]{1,0:T(8,128)S(1)} %collective-permute-done.9.aux_sub_ref, ...), custom_call_target="tpu_custom_call" | custom-call | flops 536870912 | bytes 3145728 | tf_op jit(solution)/shard_map/local/pallas_call | solution.py:513
  65.2 4.2 %collective-permute-done.11.sub_ref = f32[128,128]{1,0:T(8,128)S(1)} collective-permute-done((f32[128,128]{1,0:T(8,128)S(1)}, f32[128,128]{1,0:T(8,128)S(1)}, u32[]{:S(2)}, u32[]{:S(2)}) %collective-permute-start.11) | collective-permute-done | bytes 65568 | tf_op jit(solution)/shard_map/ppermute | solution.py:22
  70.1 3.8 %collective-permute-done.13 = f32[128,128]{1,0:T(8,128)S(1)} collective-permute-done((f32[128,128]{1,0:T(8,128)S(1)}, f32[128,128]{1,0:T(8,128)S(1)}, u32[]{:S(2)}, u32[]{:S(2)}) %collective-permute-start.13) | collective-permute-done | bytes 65568 | tf_op jit(solution)/shard_map/ppermute | solution.py:22
  74.0 4.7 %collective-permute-start.16 = (f32[2,128,128]{2,1,0:T(8,128)S(1)}, f32[2,128,128]{2,1,0:T(8,128)S(1)}, u32[]{:S(2)}, u32[]{:S(2)}) collective-permute-start(f32[2,128,128]{2,1,0:T(8,128)S(1)} %pad_maximum_fusion.refs_2_), channel_id=1, source_target_pairs={{0,28},{4,0},{8,4},{12,8},{16,12},{20,16},{24,20},{28,24},{1,29},{... | collective-permute-start | bytes 393224 | tf_op jit(solution)/shard_map/ppermute | solution.py:22
  78.7 2.0 %collective-permute-start.17 = (f32[2,128,128]{2,1,0:T(8,128)S(1)}, f32[2,128,128]{2,1,0:T(8,128)S(1)}, u32[]{:S(2)}, u32[]{:S(2)}) collective-permute-start(f32[2,128,128]{2,1,0:T(8,128)S(1)} %pad_maximum_fusion.refs_2_), channel_id=1, source_target_pairs={{0,24},{4,28},{8,0},{12,4},{16,8},{20,12},{24,16},{28,20},{1,25},{... | collective-permute-start | bytes 393224 | tf_op jit(solution)/shard_map/ppermute | solution.py:22
  81.9 1.8 %collective-permute-done.17.refs_4_ = f32[2,128,128]{2,1,0:T(8,128)S(1)} collective-permute-done((f32[2,128,128]{2,1,0:T(8,128)S(1)}, f32[2,128,128]{2,1,0:T(8,128)S(1)}, u32[]{:S(2)}, u32[]{:S(2)}) %collective-permute-start.17) | collective-permute-done | bytes 131104 | tf_op jit(solution)/shard_map/ppermute | solution.py:22
  83.8 2.1 %collective-permute-done.18.beside_ref = f32[10,128,128]{2,1,0:T(8,128)S(1)} collective-permute-done((f32[10,128,128]{2,1,0:T(8,128)S(1)}, f32[10,128,128]{2,1,0:T(8,128)S(1)}, u32[]{:S(2)}, u32[]{:S(2)}) %collective-permute-start.18) | collective-permute-done | bytes 655392 | tf_op jit(solution)/shard_map/ppermute | solution.py:617
  87.4 2.7 %collective-permute-start.21 = (f32[128,128]{1,0:T(8,128)S(1)}, f32[128,128]{1,0:T(8,128)S(1)}, u32[]{:S(2)}, u32[]{:S(2)}) collective-permute-start(f32[128,128]{1,0:T(8,128)S(1)} %get-tuple-element.57.own_ref), channel_id=1, source_target_pairs={{0,28},{4,0},{8,4},{12,8},{16,12},{20,16},{24,20},{28,24},{1,29},{... | collective-permute-start | bytes 196616 | tf_op jit(solution)/shard_map/ppermute | solution.py:22
  92.8 2.3 %collective-permute-done.20 = f32[8,128]{1,0:T(8,128)S(1)} collective-permute-done((f32[8,128]{1,0:T(8,128)S(1)}, f32[8,128]{1,0:T(8,128)S(1)}, u32[]{:S(2)}, u32[]{:S(2)}) %collective-permute-start.20) | collective-permute-done | bytes 4128 | tf_op jit(solution)/shard_map/ppermute | solution.py:31
  95.2 3.6 %collective-permute-done.23 = f32[8,128]{1,0:T(8,128)S(1)} collective-permute-done((f32[8,128]{1,0:T(8,128)S(1)}, f32[8,128]{1,0:T(8,128)S(1)}, u32[]{:S(2)}, u32[]{:S(2)}) %collective-permute-start.23) | collective-permute-done | bytes 4128 | tf_op jit(solution)/shard_map/ppermute | solution.py:31
  98.9 3.5 %collective-permute-done.24 = f32[8,128]{1,0:T(8,128)S(1)} collective-permute-done((f32[8,128]{1,0:T(8,128)S(1)}, f32[8,128]{1,0:T(8,128)S(1)}, u32[]{:S(2)}, u32[]{:S(2)}) %collective-permute-start.24) | collective-permute-done | bytes 4128 | tf_op jit(solution)/shard_map/ppermute | solution.py:31
  102.9 2.3 %spread.1 = (f32[128,2048]{1,0:T(8,128)S(1)}, f32[128,2048]{1,0:T(8,128)}) custom-call(s32[1,4]{1,0:T(1,128)S(1)} %copy-done.1, f32[128,2048]{1,0:T(8,128)S(1)} %get-tuple-element.47.solved_ref, f32[128,128]{1,0:T(8,128)S(1)} %get-tuple-element.57.own_ref, f32[128,128]{1,0:T(8,128)S(1)} %collective-permute-done.21.from_sub_ref, ...), custom_call_target="tpu_custom_call" | custom-call | flops 268435456 | bytes 3145728 | tf_op jit(solution)/shard_map/spread/pallas_call | solution.py:548
  (60 shorter events, 17.0 us)
Async XLA Ops:
  1.9 26.9 %collective-permute-start = (f32[128,1024]{1,0:T(8,128)S(1)}, f32[128,1024]{1,0:T(8,128)S(1)}, u32[]{:S(2)}, u32[]{:S(2)}) collective-permute-start(f32[128,1024]{1,0:T(8,128)S(1)} %get-tuple-element.71), channel_id=1, source_target_pairs={{0,4},{4,8},{8,12},{12,16},{16,20},{20,24},{24,28},{28,0},{1,5},{5... | collective-permute-start | bytes 1572872 | tf_op jit(solution)/shard_map/ppermute | solution.py:22
  4.9 23.9 %collective-permute-start.1 = (f32[128,1024]{1,0:T(8,128)S(1)}, f32[128,1024]{1,0:T(8,128)S(1)}, u32[]{:S(2)}, u32[]{:S(2)}) collective-permute-start(f32[128,1024]{1,0:T(8,128)S(1)} %get-tuple-element.70), channel_id=1, source_target_pairs={{0,1},{1,2},{2,3},{3,0},{4,5},{5,6},{6,7},{7,4},{8,9},{9,10},{10,1... | collective-permute-start | bytes 1572872 | tf_op jit(solution)/shard_map/ppermute | solution.py:22
  7.3 53.1 %collective-permute-start.10 = (f32[1160,128]{1,0:T(8,128)S(1)}, f32[1160,128]{1,0:T(8,128)S(1)}, u32[]{:S(2)}, u32[]{:S(2)}) collective-permute-start(f32[1160,128]{1,0:T(8,128)S(1)} %get-tuple-element.44), channel_id=1, source_target_pairs={{0,3},{1,0},{2,1},{3,2},{4,7},{5,4},{6,5},{7,6},{8,11},{9,8},{10,9... | collective-permute-start | bytes 1781768 | tf_op jit(solution)/shard_map/ppermute | solution.py:22
  9.1 51.3 %collective-permute-start.9 = (f32[1160,128]{1,0:T(8,128)S(1)}, f32[1160,128]{1,0:T(8,128)S(1)}, u32[]{:S(2)}, u32[]{:S(2)}) collective-permute-start(f32[1160,128]{1,0:T(8,128)S(1)} %get-tuple-element.43), channel_id=1, source_target_pairs={{0,28},{4,0},{8,4},{12,8},{16,12},{20,16},{24,20},{28,24},{1,29},{... | collective-permute-start | bytes 1781768 | tf_op jit(solution)/shard_map/ppermute | solution.py:22
  34.3 26.1 %collective-permute-start.2 = (f32[128,1024]{1,0:T(8,128)S(1)}, f32[128,1024]{1,0:T(8,128)S(1)}, u32[]{:S(2)}, u32[]{:S(2)}) collective-permute-start(f32[128,1024]{1,0:T(8,128)S(1)} %get-tuple-element.69), channel_id=1, source_target_pairs={{0,28},{4,0},{8,4},{12,8},{16,12},{20,16},{24,20},{28,24},{1,29},{... | collective-permute-start | bytes 1572872 | tf_op jit(solution)/shard_map/ppermute | solution.py:22
  39.9 20.5 %collective-permute-start.3 = (f32[128,1024]{1,0:T(8,128)S(1)}, f32[128,1024]{1,0:T(8,128)S(1)}, u32[]{:S(2)}, u32[]{:S(2)}) collective-permute-start(f32[128,1024]{1,0:T(8,128)S(1)} %get-tuple-element.68), channel_id=1, source_target_pairs={{0,3},{1,0},{2,1},{3,2},{4,7},{5,4},{6,5},{7,6},{8,11},{9,8},{10,9... | collective-permute-start | bytes 1572872 | tf_op jit(solution)/shard_map/ppermute | solution.py:22
  41.8 6.8 %collective-permute-start.5 = (f32[8,128]{1,0:T(8,128)S(1)}, f32[8,128]{1,0:T(8,128)S(1)}, u32[]{:S(2)}, u32[]{:S(2)}) collective-permute-start(f32[8,128]{1,0:T(8,128)S(1)} %add.36), channel_id=1, source_target_pairs={{0,2},{1,3},{2,0},{3,1},{4,6},{5,7},{6,4},{7,5},{8,10},{9,11},{10,... | collective-permute-start | bytes 12296 | tf_op jit(solution)/shard_map/ppermute | solution.py:31
  48.7 3.6 %collective-permute-start.6 = (f32[8,128]{1,0:T(8,128)S(1)}, f32[8,128]{1,0:T(8,128)S(1)}, u32[]{:S(2)}, u32[]{:S(2)}) collective-permute-start(f32[8,128]{1,0:T(8,128)S(1)} %add.37), channel_id=1, source_target_pairs={{0,4},{4,0},{8,12},{12,8},{16,20},{20,16},{24,28},{28,24},{1,5},{5... | collective-permute-start | bytes 12296 | tf_op jit(solution)/shard_map/ppermute | solution.py:31
  52.3 3.6 %collective-permute-start.7 = (f32[8,128]{1,0:T(8,128)S(1)}, f32[8,128]{1,0:T(8,128)S(1)}, u32[]{:S(2)}, u32[]{:S(2)}) collective-permute-start(f32[8,128]{1,0:T(8,128)S(1)} %add.38), channel_id=1, source_target_pairs={{0,8},{4,12},{8,0},{12,4},{16,24},{20,28},{24,16},{28,20},{1,9},{5... | collective-permute-start | bytes 12296 | tf_op jit(solution)/shard_map/ppermute | solution.py:31
  55.9 4.5 %collective-permute-start.8 = (f32[8,128]{1,0:T(8,128)S(1)}, f32[8,128]{1,0:T(8,128)S(1)}, u32[]{:S(2)}, u32[]{:S(2)}) collective-permute-start(f32[8,128]{1,0:T(8,128)S(1)} %add.39), channel_id=1, source_target_pairs={{0,16},{4,20},{8,24},{12,28},{16,0},{20,4},{24,8},{28,12},{1,17},{... | collective-permute-start | bytes 12296 | tf_op jit(solution)/shard_map/ppermute | solution.py:31
  62.4 7.0 %collective-permute-start.11 = (f32[128,128]{1,0:T(8,128)S(1)}, f32[128,128]{1,0:T(8,128)S(1)}, u32[]{:S(2)}, u32[]{:S(2)}) collective-permute-start(f32[128,128]{1,0:T(8,128)S(1)} %get-tuple-element.49), channel_id=1, source_target_pairs={{0,4},{4,8},{8,12},{12,16},{16,20},{20,24},{24,28},{28,0},{1,5},{5... | collective-permute-start | bytes 196616 | tf_op jit(solution)/shard_map/ppermute | solution.py:22
  62.4 7.0 %collective-permute-start.12 = (f32[128,128]{1,0:T(8,128)S(1)}, f32[128,128]{1,0:T(8,128)S(1)}, u32[]{:S(2)}, u32[]{:S(2)}) collective-permute-start(f32[128,128]{1,0:T(8,128)S(1)} %get-tuple-element.50), channel_id=1, source_target_pairs={{0,1},{1,2},{2,3},{3,0},{4,5},{5,6},{6,7},{7,4},{8,9},{9,10},{10,1... | collective-permute-start | bytes 196616 | tf_op jit(solution)/shard_map/ppermute | solution.py:22
  69.5 4.3 %collective-permute-start.13 = (f32[128,128]{1,0:T(8,128)S(1)}, f32[128,128]{1,0:T(8,128)S(1)}, u32[]{:S(2)}, u32[]{:S(2)}) collective-permute-start(f32[128,128]{1,0:T(8,128)S(1)} %get-tuple-element.53.first_ref), channel_id=1, source_target_pairs={{0,2},{1,3},{2,0},{3,1},{4,6},{5,7},{6,4},{7,5},{8,10},{9,11},{10,... | collective-permute-start | bytes 196616 | tf_op jit(solution)/shard_map/ppermute | solution.py:22
  73.9 6.9 %collective-permute-start.14 = (f32[2,128,128]{2,1,0:T(8,128)S(1)}, f32[2,128,128]{2,1,0:T(8,128)S(1)}, u32[]{:S(2)}, u32[]{:S(2)}) collective-permute-start(f32[2,128,128]{2,1,0:T(8,128)S(1)} %pad_maximum_fusion.refs_2_), channel_id=1, source_target_pairs={{0,8},{4,12},{8,16},{12,20},{16,24},{20,28},{24,0},{28,4},{1,9},{5... | collective-permute-start | bytes 393224 | tf_op jit(solution)/shard_map/ppermute | solution.py:22
  73.9 8.0 %collective-permute-start.15 = (f32[2,128,128]{2,1,0:T(8,128)S(1)}, f32[2,128,128]{2,1,0:T(8,128)S(1)}, u32[]{:S(2)}, u32[]{:S(2)}) collective-permute-start(f32[2,128,128]{2,1,0:T(8,128)S(1)} %pad_maximum_fusion.refs_2_), channel_id=1, source_target_pairs={{0,4},{4,8},{8,12},{12,16},{16,20},{20,24},{24,28},{28,0},{1,5},{5... | collective-permute-start | bytes 393224 | tf_op jit(solution)/shard_map/ppermute | solution.py:22
  74.0 7.9 %collective-permute-start.16 = (f32[2,128,128]{2,1,0:T(8,128)S(1)}, f32[2,128,128]{2,1,0:T(8,128)S(1)}, u32[]{:S(2)}, u32[]{:S(2)}) collective-permute-start(f32[2,128,128]{2,1,0:T(8,128)S(1)} %pad_maximum_fusion.refs_2_), channel_id=1, source_target_pairs={{0,28},{4,0},{8,4},{12,8},{16,12},{20,16},{24,20},{28,24},{1,29},{... | collective-permute-start | bytes 393224 | tf_op jit(solution)/shard_map/ppermute | solution.py:22
  78.7 5.0 %collective-permute-start.17 = (f32[2,128,128]{2,1,0:T(8,128)S(1)}, f32[2,128,128]{2,1,0:T(8,128)S(1)}, u32[]{:S(2)}, u32[]{:S(2)}) collective-permute-start(f32[2,128,128]{2,1,0:T(8,128)S(1)} %pad_maximum_fusion.refs_2_), channel_id=1, source_target_pairs={{0,24},{4,28},{8,0},{12,4},{16,8},{20,12},{24,16},{28,20},{1,25},{... | collective-permute-start | bytes 393224 | tf_op jit(solution)/shard_map/ppermute | solution.py:22
  83.7 2.2 %collective-permute-start.18 = (f32[10,128,128]{2,1,0:T(8,128)S(1)}, f32[10,128,128]{2,1,0:T(8,128)S(1)}, u32[]{:S(2)}, u32[]{:S(2)}) collective-permute-start(f32[10,128,128]{2,1,0:T(8,128)S(1)} %merge.1.window_ref), channel_id=1, source_target_pairs={{0,1},{1,0},{2,3},{3,2},{4,5},{5,4},{6,7},{7,6},{8,9},{9,8},{10,11... | collective-permute-start | bytes 1966088 | tf_op jit(solution)/shard_map/ppermute | solution.py:617
  87.4 7.7 %collective-permute-start.21 = (f32[128,128]{1,0:T(8,128)S(1)}, f32[128,128]{1,0:T(8,128)S(1)}, u32[]{:S(2)}, u32[]{:S(2)}) collective-permute-start(f32[128,128]{1,0:T(8,128)S(1)} %get-tuple-element.57.own_ref), channel_id=1, source_target_pairs={{0,28},{4,0},{8,4},{12,8},{16,12},{20,16},{24,20},{28,24},{1,29},{... | collective-permute-start | bytes 196616 | tf_op jit(solution)/shard_map/ppermute | solution.py:22
  90.2 5.0 %collective-permute-start.22 = (f32[128,128]{1,0:T(8,128)S(1)}, f32[128,128]{1,0:T(8,128)S(1)}, u32[]{:S(2)}, u32[]{:S(2)}) collective-permute-start(f32[128,128]{1,0:T(8,128)S(1)} %get-tuple-element.57.own_ref), channel_id=1, source_target_pairs={{0,3},{1,0},{2,1},{3,2},{4,7},{5,4},{6,5},{7,6},{8,11},{9,8},{10,9... | collective-permute-start | bytes 196616 | tf_op jit(solution)/shard_map/ppermute | solution.py:22
  91.5 3.6 %collective-permute-start.20 = (f32[8,128]{1,0:T(8,128)S(1)}, f32[8,128]{1,0:T(8,128)S(1)}, u32[]{:S(2)}, u32[]{:S(2)}) collective-permute-start(f32[8,128]{1,0:T(8,128)S(1)} %add.41), channel_id=1, source_target_pairs={{0,2},{1,3},{2,0},{3,1},{4,6},{5,7},{6,4},{7,5},{8,10},{9,11},{10,... | collective-permute-start | bytes 12296 | tf_op jit(solution)/shard_map/ppermute | solution.py:31
  95.1 3.7 %collective-permute-start.23 = (f32[8,128]{1,0:T(8,128)S(1)}, f32[8,128]{1,0:T(8,128)S(1)}, u32[]{:S(2)}, u32[]{:S(2)}) collective-permute-start(f32[8,128]{1,0:T(8,128)S(1)} %add.42), channel_id=1, source_target_pairs={{0,4},{4,0},{8,12},{12,8},{16,20},{20,16},{24,28},{28,24},{1,5},{5... | collective-permute-start | bytes 12296 | tf_op jit(solution)/shard_map/ppermute | solution.py:31
  98.8 3.6 %collective-permute-start.24 = (f32[8,128]{1,0:T(8,128)S(1)}, f32[8,128]{1,0:T(8,128)S(1)}, u32[]{:S(2)}, u32[]{:S(2)}) collective-permute-start(f32[8,128]{1,0:T(8,128)S(1)} %add.43), channel_id=1, source_target_pairs={{0,8},{4,12},{8,0},{12,4},{16,24},{20,28},{24,16},{28,20},{1,9},{5... | collective-permute-start | bytes 12296 | tf_op jit(solution)/shard_map/ppermute | solution.py:31
  102.4 4.5 %collective-permute-start.25 = (f32[8,128]{1,0:T(8,128)S(1)}, f32[8,128]{1,0:T(8,128)S(1)}, u32[]{:S(2)}, u32[]{:S(2)}) collective-permute-start(f32[8,128]{1,0:T(8,128)S(1)} %add.44), channel_id=1, source_target_pairs={{0,16},{4,20},{8,24},{12,28},{16,0},{20,4},{24,8},{28,12},{1,17},{... | collective-permute-start | bytes 12296 | tf_op jit(solution)/shard_map/ppermute | solution.py:31
  (6 other events, 103.8 us)

commit v3 on v2

--- a/solution.py
+++ b/solution.py
@@ -6,6 +6,7 @@
 from jax.experimental import pallas as pl
 from jax.experimental.pallas import tpu as pltpu
 from jax.sharding import PartitionSpec as P
+
 
 REACH_SUBS = 2
 F32 = jnp.float32
@@ -26,15 +27,55 @@
     count = lax.axis_size(axis)
     if count & (count - 1):
         return lax.psum(value, axis)
+    bits = [1 << k for k in range(count.bit_length() - 1)]
+    for bit in reversed(bits) if axis == "sub" else bits:
+        value = value + lax.ppermute(value, axis, [(i, i ^ bit) for i in range(count)])
+    return value
+
+
+def total_with(value, axis, late):
+    count = lax.axis_size(axis)
+    if count & (count - 1):
+        value, extra = late(value)
+        return lax.psum(value, axis), extra
     bit = 1
+    extra = None
     while bit < count:
+        if 2 * bit == count:
+            value, extra = late(value)
         value = value + lax.ppermute(value, axis, [(i, i ^ bit) for i in range(count)])
         bit *= 2
-    return value
-
-
-def grand_total(value):
-    return total(total(value, "grp"), "sub")
+    return value, extra
+
+
+def swapped_window(count):
+    return REACH_SUBS == 2 and count % 4 == 0 and count > 4
+
+
+def sub_window(group):
+    count = lax.axis_size("sub")
+    everyone = range(count)
+    if swapped_window(count):
+        targets = (
+            [i ^ 1 for i in everyone],
+            [(i - 1 + 2 * (i & 1)) % count for i in everyone],
+            [i ^ 2 for i in everyone],
+            [(i - 2 + 2 * (i & 2)) % count for i in everyone],
+        )
+    else:
+        targets = [[(i - step) % count for i in everyone] for step in range(-REACH_SUBS, REACH_SUBS + 1) if step]
+    pieces = []
+    for target in targets:
+        pieces.append(lax.ppermute(group, "sub", list(zip(everyone, target))))
+    return pieces
+
+
+def sub_slot(offset, mine, count):
+    if swapped_window(count):
+        far = jnp.where((mine & 2 == 0) == (offset == 2), 3, 4)
+        near = jnp.where((mine & 1 == 0) == (offset == 1), 1, 2)
+        return jnp.where(offset == 0, 0, jnp.where((offset == 1) | (offset == -1), near, far))
+    return jnp.where(offset == 0, 0, offset + REACH_SUBS + (offset < 0).astype(jnp.int32))
 
 
 def split(value):
@@ -67,7 +108,7 @@
     return tall.T
 
 
-def call(body, out_shapes, name, flops, moved, scratch=(), grid=None, in_specs=None, out_specs=None, limit=None):
+def call(body, out_shapes, flops, moved, scratch=(), grid=None, in_specs=None, out_specs=None, limit=None):
     params = {}
     if limit is not None:
         params["vmem_limit_bytes"] = limit
@@ -82,24 +123,24 @@
         scratch_shapes=scratch,
         compiler_params=pltpu.CompilerParams(**params),
         cost_estimate=pl.CostEstimate(flops=flops, bytes_accessed=moved, transcendentals=0),
-        name=name,
         **kwargs,
     )
 
 
-BATCH = 8
-
-
-def assemble_body(blocks, kept, couple_hbm, factor_hbm, face_hbm, *refs):
+BATCH = 16
+
+
+def in_hbm(value):
+    return pltpu.with_memory_space_constraint(value, pltpu.HBM)
+
+
+def prepare_body(kept, couple_hbm, factor_hbm, *refs):
     sources = refs[:kept]
-    high_ref, low_ref = refs[kept : kept + 2]
+    couple_ref, middle_ref = refs[kept : kept + 2]
     targets = refs[kept + 2 : 2 * kept + 2]
-    couple_ref, factor_ref, face_ref, inner_ref, middle_ref, near_ref, far_ref, sems, keep_sems = refs[2 * kept + 2 :]
-    width = face_ref.shape[1]
-    count = couple_ref.shape[0]
-    reach = count // blocks
-    pairs = blocks // 2
-    rounds = count // BATCH
+    factor_ref, inner_ref, sems, keep_sems = refs[2 * kept + 2 :]
+    width = factor_ref.shape[1]
+    rounds = couple_ref.shape[0] // BATCH
 
     def copy_of(i, which):
         part = pl.ds(i * BATCH, BATCH)
@@ -111,22 +152,10 @@
             copy_of(i, which).start()
         return carry
 
-    face_copy = pltpu.make_async_copy(face_hbm, face_ref, keep_sems.at[kept])
-    face_copy.start()
+    keeping = [pltpu.make_async_copy(a, b, keep_sems.at[i]) for i, (a, b) in enumerate(zip(sources, targets))]
     lax.fori_loop(0, rounds, begin, 0)
-    keeping = [pltpu.make_async_copy(a, b, keep_sems.at[i]) for i, (a, b) in enumerate(zip(sources, targets))]
     for copy in keeping:
         copy.start()
-    face_copy.wait()
-
-    def convert(block, carry):
-        near_ref[block] = face_ref[block].astype(F32)
-        far_ref[block] = jnp.zeros((width, width), F32)
-        return carry
-
-    lax.fori_loop(0, blocks, convert, 0)
-    for extra in range(reach):
-        far_ref[blocks + extra] = jnp.zeros((width, width), F32)
 
     def inner(i):
         for k in range(BATCH):
@@ -138,8 +167,71 @@
     def middle(i):
         for k in range(BATCH):
             high, low = split(mm(twice(couple_ref[i * BATCH + k], 1), inner_ref[i % 2, k]))
-            middle_ref[i % 2, k, :, :width] = high
-            middle_ref[i % 2, k, :, width:] = low
+            middle_ref[i * BATCH + k, :, :width] = high
+            middle_ref[i * BATCH + k, :, width:] = low
+
+    copy_of(0, 0).wait()
+    inner(0)
+
+    def steady(i, carry):
+        copy_of(i, 0).wait()
+        copy_of(i - 1, 1).wait()
+        inner(i)
+        middle(i - 1)
+        return carry
+
+    lax.fori_loop(1, rounds, steady, 0)
+    copy_of(rounds - 1, 1).wait()
+    middle(rounds - 1)
+    for copy in keeping:
+        copy.wait()
+
+
+def prepare(coupling, dirichlet, keep):
+    count, double, width = coupling.shape
+    hbm = pl.BlockSpec(memory_space=pltpu.HBM)
+    return call(
+        functools.partial(prepare_body, len(keep)),
+        (
+            jax.ShapeDtypeStruct(coupling.shape, BF16),
+            jax.ShapeDtypeStruct((count, double, double), BF16),
+        )
+        + tuple(jax.ShapeDtypeStruct(k.shape, k.dtype) for k in keep),
+        flops=count * 2 * width**3 * 6,
+        moved=coupling.size * 3,
+        scratch=[
+            pltpu.VMEM((count, width, width), BF16),
+            pltpu.VMEM((2, BATCH, double, width), BF16),
+            pltpu.SemaphoreType.DMA((2, count // BATCH)),
+            pltpu.SemaphoreType.DMA((len(keep),)),
+        ],
+        in_specs=[hbm] * (2 + len(keep)),
+        out_specs=(VMEM,) * (2 + len(keep)),
+        limit=6 * 1024 * 1024,
+    )(in_hbm(coupling), in_hbm(dirichlet), *(in_hbm(k) for k in keep))
+
+
+def assemble_body(blocks, kept, couple_ref, middle_ref, face_ref, *refs):
+    sources = refs[:kept]
+    high_ref, low_ref = refs[kept : kept + 2]
+    targets = refs[kept + 2 : 2 * kept + 2]
+    near_ref, far_ref, keep_sems = refs[2 * kept + 2 :]
+    width = face_ref.shape[1]
+    count = couple_ref.shape[0]
+    reach = count // blocks
+    pairs = blocks // 2
+    keeping = [pltpu.make_async_copy(a, b, keep_sems.at[i]) for i, (a, b) in enumerate(zip(sources, targets))]
+    for copy in keeping:
+        copy.start()
+
+    def convert(block, carry):
+        near_ref[block] = face_ref[block].astype(F32)
+        far_ref[block] = jnp.zeros((width, width), F32)
+        return carry
+
+    lax.fori_loop(0, blocks, convert, 0)
+    for extra in range(reach):
+        far_ref[blocks + extra] = jnp.zeros((width, width), F32)
 
     def put(pair, row, half, value):
         high, low = split(value)
@@ -147,12 +239,12 @@
         high_ref[pair, row, :, cols] = high
         low_ref[pair, row, :, cols] = low
 
-    def outer(i):
+    def outer(i, carry):
         per = blocks // BATCH
         q = i // per
         base = (i - q * per) * BATCH
         for k in range(BATCH):
-            full = mm(middle_ref[i % 2, k], twice(couple_ref[i * BATCH + k], 1), NT)
+            full = mm(middle_ref[i * BATCH + k], twice(couple_ref[i * BATCH + k], 1), NT)
             place = base + k
             reached = place + q + 1
             near_ref[place] += full[:width, :width]
@@ -162,30 +254,9 @@
             put(wrapped // 2, reach - 1 - q + half, half, full[:width, width:])
             side = k % 2
             put(place // 2, reach + q + 1 + side, side, full[width:, :width])
-
-    def wait(i, which):
-        copy_of(i, which).wait()
-
-    wait(0, 0)
-    inner(0)
-    wait(1, 0)
-    wait(0, 1)
-    inner(1)
-    middle(0)
-
-    def steady(i, carry):
-        wait(i, 0)
-        wait(i - 1, 1)
-        inner(i)
-        middle(i - 1)
-        outer(i - 2)
         return carry
 
-    lax.fori_loop(2, rounds, steady, 0)
-    wait(rounds - 1, 1)
-    middle(rounds - 1)
-    outer(rounds - 2)
-    outer(rounds - 1)
+    lax.fori_loop(0, count // BATCH, outer, 0)
 
     def close(pair, carry):
         zero = jnp.zeros((width, width), BF16)
@@ -203,13 +274,9 @@
         copy.wait()
 
 
-def in_hbm(value):
-    return pltpu.with_memory_space_constraint(value, pltpu.HBM)
-
-
-def assemble(coupling, dirichlet, face, keep):
+def assemble(couple, middle, face, keep):
     blocks, width, _ = face.shape
-    count = coupling.shape[0]
+    count = couple.shape[0]
     reach = count // blocks
     pairs = blocks // 2
     shape = jax.ShapeDtypeStruct((pairs, 2 * reach + 2, width, 2 * width), BF16)
@@ -217,27 +284,17 @@
     return call(
         functools.partial(assemble_body, blocks, len(keep)),
         (shape, shape) + tuple(jax.ShapeDtypeStruct(k.shape, k.dtype) for k in keep),
-        "assemble",
-        flops=count * 2 * width**3 * 12,
-        moved=coupling.size * 3,
+        flops=count * 2 * width**3 * 6,
+        moved=couple.size * 3,
         scratch=[
-            pltpu.VMEM((count, 2 * width, width), BF16),
-            pltpu.VMEM((count, width, width), BF16),
-            pltpu.VMEM((blocks, width, width), BF16),
-            pltpu.VMEM((2, BATCH, 2 * width, width), BF16),
-            pltpu.VMEM((2, BATCH, 2 * width, 2 * width), BF16),
             pltpu.VMEM((blocks, width, width), F32),
             pltpu.VMEM((blocks + reach, width, width), F32),
-            pltpu.SemaphoreType.DMA((2, count // BATCH)),
-            pltpu.SemaphoreType.DMA((len(keep) + 1,)),
+            pltpu.SemaphoreType.DMA((len(keep),)),
         ],
-        in_specs=[hbm] * (3 + len(keep)),
+        in_specs=[VMEM] * 3 + [hbm] * len(keep),
         out_specs=(VMEM,) * (2 + len(keep)),
-        limit=ASSEMBLE_LIMIT,
-    )(in_hbm(coupling), in_hbm(dirichlet), in_hbm(face), *(in_hbm(k) for k in keep))
-
-
-ASSEMBLE_LIMIT = 22 * 1024 * 1024
+        limit=6 * 1024 * 1024,
+    )(couple, middle, face, *(in_hbm(k) for k in keep))
 
 
 def apply_body(slots_ref, own_ref, from_sub_ref, from_grp_ref, high_ref, low_ref, out_ref, curve_ref, u_high, u_low):
@@ -283,7 +340,7 @@
 
 
 def apply(slots, own, from_sub, from_grp, high, low):
-    pairs, count, width, double = high.shape
+    pairs, count, width, _ = high.shape
     loads, face_width = from_sub.shape
     return call(
         apply_body,
@@ -291,7 +348,6 @@
             jax.ShapeDtypeStruct((4, loads, face_width), F32),
             jax.ShapeDtypeStruct((8, loads), F32),
         ),
-        "apply",
         flops=high.size * loads * 6,
         moved=high.size * 4,
         scratch=[pltpu.VMEM((2 * pairs + count - 1, loads, width), BF16)] * 2,
@@ -301,24 +357,13 @@
     )(slots, own, from_sub, from_grp, high, low)
 
 
-def pack_body(per_face, slots_ref, block_hbm, basis_hbm, factor_hbm, sub_ref, grp_ref, block_ref, basis_ref, factor_ref, sems):
+def pack_body(per_face, slots_ref, block_ref, basis_ref, factor_ref, sub_ref, grp_ref):
     prims, width = basis_ref.shape
     rows = per_face * width
-    copies = [
-        pltpu.make_async_copy(basis_hbm, basis_ref, sems.at[2]),
-        pltpu.make_async_copy(block_hbm, block_ref, sems.at[3]),
-    ]
-    for i, which in enumerate((0, 2)):
-        part = pl.ds(slots_ref[0, which] * per_face, per_face)
-        copies.append(pltpu.make_async_copy(factor_hbm.at[part], factor_ref.at[i], sems.at[i]))
-    for copy in copies:
-        copy.start()
-    for copy in copies:
-        copy.wait()
-    for i, (out, which) in enumerate(((sub_ref, 0), (grp_ref, 2))):
+    for out, which in ((sub_ref, 0), (grp_ref, 2)):
         first = slots_ref[0, which] * per_face
         for b in range(per_face):
-            out[b * width : (b + 1) * width, :] = factor_ref[i, b].astype(F32)
+            out[b * width : (b + 1) * width, :] = factor_ref[first + b].astype(F32)
         out[rows : rows + prims, :] = basis_ref[...].astype(F32)
         near = (block_ref[...] - first).astype(F32)
         out[rows + prims :, :] = jnp.broadcast_to(near, (8, width))
@@ -327,23 +372,15 @@
 def pack(slots, blocks, basis, factor, per_face):
     prims, width = basis.shape
     shape = jax.ShapeDtypeStruct((per_face * width + prims + 8, width), F32)
-    hbm = pl.BlockSpec(memory_space=pltpu.HBM)
     return call(
         functools.partial(pack_body, per_face),
         (shape, shape),
-        "pack",
         flops=1000,
         moved=shape.size * 12,
-        scratch=[
-            pltpu.VMEM(blocks.shape, jnp.int32),
-            pltpu.VMEM((prims, width), BF16),
-            pltpu.VMEM((2, per_face, width, width), BF16),
-            pltpu.SemaphoreType.DMA((4,)),
-        ],
-        in_specs=[SMEM, hbm, hbm, hbm],
+        in_specs=[SMEM] + [VMEM] * 3,
         out_specs=(VMEM, VMEM),
         limit=4 * 1024 * 1024,
-    )(slots, in_hbm(blocks), in_hbm(basis), in_hbm(factor))
+    )(slots, blocks, basis, factor)
 
 
 def update_body(slots_ref, y_ref, back_sub_ref, back_grp_ref, residual_ref, curve_ref, product_ref, block_ref, basis_ref, aux_sub_ref, aux_grp_ref, residual_out, half_out, own_out, sub_out, grp_out):
@@ -392,7 +429,6 @@
     return call(
         update_body,
         (jax.ShapeDtypeStruct(residual.shape, F32), jax.ShapeDtypeStruct(residual.shape, F32), small, small, small),
-        "update",
         flops=residual.size * prims * 8,
         moved=residual.size * 20,
         in_specs=[SMEM] + [VMEM] * 10,
@@ -401,25 +437,23 @@
     )(slots, y, back_sub, back_grp, residual, curve, product, blocks, basis, aux_sub, aux_grp)
 
 
-def first_body(own_ref, sub_ref, grp_ref, inverse_ref, local_ref, coarse_out, first_out, local_out):
+def first_body(own_ref, sub_ref, grp_ref, inverse_ref, coarse_out, first_out):
     coarse = own_ref[...] + sub_ref[...] + grp_ref[...]
     coarse_out[...] = coarse
     first_out[...] = mm3(coarse, inverse_ref[...])
-    local_out[...] = local_ref[...]
-
-
-def first_step(own, sub, grp, inverse, local):
+
+
+def first_step(own, sub, grp, inverse):
     shape = jax.ShapeDtypeStruct(own.shape, F32)
     return call(
         first_body,
-        (shape, shape, jax.ShapeDtypeStruct(local.shape, F32)),
-        "first",
+        (shape, shape),
         flops=own.size * 128 * 6,
         moved=own.size * 24,
-        in_specs=[VMEM] * 5,
-        out_specs=(VMEM,) * 3,
+        in_specs=[VMEM] * 4,
+        out_specs=(VMEM,) * 2,
         limit=4 * 1024 * 1024,
-    )(own, sub, grp, inverse, local)
+    )(own, sub, grp, inverse)
 
 
 def merge_body(*refs):
@@ -435,7 +469,6 @@
     return call(
         merge_body,
         shape,
-        "merge",
         flops=1000,
         moved=shape.size * 8,
         in_specs=[VMEM] * len(pieces),
@@ -457,7 +490,8 @@
         entry = pattern_ref[0, k]
         entry_sub = entry // grp_count
         entry_grp = entry - entry_sub * grp_count
-        position = lax.rem(entry_sub - my_sub + REACH_SUBS + sub_count, sub_count)
+        offset = lax.rem(entry_sub - my_sub + REACH_SUBS + sub_count, sub_count) - REACH_SUBS
+        position = sub_slot(offset, my_sub, sub_count)
         if paired:
             apart = entry_grp ^ my_grp
             index = ((apart & 1) * (2 * REACH_SUBS + 1) + position) * 2 + (apart >> 1)
@@ -476,7 +510,6 @@
     return call(
         functools.partial(correct_body, paired),
         (shape, jax.ShapeDtypeStruct((8, first.shape[0]), F32)),
-        "correct",
         flops=matrix.size * 128 * 6,
         moved=window.size * 4,
         scratch=[pltpu.VMEM((window.shape[0] + beside.shape[0],) + window.shape[1:], F32)],
@@ -513,7 +546,6 @@
     return call(
         local_body,
         (jax.ShapeDtypeStruct(fresh.shape, F32), jax.ShapeDtypeStruct((8, fresh.shape[0]), F32)),
-        "local",
         flops=fresh.size * 128 * 16,
         moved=fresh.size * 12,
         in_specs=[SMEM] + [VMEM] * 4,
@@ -548,7 +580,6 @@
     return call(
         spread_body,
         (jax.ShapeDtypeStruct(solved.shape, F32),) * 2,
-        "spread",
         flops=solved.size * 128 * 8,
         moved=solved.size * 12,
         in_specs=[SMEM] + [VMEM] * 12,
@@ -584,47 +615,52 @@
 
     from_sub = shifted(own[:, :face_width], "sub", 1)
     from_grp = shifted(own[:, face_width:], "grp", 1)
-    aux_sub, aux_grp = pack(neighbor_slots, primal_block, basis, factor, per_face)
+    keep = (face_block[0], factor, basis, primal_block)
+    couple, middle, face, factor, basis, blocks = prepare(coupling[0], dirichlet_factor[0], keep)
+    aux_sub, aux_grp = pack(neighbor_slots, blocks, basis, factor, per_face)
+    aux_sub, aux_grp, face = lax.optimization_barrier((aux_sub, aux_grp, face))
     aux_sub = shifted(aux_sub, "sub", -1)
     aux_grp = shifted(aux_grp, "grp", -1)
-    keep = (own, residual[0], factor, basis, coarse_matrix[0], coarse_block_inverse[0], primal_block, solution[0])
-    high, low, own, old, factor, basis, matrix, inverse, blocks, iterate = assemble(
-        coupling[0], dirichlet_factor[0], face_block[0], keep
-    )
+    keep = (own, residual[0], coarse_matrix[0], coarse_block_inverse[0], solution[0])
+    high, low, own, old, matrix, inverse, iterate = assemble(couple, middle, face, keep)
 
     y, curve = apply(neighbor_slots, own, from_sub, from_grp, high, low)
     back_sub = shifted(y[0], "sub", -1)
-    back_grp = shifted(y[2], "grp", -1)
-    curve = grand_total(curve)
+    curve = total(curve, "grp")
+    lower, curve = lax.optimization_barrier((y[2], curve))
+    back_grp = shifted(lower, "grp", -1)
+    curve = total(curve, "sub")
     fresh, halved, part, part_sub, part_grp = update(
         neighbor_slots, y, back_sub, back_grp, old, curve, product, blocks, basis, aux_sub, aux_grp
     )
     part_sub = shifted(part_sub, "sub", 1)
     part_grp = shifted(part_grp, "grp", 1)
     solved, local = local_solve(neighbor_slots, halved, factor, aux_sub, aux_grp)
-    coarse, first, local = first_step(part, part_sub, part_grp, inverse, local)
+    coarse, first = first_step(part, part_sub, part_grp, inverse)
 
     if grp_count == 4:
         group = jnp.stack([first, shifted(first, "grp", 2)], 0)
     else:
         group = lax.all_gather(first[None], "grp", axis=0, tiled=True)
-    pieces = []
-    for place in range(2 * REACH_SUBS + 1):
-        pieces.append(group if place == REACH_SUBS else shifted(group, "sub", REACH_SUBS - place))
-    window = merge(pieces)
+    window = merge([group] + sub_window(group))
     beside = window[:1]
     if grp_count == 4:
         beside = lax.ppermute(window, "grp", [(i, i ^ 1) for i in range(grp_count)])
 
     correction, partial = correct(grp_count == 4, coarse_pattern, window, beside, coarse, first, matrix, inverse, local)
-    other_sub = shifted(correction, "sub", -1)
-    other_grp = shifted(correction, "grp", -1)
     partial = total(partial, "grp")
-    partial, other_sub, other_grp = lax.optimization_barrier((partial, other_sub, other_grp))
-    preconditioned, new_solution = spread(
-        neighbor_slots, solved, correction, other_sub, other_grp, blocks, basis, aux_sub, aux_grp, iterate, own, curve, product
-    )
-    new_product = total(partial, "sub")[0]
+    sent, partial = lax.optimization_barrier((correction, partial))
+    other_sub = shifted(sent, "sub", -1)
+    other_grp = shifted(sent, "grp", -1)
+
+    def late(value):
+        value, first_in, second_in = lax.optimization_barrier((value, other_sub, other_grp))
+        return value, spread(
+            neighbor_slots, solved, correction, first_in, second_in, blocks, basis, aux_sub, aux_grp, iterate, own, curve, product
+        )
+
+    new_product, (preconditioned, new_solution) = total_with(partial, "sub", late)
+    new_product = new_product[0]
     step_ratio = new_product / residual_product
     new_direction = preconditioned[None] + step_ratio[None, :, None] * own[None]
     return (new_solution[None], fresh[None], new_direction, new_product)
@@ -653,4 +689,5 @@
         P(("sub", "grp"), None, None),
         P(),
     )
+
     return jax.shard_map(shards, mesh=mesh, in_specs=in_specs, out_specs=out_specs, check_vma=False)

time: 109 us -> 112 us (1.028)
  waiting for transfers between devices: 44.3 us -> 54.3 us
  starting transfers between devices: 28.2 us -> 24.4 us
  Pallas kernels: 31.5 us -> 29.2 us
    ppermute x0 -> x7, waiting for transfers between devices: none -> 14.3 us  [the longest x3 8.19 us: total_with(): lax.ppermute(value, axis, [(i, i ^ bit) for i in range(count)])]
    ppermute x15 -> x11, starting transfers between devices: 23.6 us -> 10.3 us  [shifted(): return lax.ppermute(value, axis, pairs)]
    pallas_call x1, Pallas kernels: 15.7 us -> 6.7 us  [assemble(): call(functools.partial(assemble_body, blocks, len(keep)), (shape, shape)...]
    pallas_call x4 -> x5, Pallas kernels: 4.23 us -> 10.9 us  [the longest x1 7.84 us: prepare(): call(functools.partial(prepare_body, len(keep)), (jax.ShapeDtypeStruct(co...]
    ppermute x0 -> x7, starting transfers between devices: none -> 5.53 us  [the longest x4 4.21 us: sub_window(): pieces.append(lax.ppermute(group, 'sub', list(zip(everyone, target))))]
    ppermute x10 -> x7, starting transfers between devices: 4.56 us -> 8.49 us  [total(): lax.ppermute(value, axis, [(i, i ^ bit) for i in range(count)])]
    ppermute x1, waiting for transfers between devices: 2.08 us -> 0.01 us  [shards(): beside = lax.ppermute(window, 'grp', [(i, i ^ 1) for i in range(grp_count)])]
    ppermute x15 -> x11, waiting for transfers between devices: 11.9 us -> 10.7 us  [shifted(): return lax.ppermute(value, axis, pairs)]
  transfers between devices with their start and end apart: 26 -> 26, of which waited for: 17 -> 14; matrix products, arithmetic and copies ran while one was open for 0% -> 0% of each run, Pallas kernels for 26% -> 18%
where the time goes in v3:
time: 112 us
  waiting for transfers between devices  54.3 us (48%)
  Pallas kernels  29.2 us (26%)
  starting transfers between devices  24.4 us (22%)
  other arithmetic  1.74 us (2%)
  local copies, waits for them, and re-layouts  1.39 us (1%)
    ppermute x7, waiting for transfers between devices, total(): lax.ppermute(value, axis, [(i, i ^ bit) for i in range(count)])  29.3 us
    ppermute x11, waiting for transfers between devices, shifted(): return lax.ppermute(value, axis, pairs)  10.7 us
    ppermute x11, starting transfers between devices, shifted(): return lax.ppermute(value, axis, pairs)  10.3 us
    ppermute x7, starting transfers between devices, total(): lax.ppermute(value, axis, [(i, i ^ bit) for i in range(count)])  8.49 us
    ppermute x3, waiting for transfers between devices, total_with(): lax.ppermute(value, axis, [(i, i ^ bit) for i in range(count)])  8.19 us
    pallas_call x1, Pallas kernels, prepare(): call(functools.partial(prepare_body, len(keep)), (jax.ShapeDtypeStruct(co...  7.84 us
    pallas_call x1, Pallas kernels, assemble(): call(functools.partial(assemble_body, blocks, len(keep)), (shape, shape)...  6.7 us
    ppermute x4, waiting for transfers between devices, sub_window(): pieces.append(lax.ppermute(group, 'sub', list(zip(everyone, target))))  6.1 us
  transfers between devices with their start and end apart: 26, of which 14 were waited for; matrix products, arithmetic and copies ran while one was open for 0% of the time, Pallas kernels for 18%

profile of v3, /device:TPU:0, one launch (start us, length us, event | category | flops | bytes accessed | tf_op | source)
XLA Modules:
  0.0 111.8 jit_solution(6780584412188775277)
XLA Ops:
  2.0 3.0 %collective-permute-start = (f32[128,1024]{1,0:T(8,128)S(1)}, f32[128,1024]{1,0:T(8,128)S(1)}, u32[]{:S(2)}, u32[]{:S(2)}) collective-permute-start(f32[128,1024]{1,0:T(8,128)S(1)} %get-tuple-element.89), channel_id=1, source_target_pairs={{0,4},{4,8},{8,12},{12,16},{16,20},{20,24},{24,28},{28,0},{1,5},{5... | collective-permute-start | bytes 1572872 | tf_op jit(solution)/shard_map/ppermute | solution.py:23
  5.0 7.8 %shard_map.165 = (bf16[96,256,128]{2,1,0:T(8,128)(2,1)S(1)}, bf16[96,256,256]{2,1,0:T(8,128)(2,1)S(1)}, bf16[32,128,128]{2,1,0:T(8,128)(2,1)S(1)}, bf16[32,128,1...) custom-call(bf16[96,256,128]{2,1,0:T(8,128)(2,1)} %bitcast.27, ...), custom_call_target="tpu_custom_call" | custom-call | flops 2415919104 | bytes 9437184 | tf_op jit(solution)/shard_map/pallas_call | solution.py:193
  13.5 6.7 %shard_map.167 = (bf16[16,8,128,256]{3,2,1,0:T(8,128)(2,1)S(1)}, bf16[16,8,128,256]{3,2,1,0:T(8,128)(2,1)S(1)}, f32[128,2048]{1,0:T(8,128)S(1)}, f32[128,2048]{1...) custom-call(bf16[96,256,128]{2,1,0:T(8,128)(2,1)S(1)} %get-tuple-element.44.couple_ref,, ...), custom_call_target="tpu_custom_call" | custom-call | flops 2415919104 | bytes 9437184 | tf_op jit(solution)/shard_map/pallas_call | solution.py:284
  20.2 5.3 %shard_map.168 = (f32[4,128,1024]{2,1,0:T(8,128)S(1)}, f32[8,128]{1,0:T(8,128)S(1)}) custom-call(s32[1,4]{1,0:T(1,128)S(1)} %copy-done, f32[128,2048]{1,0:T(8,128)S(1)} %get-tuple-element.53.own_ref.direction_ref, f32[128,1024]{1,0:T(8,128)S(1)} %collective-permute-done.from_sub_ref, f32[128,1024]{1,0:T(8,128)S(1)} %collective-permute-done.1.from_grp_ref, ...), custom_call_target="tpu_custom_call" | custom-call | flops 3221225472 | bytes 16777216 | tf_op jit(solution)/shard_map/pallas_call | solution.py:345
  25.5 1.7 %collective-permute-start.3 = (f32[8,128]{1,0:T(8,128)S(1)}, f32[8,128]{1,0:T(8,128)S(1)}, u32[]{:S(2)}, u32[]{:S(2)}) collective-permute-start(f32[8,128]{1,0:T(8,128)S(1)} %get-tuple-element.57), channel_id=1, source_target_pairs={{0,1},{1,0},{2,3},{3,2},{4,5},{5,4},{6,7},{7,6},{8,9},{9,8},{10,11... | collective-permute-start | bytes 12296 | tf_op jit(solution)/shard_map/ppermute | solution.py:32
  27.3 3.1 %collective-permute-start.9 = (f32[1160,128]{1,0:T(8,128)S(1)}, f32[1160,128]{1,0:T(8,128)S(1)}, u32[]{:S(2)}, u32[]{:S(2)}) collective-permute-start(f32[1160,128]{1,0:T(8,128)S(1)} %get-tuple-element.61), channel_id=1, source_target_pairs={{0,28},{4,0},{8,4},{12,8},{16,12},{20,16},{24,20},{28,24},{1,29},{... | collective-permute-start | bytes 1781768 | tf_op jit(solution)/shard_map/ppermute | solution.py:23
  32.1 1.9 %collective-permute-start.2 = (f32[128,1024]{1,0:T(8,128)S(1)}, f32[128,1024]{1,0:T(8,128)S(1)}, u32[]{:S(2)}, u32[]{:S(2)}) collective-permute-start(f32[128,1024]{1,0:T(8,128)S(1)} %get-tuple-element.87), channel_id=1, source_target_pairs={{0,28},{4,0},{8,4},{12,8},{16,12},{20,16},{24,20},{28,24},{1,29},{... | collective-permute-start | bytes 1572872 | tf_op jit(solution)/shard_map/ppermute | solution.py:23
  34.0 2.8 %collective-permute-done.4 = f32[8,128]{1,0:T(8,128)S(1)} collective-permute-done((f32[8,128]{1,0:T(8,128)S(1)}, f32[8,128]{1,0:T(8,128)S(1)}, u32[]{:S(2)}, u32[]{:S(2)}) %collective-permute-start.4) | collective-permute-done | bytes 4128 | tf_op jit(solution)/shard_map/ppermute | solution.py:32
  36.8 2.6 %collective-permute-start.6 = (f32[8,128]{1,0:T(8,128)S(1)}, f32[8,128]{1,0:T(8,128)S(1)}, u32[]{:S(2)}, u32[]{:S(2)}) collective-permute-start(f32[8,128]{1,0:T(8,128)S(1)} %add.37), channel_id=1, source_target_pairs={{0,16},{4,20},{8,24},{12,28},{16,0},{20,4},{24,8},{28,12},{1,17},{... | collective-permute-start | bytes 12296 | tf_op jit(solution)/shard_map/ppermute | solution.py:32
  39.4 16.9 %collective-permute-done.6 = f32[8,128]{1,0:T(8,128)S(1)} collective-permute-done((f32[8,128]{1,0:T(8,128)S(1)}, f32[8,128]{1,0:T(8,128)S(1)}, u32[]{:S(2)}, u32[]{:S(2)}) %collective-permute-start.6) | collective-permute-done | bytes 4128 | tf_op jit(solution)/shard_map/ppermute | solution.py:32
  57.9 2.0 %collective-permute-done.7 = f32[8,128]{1,0:T(8,128)S(1)} collective-permute-done((f32[8,128]{1,0:T(8,128)S(1)}, f32[8,128]{1,0:T(8,128)S(1)}, u32[]{:S(2)}, u32[]{:S(2)}) %collective-permute-start.7) | collective-permute-done | bytes 4128 | tf_op jit(solution)/shard_map/ppermute | solution.py:32
  59.9 3.6 %collective-permute-done.8 = f32[8,128]{1,0:T(8,128)S(1)} collective-permute-done((f32[8,128]{1,0:T(8,128)S(1)}, f32[8,128]{1,0:T(8,128)S(1)}, u32[]{:S(2)}, u32[]{:S(2)}) %collective-permute-start.8) | collective-permute-done | bytes 4128 | tf_op jit(solution)/shard_map/ppermute | solution.py:32
  63.6 1.9 %shard_map.169 = (f32[128,2048]{1,0:T(8,128)}, f32[128,2048]{1,0:T(8,128)S(1)}, f32[128,128]{1,0:T(8,128)S(1)}, f32[128,128]{1,0:T(8,128)S(1)}, f32[128,128]{1,0:T(8,128)S(1)}) custom-call(s32[1,4]{1,0:T(1,128)S(1)} %copy-done, f32[4,128,1024]{2,1,0:T(8,128)S(1)} %get-tuple-element.56.y_ref, f32[128,1024]{1,0:T(8,128)S(1)} %collective-permute-done.2.back_sub_ref, ...), custom_call_target="tpu_custom_call" | custom-call | flops 268435456 | bytes 5242880 | tf_op jit(solution)/shard_map/pallas_call | solution.py:429
  65.5 7.0 %collective-permute-done.11.sub_ref = f32[128,128]{1,0:T(8,128)S(1)} collective-permute-done((f32[128,128]{1,0:T(8,128)S(1)}, f32[128,128]{1,0:T(8,128)S(1)}, u32[]{:S(2)}, u32[]{:S(2)}) %collective-permute-start.11) | collective-permute-done | bytes 65568 | tf_op jit(solution)/shard_map/ppermute | solution.py:23
  73.3 3.7 %collective-permute-done.13 = f32[128,128]{1,0:T(8,128)S(1)} collective-permute-done((f32[128,128]{1,0:T(8,128)S(1)}, f32[128,128]{1,0:T(8,128)S(1)}, u32[]{:S(2)}, u32[]{:S(2)}) %collective-permute-start.13) | collective-permute-done | bytes 65568 | tf_op jit(solution)/shard_map/ppermute | solution.py:23
  78.6 2.0 %collective-permute-start.16 = (f32[2,128,128]{2,1,0:T(8,128)S(1)}, f32[2,128,128]{2,1,0:T(8,128)S(1)}, u32[]{:S(2)}, u32[]{:S(2)}) collective-permute-start(f32[2,128,128]{2,1,0:T(8,128)S(1)} %pad_maximum_fusion.refs_0_), channel_id=1, source_target_pairs={{0,8},{4,12},{8,0},{12,4},{16,24},{20,28},{24,16},{28,20},{1,9},{5... | collective-permute-start | bytes 393224 | tf_op jit(solution)/shard_map/ppermute | solution.py:69
  82.0 2.9 %collective-permute-done.15.refs_2_ = f32[2,128,128]{2,1,0:T(8,128)S(1)} collective-permute-done((f32[2,128,128]{2,1,0:T(8,128)S(1)}, f32[2,128,128]{2,1,0:T(8,128)S(1)}, u32[]{:S(2)}, u32[]{:S(2)}) %collective-permute-start.15) | collective-permute-done | bytes 131104 | tf_op jit(solution)/shard_map/ppermute | solution.py:69
  84.9 2.4 %collective-permute-done.17.refs_4_ = f32[2,128,128]{2,1,0:T(8,128)S(1)} collective-permute-done((f32[2,128,128]{2,1,0:T(8,128)S(1)}, f32[2,128,128]{2,1,0:T(8,128)S(1)}, u32[]{:S(2)}, u32[]{:S(2)}) %collective-permute-start.17) | collective-permute-done | bytes 131104 | tf_op jit(solution)/shard_map/ppermute | solution.py:69
  87.4 2.8 %shard_map.170 = (f32[128,2048]{1,0:T(8,128)S(1)}, f32[8,128]{1,0:T(8,128)S(1)}) custom-call(s32[1,4]{1,0:T(1,128)S(1)} %copy-done, f32[128,2048]{1,0:T(8,128)S(1)} %get-tuple-element.63.halved_ref, bf16[32,128,128]{2,1,0:T(8,128)(2,1)S(1)} %get-tuple-element.48.factor_ref, f32[1160,128]{1,0:T(8,128)S(1)} %collective-permute-done.9.aux_sub_ref, ...), custom_call_target="tpu_custom_call" | custom-call | flops 536870912 | bytes 3145728 | tf_op jit(solution)/shard_map/pallas_call | solution.py:546
  93.7 3.1 %collective-permute-done.20 = f32[8,128]{1,0:T(8,128)S(1)} collective-permute-done((f32[8,128]{1,0:T(8,128)S(1)}, f32[8,128]{1,0:T(8,128)S(1)}, u32[]{:S(2)}, u32[]{:S(2)}) %collective-permute-start.20) | collective-permute-done | bytes 4128 | tf_op jit(solution)/shard_map/ppermute | solution.py:32
  98.8 3.1 %collective-permute-done.21 = f32[8,128]{1,0:T(8,128)S(1)} collective-permute-done((f32[8,128]{1,0:T(8,128)S(1)}, f32[8,128]{1,0:T(8,128)S(1)}, u32[]{:S(2)}, u32[]{:S(2)}) %collective-permute-start.21) | collective-permute-done | bytes 4128 | tf_op jit(solution)/shard_map/ppermute | solution.py:46
  102.7 2.8 %collective-permute-done.22 = f32[8,128]{1,0:T(8,128)S(1)} collective-permute-done((f32[8,128]{1,0:T(8,128)S(1)}, f32[8,128]{1,0:T(8,128)S(1)}, u32[]{:S(2)}, u32[]{:S(2)}) %collective-permute-start.22) | collective-permute-done | bytes 4128 | tf_op jit(solution)/shard_map/ppermute | solution.py:46
  105.6 2.3 %shard_map.174 = (f32[128,2048]{1,0:T(8,128)S(1)}, f32[128,2048]{1,0:T(8,128)}) custom-call(s32[1,4]{1,0:T(1,128)S(1)} %copy-done, f32[128,2048]{1,0:T(8,128)S(1)} %get-tuple-element.64.solved_ref, f32[128,128]{1,0:T(8,128)S(1)} %get-tuple-element.76.own_ref, f32[128,128]{1,0:T(8,128)S(1)} %collective-permute-done.23.from_sub_ref, ...), custom_call_target="tpu_custom_call" | custom-call | flops 268435456 | bytes 3145728 | tf_op jit(solution)/shard_map/pallas_call | solution.py:580
  107.9 2.2 %collective-permute-done.25 = f32[8,128]{1,0:T(8,128)S(1)} collective-permute-done((f32[8,128]{1,0:T(8,128)S(1)}, f32[8,128]{1,0:T(8,128)S(1)}, u32[]{:S(2)}, u32[]{:S(2)}) %collective-permute-start.25) | collective-permute-done | bytes 4128 | tf_op jit(solution)/shard_map/ppermute | solution.py:46
  (59 shorter events, 17.4 us)
Async XLA Ops:
  2.0 18.2 %collective-permute-start = (f32[128,1024]{1,0:T(8,128)S(1)}, f32[128,1024]{1,0:T(8,128)S(1)}, u32[]{:S(2)}, u32[]{:S(2)}) collective-permute-start(f32[128,1024]{1,0:T(8,128)S(1)} %get-tuple-element.89), channel_id=1, source_target_pairs={{0,4},{4,8},{8,12},{12,16},{16,20},{20,24},{24,28},{28,0},{1,5},{5... | collective-permute-start | bytes 1572872 | tf_op jit(solution)/shard_map/ppermute | solution.py:23
  5.0 15.2 %collective-permute-start.1 = (f32[128,1024]{1,0:T(8,128)S(1)}, f32[128,1024]{1,0:T(8,128)S(1)}, u32[]{:S(2)}, u32[]{:S(2)}) collective-permute-start(f32[128,1024]{1,0:T(8,128)S(1)} %get-tuple-element.88), channel_id=1, source_target_pairs={{0,1},{1,2},{2,3},{3,0},{4,5},{5,6},{6,7},{7,4},{8,9},{9,10},{10,1... | collective-permute-start | bytes 1572872 | tf_op jit(solution)/shard_map/ppermute | solution.py:23
  25.5 4.9 %collective-permute-start.3 = (f32[8,128]{1,0:T(8,128)S(1)}, f32[8,128]{1,0:T(8,128)S(1)}, u32[]{:S(2)}, u32[]{:S(2)}) collective-permute-start(f32[8,128]{1,0:T(8,128)S(1)} %get-tuple-element.57), channel_id=1, source_target_pairs={{0,1},{1,0},{2,3},{3,2},{4,5},{5,4},{6,7},{7,6},{8,9},{9,8},{10,11... | collective-permute-start | bytes 12296 | tf_op jit(solution)/shard_map/ppermute | solution.py:32
  27.1 36.4 %collective-permute-start.10 = (f32[1160,128]{1,0:T(8,128)S(1)}, f32[1160,128]{1,0:T(8,128)S(1)}, u32[]{:S(2)}, u32[]{:S(2)}) collective-permute-start(f32[1160,128]{1,0:T(8,128)S(1)} %get-tuple-element.62), channel_id=1, source_target_pairs={{0,3},{1,0},{2,1},{3,2},{4,7},{5,4},{6,5},{7,6},{8,11},{9,8},{10,9... | collective-permute-start | bytes 1781768 | tf_op jit(solution)/shard_map/ppermute | solution.py:23
  27.3 36.3 %collective-permute-start.9 = (f32[1160,128]{1,0:T(8,128)S(1)}, f32[1160,128]{1,0:T(8,128)S(1)}, u32[]{:S(2)}, u32[]{:S(2)}) collective-permute-start(f32[1160,128]{1,0:T(8,128)S(1)} %get-tuple-element.61), channel_id=1, source_target_pairs={{0,28},{4,0},{8,4},{12,8},{16,12},{20,16},{24,20},{28,24},{1,29},{... | collective-permute-start | bytes 1781768 | tf_op jit(solution)/shard_map/ppermute | solution.py:23
  30.4 6.4 %collective-permute-start.4 = (f32[8,128]{1,0:T(8,128)S(1)}, f32[8,128]{1,0:T(8,128)S(1)}, u32[]{:S(2)}, u32[]{:S(2)}) collective-permute-start(f32[8,128]{1,0:T(8,128)S(1)} %add.36), channel_id=1, source_target_pairs={{0,2},{1,3},{2,0},{3,1},{4,6},{5,7},{6,4},{7,5},{8,10},{9,11},{10,... | collective-permute-start | bytes 12296 | tf_op jit(solution)/shard_map/ppermute | solution.py:32
  32.1 31.4 %collective-permute-start.2 = (f32[128,1024]{1,0:T(8,128)S(1)}, f32[128,1024]{1,0:T(8,128)S(1)}, u32[]{:S(2)}, u32[]{:S(2)}) collective-permute-start(f32[128,1024]{1,0:T(8,128)S(1)} %get-tuple-element.87), channel_id=1, source_target_pairs={{0,28},{4,0},{8,4},{12,8},{16,12},{20,16},{24,20},{28,24},{1,29},{... | collective-permute-start | bytes 1572872 | tf_op jit(solution)/shard_map/ppermute | solution.py:23
  36.8 26.8 %collective-permute-start.5 = (f32[128,1024]{1,0:T(8,128)S(1)}, f32[128,1024]{1,0:T(8,128)S(1)}, u32[]{:S(2)}, u32[]{:S(2)}) collective-permute-start(f32[128,1024]{1,0:T(8,128)S(1)} %get-tuple-element.58), channel_id=1, source_target_pairs={{0,3},{1,0},{2,1},{3,2},{4,7},{5,4},{6,5},{7,6},{8,11},{9,8},{10,9... | collective-permute-start | bytes 1572872 | tf_op jit(solution)/shard_map/ppermute | solution.py:23
  36.8 19.5 %collective-permute-start.6 = (f32[8,128]{1,0:T(8,128)S(1)}, f32[8,128]{1,0:T(8,128)S(1)}, u32[]{:S(2)}, u32[]{:S(2)}) collective-permute-start(f32[8,128]{1,0:T(8,128)S(1)} %add.37), channel_id=1, source_target_pairs={{0,16},{4,20},{8,24},{12,28},{16,0},{20,4},{24,8},{28,12},{1,17},{... | collective-permute-start | bytes 12296 | tf_op jit(solution)/shard_map/ppermute | solution.py:32
  56.3 3.6 %collective-permute-start.7 = (f32[8,128]{1,0:T(8,128)S(1)}, f32[8,128]{1,0:T(8,128)S(1)}, u32[]{:S(2)}, u32[]{:S(2)}) collective-permute-start(f32[8,128]{1,0:T(8,128)S(1)} %add.38), channel_id=1, source_target_pairs={{0,8},{4,12},{8,0},{12,4},{16,24},{20,28},{24,16},{28,20},{1,9},{5... | collective-permute-start | bytes 12296 | tf_op jit(solution)/shard_map/ppermute | solution.py:32
  59.9 3.6 %collective-permute-start.8 = (f32[8,128]{1,0:T(8,128)S(1)}, f32[8,128]{1,0:T(8,128)S(1)}, u32[]{:S(2)}, u32[]{:S(2)}) collective-permute-start(f32[8,128]{1,0:T(8,128)S(1)} %add.39), channel_id=1, source_target_pairs={{0,4},{4,0},{8,12},{12,8},{16,20},{20,16},{24,28},{28,24},{1,5},{5... | collective-permute-start | bytes 12296 | tf_op jit(solution)/shard_map/ppermute | solution.py:32
  65.5 7.0 %collective-permute-start.11 = (f32[128,128]{1,0:T(8,128)S(1)}, f32[128,128]{1,0:T(8,128)S(1)}, u32[]{:S(2)}, u32[]{:S(2)}) collective-permute-start(f32[128,128]{1,0:T(8,128)S(1)} %get-tuple-element.66), channel_id=1, source_target_pairs={{0,4},{4,8},{8,12},{12,16},{16,20},{20,24},{24,28},{28,0},{1,5},{5... | collective-permute-start | bytes 196616 | tf_op jit(solution)/shard_map/ppermute | solution.py:23
  65.5 7.0 %collective-permute-start.12 = (f32[128,128]{1,0:T(8,128)S(1)}, f32[128,128]{1,0:T(8,128)S(1)}, u32[]{:S(2)}, u32[]{:S(2)}) collective-permute-start(f32[128,128]{1,0:T(8,128)S(1)} %get-tuple-element.67), channel_id=1, source_target_pairs={{0,1},{1,2},{2,3},{3,0},{4,5},{5,6},{6,7},{7,4},{8,9},{9,10},{10,1... | collective-permute-start | bytes 196616 | tf_op jit(solution)/shard_map/ppermute | solution.py:23
  72.7 4.3 %collective-permute-start.13 = (f32[128,128]{1,0:T(8,128)S(1)}, f32[128,128]{1,0:T(8,128)S(1)}, u32[]{:S(2)}, u32[]{:S(2)}) collective-permute-start(f32[128,128]{1,0:T(8,128)S(1)} %get-tuple-element.69.first_ref), channel_id=1, source_target_pairs={{0,2},{1,3},{2,0},{3,1},{4,6},{5,7},{6,4},{7,5},{8,10},{9,11},{10,... | collective-permute-start | bytes 196616 | tf_op jit(solution)/shard_map/ppermute | solution.py:23
  77.0 5.0 %collective-permute-start.14 = (f32[2,128,128]{2,1,0:T(8,128)S(1)}, f32[2,128,128]{2,1,0:T(8,128)S(1)}, u32[]{:S(2)}, u32[]{:S(2)}) collective-permute-start(f32[2,128,128]{2,1,0:T(8,128)S(1)} %pad_maximum_fusion.refs_0_), channel_id=1, source_target_pairs={{0,4},{4,0},{8,12},{12,8},{16,20},{20,16},{24,28},{28,24},{1,5},{5... | collective-permute-start | bytes 393224 | tf_op jit(solution)/shard_map/ppermute | solution.py:69
  77.1 7.8 %collective-permute-start.15 = (f32[2,128,128]{2,1,0:T(8,128)S(1)}, f32[2,128,128]{2,1,0:T(8,128)S(1)}, u32[]{:S(2)}, u32[]{:S(2)}) collective-permute-start(f32[2,128,128]{2,1,0:T(8,128)S(1)} %pad_maximum_fusion.refs_0_), channel_id=1, source_target_pairs={{0,28},{4,8},{8,4},{12,16},{16,12},{20,24},{24,20},{28,0},{1,29},{... | collective-permute-start | bytes 393224 | tf_op jit(solution)/shard_map/ppermute | solution.py:69
  78.6 6.3 %collective-permute-start.16 = (f32[2,128,128]{2,1,0:T(8,128)S(1)}, f32[2,128,128]{2,1,0:T(8,128)S(1)}, u32[]{:S(2)}, u32[]{:S(2)}) collective-permute-start(f32[2,128,128]{2,1,0:T(8,128)S(1)} %pad_maximum_fusion.refs_0_), channel_id=1, source_target_pairs={{0,8},{4,12},{8,0},{12,4},{16,24},{20,28},{24,16},{28,20},{1,9},{5... | collective-permute-start | bytes 393224 | tf_op jit(solution)/shard_map/ppermute | solution.py:69
  80.6 6.8 %collective-permute-start.17 = (f32[2,128,128]{2,1,0:T(8,128)S(1)}, f32[2,128,128]{2,1,0:T(8,128)S(1)}, u32[]{:S(2)}, u32[]{:S(2)}) collective-permute-start(f32[2,128,128]{2,1,0:T(8,128)S(1)} %pad_maximum_fusion.refs_0_), channel_id=1, source_target_pairs={{0,24},{4,28},{8,16},{12,20},{16,8},{20,12},{24,0},{28,4},{1,25},{... | collective-permute-start | bytes 393224 | tf_op jit(solution)/shard_map/ppermute | solution.py:69
  93.1 3.6 %collective-permute-start.20 = (f32[8,128]{1,0:T(8,128)S(1)}, f32[8,128]{1,0:T(8,128)S(1)}, u32[]{:S(2)}, u32[]{:S(2)}) collective-permute-start(f32[8,128]{1,0:T(8,128)S(1)} %add.41), channel_id=1, source_target_pairs={{0,2},{1,3},{2,0},{3,1},{4,6},{5,7},{6,4},{7,5},{8,10},{9,11},{10,... | collective-permute-start | bytes 12296 | tf_op jit(solution)/shard_map/ppermute | solution.py:32
  96.7 8.8 %collective-permute-start.23 = (f32[128,128]{1,0:T(8,128)S(1)}, f32[128,128]{1,0:T(8,128)S(1)}, u32[]{:S(2)}, u32[]{:S(2)}) collective-permute-start(f32[128,128]{1,0:T(8,128)S(1)} %get-tuple-element.76.own_ref), channel_id=1, source_target_pairs={{0,28},{4,0},{8,4},{12,8},{16,12},{20,16},{24,20},{28,24},{1,29},{... | collective-permute-start | bytes 196616 | tf_op jit(solution)/shard_map/ppermute | solution.py:23
  98.3 7.2 %collective-permute-start.24 = (f32[128,128]{1,0:T(8,128)S(1)}, f32[128,128]{1,0:T(8,128)S(1)}, u32[]{:S(2)}, u32[]{:S(2)}) collective-permute-start(f32[128,128]{1,0:T(8,128)S(1)} %get-tuple-element.76.own_ref), channel_id=1, source_target_pairs={{0,3},{1,0},{2,1},{3,2},{4,7},{5,4},{6,5},{7,6},{8,11},{9,8},{10,9... | collective-permute-start | bytes 196616 | tf_op jit(solution)/shard_map/ppermute | solution.py:23
  98.3 3.6 %collective-permute-start.21 = (f32[8,128]{1,0:T(8,128)S(1)}, f32[8,128]{1,0:T(8,128)S(1)}, u32[]{:S(2)}, u32[]{:S(2)}) collective-permute-start(f32[8,128]{1,0:T(8,128)S(1)} %add.42), channel_id=1, source_target_pairs={{0,4},{4,0},{8,12},{12,8},{16,20},{20,16},{24,28},{28,24},{1,5},{5... | collective-permute-start | bytes 12296 | tf_op jit(solution)/shard_map/ppermute | solution.py:46
  101.9 3.6 %collective-permute-start.22 = (f32[8,128]{1,0:T(8,128)S(1)}, f32[8,128]{1,0:T(8,128)S(1)}, u32[]{:S(2)}, u32[]{:S(2)}) collective-permute-start(f32[8,128]{1,0:T(8,128)S(1)} %add.43), channel_id=1, source_target_pairs={{0,8},{4,12},{8,0},{12,4},{16,24},{20,28},{24,16},{28,20},{1,9},{5... | collective-permute-start | bytes 12296 | tf_op jit(solution)/shard_map/ppermute | solution.py:46
  105.5 4.6 %collective-permute-start.25 = (f32[8,128]{1,0:T(8,128)S(1)}, f32[8,128]{1,0:T(8,128)S(1)}, u32[]{:S(2)}, u32[]{:S(2)}) collective-permute-start(f32[8,128]{1,0:T(8,128)S(1)} %add.44), channel_id=1, source_target_pairs={{0,16},{4,20},{8,24},{12,28},{16,0},{20,4},{24,8},{28,12},{1,17},{... | collective-permute-start | bytes 12296 | tf_op jit(solution)/shard_map/ppermute | solution.py:46
  (5 other events, 116.6 us)

commit v4 on v3

--- a/solution.py
+++ b/solution.py
@@ -383,13 +383,12 @@
     )(slots, blocks, basis, factor)
 
 
-def update_body(slots_ref, y_ref, back_sub_ref, back_grp_ref, residual_ref, curve_ref, product_ref, block_ref, basis_ref, aux_sub_ref, aux_grp_ref, residual_out, half_out, own_out, sub_out, grp_out):
-    width = basis_ref.shape[1]
-    prims = basis_ref.shape[0]
+def image_body(slots_ref, y_ref, back_sub_ref, back_grp_ref, residual_ref, block_ref, basis_ref, aux_sub_ref, aux_grp_ref, image_out, own_out, sub_out, grp_out):
+    prims, width = basis_ref.shape
     face_width = back_sub_ref.shape[1]
     per_face = face_width // width
     rows = face_width
-    scale = per_row(product_ref[...] / curve_ref[...], width)
+    loads = residual_ref.shape[0]
     basis = basis_ref[...].astype(F32).T
     own_total = None
     for which, back, aux, out in (
@@ -400,60 +399,86 @@
         other = aux[rows : rows + prims, :].T
         own_near = block_ref[...] - slots_ref[0, which] * per_face
         other_near = aux[rows + prims : rows + prims + 1, :]
-        lefts = []
-        rights = []
+        both = None
         for b in range(per_face):
             cols = slice(b * width, (b + 1) * width)
+            wide = slice(offset + b * width, offset + (b + 1) * width)
             image = y_ref[which, :, cols] + back[:, cols]
-            fresh = residual_ref[:, offset + b * width : offset + (b + 1) * width] - scale * image
-            residual_out[:, offset + b * width : offset + (b + 1) * width] = fresh
-            half = fresh * 0.5
-            half_out[:, offset + b * width : offset + (b + 1) * width] = half
-            lefts.append(half)
+            image_out[:, wide] = image
+            image_high, image_low = split(image)
+            high, low = split(residual_ref[:, wide])
+            left = jnp.concatenate(
+                [jnp.concatenate([image_high, image_low], 1), jnp.concatenate([high, low], 1)], 0
+            )
             mine = jnp.where(own_near == b, basis, 0.0).astype(BF16)
             theirs = jnp.where(other_near == b, other, 0.0).astype(BF16)
-            rights.append(jnp.concatenate([mine, theirs], 1))
-        high, low = split(jnp.concatenate(lefts, 1))
-        right = jnp.concatenate(rights, 0)
-        both = mm(high, right) + mm(low, right)
+            term = mm(left, twice(jnp.concatenate([mine, theirs], 1), 0))
+            both = term if both is None else both + term
         own = both[:, :prims]
         own_total = own if own_total is None else own_total + own
-        out[...] = both[:, prims:]
-    own_out[...] = own_total
-
-
-def update(slots, y, back_sub, back_grp, residual, curve, product, blocks, basis, aux_sub, aux_grp):
+        out[0] = both[:loads, prims:] * 0.5
+        out[1] = both[loads:, prims:] * 0.5
+    own_out[0] = own_total[:loads] * 0.5
+    own_out[1] = own_total[loads:] * 0.5
+
+
+def find_image(slots, y, back_sub, back_grp, residual, blocks, basis, aux_sub, aux_grp):
     loads = residual.shape[0]
     prims = basis.shape[0]
-    small = jax.ShapeDtypeStruct((loads, prims), F32)
-    return call(
-        update_body,
-        (jax.ShapeDtypeStruct(residual.shape, F32), jax.ShapeDtypeStruct(residual.shape, F32), small, small, small),
-        flops=residual.size * prims * 8,
+    small = jax.ShapeDtypeStruct((2, loads, prims), F32)
+    return call(
+        image_body,
+        (jax.ShapeDtypeStruct(residual.shape, F32), small, small, small),
+        flops=residual.size * prims * 16,
         moved=residual.size * 20,
-        in_specs=[SMEM] + [VMEM] * 10,
-        out_specs=(VMEM,) * 5,
-        limit=16 * 1024 * 1024,
-    )(slots, y, back_sub, back_grp, residual, curve, product, blocks, basis, aux_sub, aux_grp)
-
-
-def first_body(own_ref, sub_ref, grp_ref, inverse_ref, coarse_out, first_out):
-    coarse = own_ref[...] + sub_ref[...] + grp_ref[...]
+        in_specs=[SMEM] + [VMEM] * 8,
+        out_specs=(VMEM,) * 4,
+        limit=8 * 1024 * 1024,
+    )(slots, y, back_sub, back_grp, residual, blocks, basis, aux_sub, aux_grp)
+
+
+def advance_body(image_ref, residual_ref, curve_ref, product_ref, residual_out, half_out):
+    width = curve_ref.shape[1]
+    scale = per_row(product_ref[...] / curve_ref[...], width)
+    for b in range(image_ref.shape[1] // width):
+        cols = slice(b * width, (b + 1) * width)
+        fresh = residual_ref[:, cols] - scale * image_ref[:, cols]
+        residual_out[:, cols] = fresh
+        half_out[:, cols] = fresh * 0.5
+
+
+def advance(image, residual, curve, product):
+    shape = jax.ShapeDtypeStruct(residual.shape, F32)
+    return call(
+        advance_body,
+        (shape, shape),
+        flops=residual.size * 400,
+        moved=residual.size * 16,
+        in_specs=[VMEM] * 4,
+        out_specs=(VMEM,) * 2,
+        limit=4 * 1024 * 1024,
+    )(image, residual, curve, product)
+
+
+def first_body(own_ref, sub_ref, grp_ref, curve_ref, product_ref, inverse_ref, coarse_out, first_out):
+    scale = per_row(product_ref[...] / curve_ref[...], own_ref.shape[2])
+    parts = own_ref[...] + sub_ref[...] + grp_ref[...]
+    coarse = parts[1] - scale * parts[0]
     coarse_out[...] = coarse
     first_out[...] = mm3(coarse, inverse_ref[...])
 
 
-def first_step(own, sub, grp, inverse):
-    shape = jax.ShapeDtypeStruct(own.shape, F32)
+def first_step(own, sub, grp, curve, product, inverse):
+    shape = jax.ShapeDtypeStruct(own.shape[1:], F32)
     return call(
         first_body,
         (shape, shape),
         flops=own.size * 128 * 6,
         moved=own.size * 24,
-        in_specs=[VMEM] * 4,
+        in_specs=[VMEM] * 6,
         out_specs=(VMEM,) * 2,
         limit=4 * 1024 * 1024,
-    )(own, sub, grp, inverse)
+    )(own, sub, grp, curve, product, inverse)
 
 
 def merge_body(*refs):
@@ -630,16 +655,18 @@
     lower, curve = lax.optimization_barrier((y[2], curve))
     back_grp = shifted(lower, "grp", -1)
     curve = total(curve, "sub")
-    fresh, halved, part, part_sub, part_grp = update(
-        neighbor_slots, y, back_sub, back_grp, old, curve, product, blocks, basis, aux_sub, aux_grp
+    image, part, part_sub, part_grp = find_image(
+        neighbor_slots, y, back_sub, back_grp, old, blocks, basis, aux_sub, aux_grp
     )
     part_sub = shifted(part_sub, "sub", 1)
     part_grp = shifted(part_grp, "grp", 1)
+    coarse, first = first_step(part, part_sub, part_grp, curve, product, inverse)
+    fresh, halved = advance(image, old, curve, product)
     solved, local = local_solve(neighbor_slots, halved, factor, aux_sub, aux_grp)
-    coarse, first = first_step(part, part_sub, part_grp, inverse)
 
     if grp_count == 4:
-        group = jnp.stack([first, shifted(first, "grp", 2)], 0)
+        beyond = shifted(first, "grp", 2)
+        group = jnp.stack([first, beyond], 0)
     else:
         group = lax.all_gather(first[None], "grp", axis=0, tiled=True)
     window = merge([group] + sub_window(group))

time: 112 us -> 112 us (level)
  waiting for transfers between devices: 54.3 us -> 48.9 us
  starting transfers between devices: 24.4 us -> 29.3 us
    ppermute x7, waiting for transfers between devices: 29.3 us -> 16.4 us  [total(): lax.ppermute(value, axis, [(i, i ^ bit) for i in range(count)])]
    ppermute x11, waiting for transfers between devices: 10.7 us -> 18.5 us  [shifted(): return lax.ppermute(value, axis, pairs)]
    ppermute x4, starting transfers between devices: 4.21 us -> 6.15 us  [sub_window(): pieces.append(lax.ppermute(group, 'sub', list(zip(everyone, target))))]
    ppermute x11, starting transfers between devices: 10.3 us -> 12 us  [shifted(): return lax.ppermute(value, axis, pairs)]
    pallas_call x1 -> x2, Pallas kernels: 1.94 us -> 2.56 us  [the longest x1 1.37 us: find_image(): call(image_body, (jax.ShapeDtypeStruct(residual.shape, F32), small, small...]
  transfers between devices with their start and end apart: 26 -> 26, of which waited for: 14 -> 15; matrix products, arithmetic and copies ran while one was open for 0% -> 0% of each run, Pallas kernels for 18% -> 19%
where the time goes in v4:
time: 112 us
  waiting for transfers between devices  48.9 us (44%)
  Pallas kernels  29.9 us (27%)
  starting transfers between devices  29.3 us (26%)
  other arithmetic  1.7 us (2%)
  local copies, waits for them, and re-layouts  1.41 us (1%)
    ppermute x11, waiting for transfers between devices, shifted(): return lax.ppermute(value, axis, pairs)  18.5 us
    ppermute x7, waiting for transfers between devices, total(): lax.ppermute(value, axis, [(i, i ^ bit) for i in range(count)])  16.4 us
    ppermute x11, starting transfers between devices, shifted(): return lax.ppermute(value, axis, pairs)  12 us
    ppermute x7, starting transfers between devices, total(): lax.ppermute(value, axis, [(i, i ^ bit) for i in range(count)])  9.32 us
    pallas_call x1, Pallas kernels, prepare(): call(functools.partial(prepare_body, len(keep)), (jax.ShapeDtypeStruct(co...  7.84 us
    ppermute x3, waiting for transfers between devices, total_with(): lax.ppermute(value, axis, [(i, i ^ bit) for i in range(count)])  7.75 us
    pallas_call x1, Pallas kernels, assemble(): call(functools.partial(assemble_body, blocks, len(keep)), (shape, shape)...  6.7 us
    ppermute x4, waiting for transfers between devices, sub_window(): pieces.append(lax.ppermute(group, 'sub', list(zip(everyone, target))))  6.3 us
  transfers between devices with their start and end apart: 26, of which 15 were waited for; matrix products, arithmetic and copies ran while one was open for 0% of the time, Pallas kernels for 19%

profile of v4, /device:TPU:0, one launch (start us, length us, event | category | flops | bytes accessed | tf_op | source)
XLA Modules:
  0.0 112.0 jit_solution(18276007446277017100)
XLA Ops:
  2.0 3.0 %collective-permute-start = (f32[128,1024]{1,0:T(8,128)S(1)}, f32[128,1024]{1,0:T(8,128)S(1)}, u32[]{:S(2)}, u32[]{:S(2)}) collective-permute-start(f32[128,1024]{1,0:T(8,128)S(1)} %get-tuple-element.91), channel_id=1, source_target_pairs={{0,4},{4,8},{8,12},{12,16},{16,20},{20,24},{24,28},{28,0},{1,5},{5... | collective-permute-start | bytes 1572872 | tf_op jit(solution)/shard_map/ppermute | solution.py:23
  5.0 7.8 %shard_map.165 = (bf16[96,256,128]{2,1,0:T(8,128)(2,1)S(1)}, bf16[96,256,256]{2,1,0:T(8,128)(2,1)S(1)}, bf16[32,128,128]{2,1,0:T(8,128)(2,1)S(1)}, bf16[32,128,1...) custom-call(bf16[96,256,128]{2,1,0:T(8,128)(2,1)} %bitcast.28, ...), custom_call_target="tpu_custom_call" | custom-call | flops 2415919104 | bytes 9437184 | tf_op jit(solution)/shard_map/pallas_call | solution.py:193
  13.5 6.7 %shard_map.167 = (bf16[16,8,128,256]{3,2,1,0:T(8,128)(2,1)S(1)}, bf16[16,8,128,256]{3,2,1,0:T(8,128)(2,1)S(1)}, f32[128,2048]{1,0:T(8,128)S(1)}, f32[128,2048]{1...) custom-call(bf16[96,256,128]{2,1,0:T(8,128)(2,1)S(1)} %get-tuple-element.45.couple_ref,, ...), custom_call_target="tpu_custom_call" | custom-call | flops 2415919104 | bytes 9437184 | tf_op jit(solution)/shard_map/pallas_call | solution.py:284
  20.2 5.3 %shard_map.168 = (f32[4,128,1024]{2,1,0:T(8,128)S(1)}, f32[8,128]{1,0:T(8,128)S(1)}) custom-call(s32[1,4]{1,0:T(1,128)S(1)} %copy-done, f32[128,2048]{1,0:T(8,128)S(1)} %get-tuple-element.54.own_ref.direction_ref, f32[128,1024]{1,0:T(8,128)S(1)} %collective-permute-done.from_sub_ref, f32[128,1024]{1,0:T(8,128)S(1)} %collective-permute-done.1.from_grp_ref, ...), custom_call_target="tpu_custom_call" | custom-call | flops 3221225472 | bytes 16777216 | tf_op jit(solution)/shard_map/pallas_call | solution.py:345
  27.1 3.2 %collective-permute-start.6 = (f32[1160,128]{1,0:T(8,128)S(1)}, f32[1160,128]{1,0:T(8,128)S(1)}, u32[]{:S(2)}, u32[]{:S(2)}) collective-permute-start(f32[1160,128]{1,0:T(8,128)S(1)} %get-tuple-element.61), channel_id=1, source_target_pairs={{0,28},{4,0},{8,4},{12,8},{16,12},{20,16},{24,20},{28,24},{1,29},{... | collective-permute-start | bytes 1781768 | tf_op jit(solution)/shard_map/ppermute | solution.py:23
  31.8 1.9 %collective-permute-start.2 = (f32[128,1024]{1,0:T(8,128)S(1)}, f32[128,1024]{1,0:T(8,128)S(1)}, u32[]{:S(2)}, u32[]{:S(2)}) collective-permute-start(f32[128,1024]{1,0:T(8,128)S(1)} %get-tuple-element.89), channel_id=1, source_target_pairs={{0,28},{4,0},{8,4},{12,8},{16,12},{20,16},{24,20},{28,24},{1,29},{... | collective-permute-start | bytes 1572872 | tf_op jit(solution)/shard_map/ppermute | solution.py:23
  33.7 6.0 %collective-permute-done.4 = f32[8,128]{1,0:T(8,128)S(1)} collective-permute-done((f32[8,128]{1,0:T(8,128)S(1)}, f32[8,128]{1,0:T(8,128)S(1)}, u32[]{:S(2)}, u32[]{:S(2)}) %collective-permute-start.4) | collective-permute-done | bytes 4128 | tf_op jit(solution)/shard_map/ppermute | solution.py:32
  39.7 4.5 %collective-permute-done.6.aux_sub_ref = f32[1160,128]{1,0:T(8,128)S(1)} collective-permute-done((f32[1160,128]{1,0:T(8,128)S(1)}, f32[1160,128]{1,0:T(8,128)S(1)}, u32[]{:S(2)}, u32[]{:S(2)}) %collective-permute-start.6) | collective-permute-done | bytes 593952 | tf_op jit(solution)/shard_map/ppermute | solution.py:23
  44.2 10.3 %collective-permute-done.2.back_sub_ref = f32[128,1024]{1,0:T(8,128)S(1)} collective-permute-done((f32[128,1024]{1,0:T(8,128)S(1)}, f32[128,1024]{1,0:T(8,128)S(1)}, u32[]{:S(2)}, u32[]{:S(2)}) %collective-permute-start.2) | collective-permute-done | bytes 524320 | tf_op jit(solution)/shard_map/ppermute | solution.py:23
  55.8 1.7 %collective-permute-start.11 = (f32[2,128,128]{2,1,0:T(8,128)S(1)}, f32[2,128,128]{2,1,0:T(8,128)S(1)}, u32[]{:S(2)}, u32[]{:S(2)}) collective-permute-start(f32[2,128,128]{2,1,0:T(8,128)S(1)} %get-tuple-element.68), channel_id=1, source_target_pairs={{0,4},{4,8},{8,12},{12,16},{16,20},{20,24},{24,28},{28,0},{1,5},{5... | collective-permute-start | bytes 393224 | tf_op jit(solution)/shard_map/ppermute | solution.py:23
  57.6 2.6 %collective-permute-start.8 = (f32[8,128]{1,0:T(8,128)S(1)}, f32[8,128]{1,0:T(8,128)S(1)}, u32[]{:S(2)}, u32[]{:S(2)}) collective-permute-start(f32[8,128]{1,0:T(8,128)S(1)} %add.37), channel_id=1, source_target_pairs={{0,16},{4,20},{8,24},{12,28},{16,0},{20,4},{24,8},{28,12},{1,17},{... | collective-permute-start | bytes 12296 | tf_op jit(solution)/shard_map/ppermute | solution.py:32
  60.2 1.9 %collective-permute-done.8 = f32[8,128]{1,0:T(8,128)S(1)} collective-permute-done((f32[8,128]{1,0:T(8,128)S(1)}, f32[8,128]{1,0:T(8,128)S(1)}, u32[]{:S(2)}, u32[]{:S(2)}) %collective-permute-start.8) | collective-permute-done | bytes 4128 | tf_op jit(solution)/shard_map/ppermute | solution.py:32
  63.8 1.9 %collective-permute-done.9 = f32[8,128]{1,0:T(8,128)S(1)} collective-permute-done((f32[8,128]{1,0:T(8,128)S(1)}, f32[8,128]{1,0:T(8,128)S(1)}, u32[]{:S(2)}, u32[]{:S(2)}) %collective-permute-start.9) | collective-permute-done | bytes 4128 | tf_op jit(solution)/shard_map/ppermute | solution.py:32
  66.8 2.5 %collective-permute-done.10 = f32[8,128]{1,0:T(8,128)S(1)} collective-permute-done((f32[8,128]{1,0:T(8,128)S(1)}, f32[8,128]{1,0:T(8,128)S(1)}, u32[]{:S(2)}, u32[]{:S(2)}) %collective-permute-start.10) | collective-permute-done | bytes 4128 | tf_op jit(solution)/shard_map/ppermute | solution.py:32
  70.2 3.7 %collective-permute-done.13 = f32[128,128]{1,0:T(8,128)S(1)} collective-permute-done((f32[128,128]{1,0:T(8,128)S(1)}, f32[128,128]{1,0:T(8,128)S(1)}, u32[]{:S(2)}, u32[]{:S(2)}) %collective-permute-start.13) | collective-permute-done | bytes 65568 | tf_op jit(solution)/shard_map/ppermute | solution.py:23
  75.1 4.4 %collective-permute-start.15 = (f32[2,128,128]{2,1,0:T(8,128)S(1)}, f32[2,128,128]{2,1,0:T(8,128)S(1)}, u32[]{:S(2)}, u32[]{:S(2)}) collective-permute-start(f32[2,128,128]{2,1,0:T(8,128)S(1)} %pad_maximum_fusion.refs_0_), channel_id=1, source_target_pairs={{0,28},{4,8},{8,4},{12,16},{16,12},{20,24},{24,20},{28,0},{1,29},{... | collective-permute-start | bytes 393224 | tf_op jit(solution)/shard_map/ppermute | solution.py:69
  80.1 2.8 %collective-permute-done.15.refs_2_ = f32[2,128,128]{2,1,0:T(8,128)S(1)} collective-permute-done((f32[2,128,128]{2,1,0:T(8,128)S(1)}, f32[2,128,128]{2,1,0:T(8,128)S(1)}, u32[]{:S(2)}, u32[]{:S(2)}) %collective-permute-start.15) | collective-permute-done | bytes 131104 | tf_op jit(solution)/shard_map/ppermute | solution.py:69
  84.5 1.9 %collective-permute-done.17.refs_4_ = f32[2,128,128]{2,1,0:T(8,128)S(1)} collective-permute-done((f32[2,128,128]{2,1,0:T(8,128)S(1)}, f32[2,128,128]{2,1,0:T(8,128)S(1)}, u32[]{:S(2)}, u32[]{:S(2)}) %collective-permute-start.17) | collective-permute-done | bytes 131104 | tf_op jit(solution)/shard_map/ppermute | solution.py:69
  87.7 2.8 %shard_map.171 = (f32[128,2048]{1,0:T(8,128)S(1)}, f32[8,128]{1,0:T(8,128)S(1)}) custom-call(s32[1,4]{1,0:T(1,128)S(1)} %copy-done, f32[128,2048]{1,0:T(8,128)S(1)} %get-tuple-element.65.halved_ref, bf16[32,128,128]{2,1,0:T(8,128)(2,1)S(1)} %get-tuple-element.49.factor_ref, f32[1160,128]{1,0:T(8,128)S(1)} %collective-permute-done.6.aux_sub_ref, ...), custom_call_target="tpu_custom_call" | custom-call | flops 536870912 | bytes 3145728 | tf_op jit(solution)/shard_map/pallas_call | solution.py:571
  93.8 3.2 %collective-permute-done.20 = f32[8,128]{1,0:T(8,128)S(1)} collective-permute-done((f32[8,128]{1,0:T(8,128)S(1)}, f32[8,128]{1,0:T(8,128)S(1)}, u32[]{:S(2)}, u32[]{:S(2)}) %collective-permute-start.20) | collective-permute-done | bytes 4128 | tf_op jit(solution)/shard_map/ppermute | solution.py:32
  99.0 3.1 %collective-permute-done.21 = f32[8,128]{1,0:T(8,128)S(1)} collective-permute-done((f32[8,128]{1,0:T(8,128)S(1)}, f32[8,128]{1,0:T(8,128)S(1)}, u32[]{:S(2)}, u32[]{:S(2)}) %collective-permute-start.21) | collective-permute-done | bytes 4128 | tf_op jit(solution)/shard_map/ppermute | solution.py:46
  102.8 2.9 %collective-permute-done.22 = f32[8,128]{1,0:T(8,128)S(1)} collective-permute-done((f32[8,128]{1,0:T(8,128)S(1)}, f32[8,128]{1,0:T(8,128)S(1)}, u32[]{:S(2)}, u32[]{:S(2)}) %collective-permute-start.22) | collective-permute-done | bytes 4128 | tf_op jit(solution)/shard_map/ppermute | solution.py:46
  106.3 2.3 %shard_map.175 = (f32[128,2048]{1,0:T(8,128)S(1)}, f32[128,2048]{1,0:T(8,128)}) custom-call(s32[1,4]{1,0:T(1,128)S(1)} %copy-done, f32[128,2048]{1,0:T(8,128)S(1)} %get-tuple-element.66.solved_ref, f32[128,128]{1,0:T(8,128)S(1)} %get-tuple-element.78.own_ref, f32[128,128]{1,0:T(8,128)S(1)} %collective-permute-done.23.from_sub_ref, ...), custom_call_target="tpu_custom_call" | custom-call | flops 268435456 | bytes 3145728 | tf_op jit(solution)/shard_map/pallas_call | solution.py:605
  108.5 1.8 %collective-permute-done.25 = f32[8,128]{1,0:T(8,128)S(1)} collective-permute-done((f32[8,128]{1,0:T(8,128)S(1)}, f32[8,128]{1,0:T(8,128)S(1)}, u32[]{:S(2)}, u32[]{:S(2)}) %collective-permute-start.25) | collective-permute-done | bytes 4128 | tf_op jit(solution)/shard_map/ppermute | solution.py:46
  (60 shorter events, 23.0 us)
Async XLA Ops:
  2.0 18.2 %collective-permute-start = (f32[128,1024]{1,0:T(8,128)S(1)}, f32[128,1024]{1,0:T(8,128)S(1)}, u32[]{:S(2)}, u32[]{:S(2)}) collective-permute-start(f32[128,1024]{1,0:T(8,128)S(1)} %get-tuple-element.91), channel_id=1, source_target_pairs={{0,4},{4,8},{8,12},{12,16},{16,20},{20,24},{24,28},{28,0},{1,5},{5... | collective-permute-start | bytes 1572872 | tf_op jit(solution)/shard_map/ppermute | solution.py:23
  5.0 15.2 %collective-permute-start.1 = (f32[128,1024]{1,0:T(8,128)S(1)}, f32[128,1024]{1,0:T(8,128)S(1)}, u32[]{:S(2)}, u32[]{:S(2)}) collective-permute-start(f32[128,1024]{1,0:T(8,128)S(1)} %get-tuple-element.90), channel_id=1, source_target_pairs={{0,1},{1,2},{2,3},{3,0},{4,5},{5,6},{6,7},{7,4},{8,9},{9,10},{10,1... | collective-permute-start | bytes 1572872 | tf_op jit(solution)/shard_map/ppermute | solution.py:23
  25.5 4.9 %collective-permute-start.3 = (f32[8,128]{1,0:T(8,128)S(1)}, f32[8,128]{1,0:T(8,128)S(1)}, u32[]{:S(2)}, u32[]{:S(2)}) collective-permute-start(f32[8,128]{1,0:T(8,128)S(1)} %get-tuple-element.58), channel_id=1, source_target_pairs={{0,1},{1,0},{2,3},{3,2},{4,5},{5,4},{6,7},{7,6},{8,9},{9,8},{10,11... | collective-permute-start | bytes 12296 | tf_op jit(solution)/shard_map/ppermute | solution.py:32
  27.1 17.0 %collective-permute-start.6 = (f32[1160,128]{1,0:T(8,128)S(1)}, f32[1160,128]{1,0:T(8,128)S(1)}, u32[]{:S(2)}, u32[]{:S(2)}) collective-permute-start(f32[1160,128]{1,0:T(8,128)S(1)} %get-tuple-element.61), channel_id=1, source_target_pairs={{0,28},{4,0},{8,4},{12,8},{16,12},{20,16},{24,20},{28,24},{1,29},{... | collective-permute-start | bytes 1781768 | tf_op jit(solution)/shard_map/ppermute | solution.py:23
  30.4 13.8 %collective-permute-start.7 = (f32[1160,128]{1,0:T(8,128)S(1)}, f32[1160,128]{1,0:T(8,128)S(1)}, u32[]{:S(2)}, u32[]{:S(2)}) collective-permute-start(f32[1160,128]{1,0:T(8,128)S(1)} %get-tuple-element.62), channel_id=1, source_target_pairs={{0,3},{1,0},{2,1},{3,2},{4,7},{5,4},{6,5},{7,6},{8,11},{9,8},{10,9... | collective-permute-start | bytes 1781768 | tf_op jit(solution)/shard_map/ppermute | solution.py:23
  30.4 9.3 %collective-permute-start.4 = (f32[8,128]{1,0:T(8,128)S(1)}, f32[8,128]{1,0:T(8,128)S(1)}, u32[]{:S(2)}, u32[]{:S(2)}) collective-permute-start(f32[8,128]{1,0:T(8,128)S(1)} %add.36), channel_id=1, source_target_pairs={{0,2},{1,3},{2,0},{3,1},{4,6},{5,7},{6,4},{7,5},{8,10},{9,11},{10,... | collective-permute-start | bytes 12296 | tf_op jit(solution)/shard_map/ppermute | solution.py:32
  31.8 22.6 %collective-permute-start.2 = (f32[128,1024]{1,0:T(8,128)S(1)}, f32[128,1024]{1,0:T(8,128)S(1)}, u32[]{:S(2)}, u32[]{:S(2)}) collective-permute-start(f32[128,1024]{1,0:T(8,128)S(1)} %get-tuple-element.89), channel_id=1, source_target_pairs={{0,28},{4,0},{8,4},{12,8},{16,12},{20,16},{24,20},{28,24},{1,29},{... | collective-permute-start | bytes 1572872 | tf_op jit(solution)/shard_map/ppermute | solution.py:23
  39.7 14.7 %collective-permute-start.5 = (f32[128,1024]{1,0:T(8,128)S(1)}, f32[128,1024]{1,0:T(8,128)S(1)}, u32[]{:S(2)}, u32[]{:S(2)}) collective-permute-start(f32[128,1024]{1,0:T(8,128)S(1)} %get-tuple-element.59), channel_id=1, source_target_pairs={{0,3},{1,0},{2,1},{3,2},{4,7},{5,4},{6,5},{7,6},{8,11},{9,8},{10,9... | collective-permute-start | bytes 1572872 | tf_op jit(solution)/shard_map/ppermute | solution.py:23
  55.8 13.5 %collective-permute-start.11 = (f32[2,128,128]{2,1,0:T(8,128)S(1)}, f32[2,128,128]{2,1,0:T(8,128)S(1)}, u32[]{:S(2)}, u32[]{:S(2)}) collective-permute-start(f32[2,128,128]{2,1,0:T(8,128)S(1)} %get-tuple-element.68), channel_id=1, source_target_pairs={{0,4},{4,8},{8,12},{12,16},{16,20},{20,24},{24,28},{28,0},{1,5},{5... | collective-permute-start | bytes 393224 | tf_op jit(solution)/shard_map/ppermute | solution.py:23
  57.6 11.7 %collective-permute-start.12 = (f32[2,128,128]{2,1,0:T(8,128)S(1)}, f32[2,128,128]{2,1,0:T(8,128)S(1)}, u32[]{:S(2)}, u32[]{:S(2)}) collective-permute-start(f32[2,128,128]{2,1,0:T(8,128)S(1)} %get-tuple-element.69), channel_id=1, source_target_pairs={{0,1},{1,2},{2,3},{3,0},{4,5},{5,6},{6,7},{7,4},{8,9},{9,10},{10,1... | collective-permute-start | bytes 393224 | tf_op jit(solution)/shard_map/ppermute | solution.py:23
  57.6 4.5 %collective-permute-start.8 = (f32[8,128]{1,0:T(8,128)S(1)}, f32[8,128]{1,0:T(8,128)S(1)}, u32[]{:S(2)}, u32[]{:S(2)}) collective-permute-start(f32[8,128]{1,0:T(8,128)S(1)} %add.37), channel_id=1, source_target_pairs={{0,16},{4,20},{8,24},{12,28},{16,0},{20,4},{24,8},{28,12},{1,17},{... | collective-permute-start | bytes 12296 | tf_op jit(solution)/shard_map/ppermute | solution.py:32
  62.1 3.6 %collective-permute-start.9 = (f32[8,128]{1,0:T(8,128)S(1)}, f32[8,128]{1,0:T(8,128)S(1)}, u32[]{:S(2)}, u32[]{:S(2)}) collective-permute-start(f32[8,128]{1,0:T(8,128)S(1)} %add.38), channel_id=1, source_target_pairs={{0,8},{4,12},{8,0},{12,4},{16,24},{20,28},{24,16},{28,20},{1,9},{5... | collective-permute-start | bytes 12296 | tf_op jit(solution)/shard_map/ppermute | solution.py:32
  65.7 3.6 %collective-permute-start.10 = (f32[8,128]{1,0:T(8,128)S(1)}, f32[8,128]{1,0:T(8,128)S(1)}, u32[]{:S(2)}, u32[]{:S(2)}) collective-permute-start(f32[8,128]{1,0:T(8,128)S(1)} %add.39), channel_id=1, source_target_pairs={{0,4},{4,0},{8,12},{12,8},{16,20},{20,16},{24,28},{28,24},{1,5},{5... | collective-permute-start | bytes 12296 | tf_op jit(solution)/shard_map/ppermute | solution.py:32
  69.6 4.3 %collective-permute-start.13 = (f32[128,128]{1,0:T(8,128)S(1)}, f32[128,128]{1,0:T(8,128)S(1)}, u32[]{:S(2)}, u32[]{:S(2)}) collective-permute-start(f32[128,128]{1,0:T(8,128)S(1)} %get-tuple-element.71.first_ref), channel_id=1, source_target_pairs={{0,2},{1,3},{2,0},{3,1},{4,6},{5,7},{6,4},{7,5},{8,10},{9,11},{10,... | collective-permute-start | bytes 196616 | tf_op jit(solution)/shard_map/ppermute | solution.py:23
  73.9 6.2 %collective-permute-start.14 = (f32[2,128,128]{2,1,0:T(8,128)S(1)}, f32[2,128,128]{2,1,0:T(8,128)S(1)}, u32[]{:S(2)}, u32[]{:S(2)}) collective-permute-start(f32[2,128,128]{2,1,0:T(8,128)S(1)} %pad_maximum_fusion.refs_0_), channel_id=1, source_target_pairs={{0,4},{4,0},{8,12},{12,8},{16,20},{20,16},{24,28},{28,24},{1,5},{5... | collective-permute-start | bytes 393224 | tf_op jit(solution)/shard_map/ppermute | solution.py:69
  75.1 7.8 %collective-permute-start.15 = (f32[2,128,128]{2,1,0:T(8,128)S(1)}, f32[2,128,128]{2,1,0:T(8,128)S(1)}, u32[]{:S(2)}, u32[]{:S(2)}) collective-permute-start(f32[2,128,128]{2,1,0:T(8,128)S(1)} %pad_maximum_fusion.refs_0_), channel_id=1, source_target_pairs={{0,28},{4,8},{8,4},{12,16},{16,12},{20,24},{24,20},{28,0},{1,29},{... | collective-permute-start | bytes 393224 | tf_op jit(solution)/shard_map/ppermute | solution.py:69
  79.5 5.0 %collective-permute-start.16 = (f32[2,128,128]{2,1,0:T(8,128)S(1)}, f32[2,128,128]{2,1,0:T(8,128)S(1)}, u32[]{:S(2)}, u32[]{:S(2)}) collective-permute-start(f32[2,128,128]{2,1,0:T(8,128)S(1)} %pad_maximum_fusion.refs_0_), channel_id=1, source_target_pairs={{0,8},{4,12},{8,0},{12,4},{16,24},{20,28},{24,16},{28,20},{1,9},{5... | collective-permute-start | bytes 393224 | tf_op jit(solution)/shard_map/ppermute | solution.py:69
  79.5 6.9 %collective-permute-start.17 = (f32[2,128,128]{2,1,0:T(8,128)S(1)}, f32[2,128,128]{2,1,0:T(8,128)S(1)}, u32[]{:S(2)}, u32[]{:S(2)}) collective-permute-start(f32[2,128,128]{2,1,0:T(8,128)S(1)} %pad_maximum_fusion.refs_0_), channel_id=1, source_target_pairs={{0,24},{4,28},{8,16},{12,20},{16,8},{20,12},{24,0},{28,4},{1,25},{... | collective-permute-start | bytes 393224 | tf_op jit(solution)/shard_map/ppermute | solution.py:69
  86.4 4.0 %collective-permute-start.18 = (f32[10,128,128]{2,1,0:T(8,128)S(1)}, f32[10,128,128]{2,1,0:T(8,128)S(1)}, u32[]{:S(2)}, u32[]{:S(2)}) collective-permute-start(f32[10,128,128]{2,1,0:T(8,128)S(1)} %shard_map.173.window_ref), channel_id=1, source_target_pairs={{0,1},{1,0},{2,3},{3,2},{4,5},{5,4},{6,7},{7,6},{8,9},{9,8},{10,11... | collective-permute-start | bytes 1966088 | tf_op jit(solution)/shard_map/ppermute | solution.py:675
  93.4 3.6 %collective-permute-start.20 = (f32[8,128]{1,0:T(8,128)S(1)}, f32[8,128]{1,0:T(8,128)S(1)}, u32[]{:S(2)}, u32[]{:S(2)}) collective-permute-start(f32[8,128]{1,0:T(8,128)S(1)} %add.41), channel_id=1, source_target_pairs={{0,2},{1,3},{2,0},{3,1},{4,6},{5,7},{6,4},{7,5},{8,10},{9,11},{10,... | collective-permute-start | bytes 12296 | tf_op jit(solution)/shard_map/ppermute | solution.py:32
  97.0 8.7 %collective-permute-start.23 = (f32[128,128]{1,0:T(8,128)S(1)}, f32[128,128]{1,0:T(8,128)S(1)}, u32[]{:S(2)}, u32[]{:S(2)}) collective-permute-start(f32[128,128]{1,0:T(8,128)S(1)} %get-tuple-element.78.own_ref), channel_id=1, source_target_pairs={{0,28},{4,0},{8,4},{12,8},{16,12},{20,16},{24,20},{28,24},{1,29},{... | collective-permute-start | bytes 196616 | tf_op jit(solution)/shard_map/ppermute | solution.py:23
  98.5 7.2 %collective-permute-start.24 = (f32[128,128]{1,0:T(8,128)S(1)}, f32[128,128]{1,0:T(8,128)S(1)}, u32[]{:S(2)}, u32[]{:S(2)}) collective-permute-start(f32[128,128]{1,0:T(8,128)S(1)} %get-tuple-element.78.own_ref), channel_id=1, source_target_pairs={{0,3},{1,0},{2,1},{3,2},{4,7},{5,4},{6,5},{7,6},{8,11},{9,8},{10,9... | collective-permute-start | bytes 196616 | tf_op jit(solution)/shard_map/ppermute | solution.py:23
  98.5 3.6 %collective-permute-start.21 = (f32[8,128]{1,0:T(8,128)S(1)}, f32[8,128]{1,0:T(8,128)S(1)}, u32[]{:S(2)}, u32[]{:S(2)}) collective-permute-start(f32[8,128]{1,0:T(8,128)S(1)} %add.42), channel_id=1, source_target_pairs={{0,4},{4,0},{8,12},{12,8},{16,20},{20,16},{24,28},{28,24},{1,5},{5... | collective-permute-start | bytes 12296 | tf_op jit(solution)/shard_map/ppermute | solution.py:46
  105.7 4.6 %collective-permute-start.25 = (f32[8,128]{1,0:T(8,128)S(1)}, f32[8,128]{1,0:T(8,128)S(1)}, u32[]{:S(2)}, u32[]{:S(2)}) collective-permute-start(f32[8,128]{1,0:T(8,128)S(1)} %add.44), channel_id=1, source_target_pairs={{0,16},{4,20},{8,24},{12,28},{16,0},{20,4},{24,8},{28,12},{1,17},{... | collective-permute-start | bytes 12296 | tf_op jit(solution)/shard_map/ppermute | solution.py:46
  (5 other events, 95.7 us)

commit v5 on v4

--- a/solution.py
+++ b/solution.py
@@ -128,6 +128,7 @@
 
 
 BATCH = 16
+LAST_BATCH = 32
 
 
 def in_hbm(value):
@@ -240,11 +241,11 @@
         low_ref[pair, row, :, cols] = low
 
     def outer(i, carry):
-        per = blocks // BATCH
+        per = blocks // LAST_BATCH
         q = i // per
-        base = (i - q * per) * BATCH
-        for k in range(BATCH):
-            full = mm(middle_ref[i * BATCH + k], twice(couple_ref[i * BATCH + k], 1), NT)
+        base = (i - q * per) * LAST_BATCH
+        for k in range(LAST_BATCH):
+            full = mm(middle_ref[i * LAST_BATCH + k], twice(couple_ref[i * LAST_BATCH + k], 1), NT)
             place = base + k
             reached = place + q + 1
             near_ref[place] += full[:width, :width]
@@ -256,7 +257,7 @@
             put(place // 2, reach + q + 1 + side, side, full[width:, :width])
         return carry
 
-    lax.fori_loop(0, count // BATCH, outer, 0)
+    lax.fori_loop(0, count // LAST_BATCH, outer, 0)
 
     def close(pair, carry):
         zero = jnp.zeros((width, width), BF16)
@@ -319,7 +320,8 @@
             ref[blocks + reach + i] = ref[reach + i]
     half_face = per_face // 2
 
-    def one_face(which, carry):
+    acc = jnp.zeros((loads, width), F32)
+    for which, (ref, base) in enumerate(faces):
         slot = slots_ref[0, which]
         for part in range(half_face):
             pair = slot * half_face + part
@@ -328,14 +330,10 @@
             weight = high_ref[pair].reshape(count * width, 2 * width)
             both = mm(jnp.concatenate([high, low], 0), weight)
             result = both[:loads] + both[loads:] + mm(high, low_ref[pair].reshape(count * width, 2 * width))
-            out_ref[which, :, part * 2 * width : (part + 1) * 2 * width] = result
-        return carry
-
-    lax.fori_loop(0, 4, one_face, 0)
-    acc = jnp.zeros((loads, width), F32)
-    for which, (ref, base) in enumerate(faces):
-        for b in range(per_face):
-            acc += ref[:, base + b * width : base + (b + 1) * width] * out_ref[which, :, b * width : (b + 1) * width]
+            first = 2 * part * width
+            out_ref[which, :, first : first + 2 * width] = result
+            acc += ref[:, base + first : base + first + width] * result[:, :width]
+            acc += ref[:, base + first + width : base + first + 2 * width] * result[:, width:]
     curve_ref[...] = row_sums(acc)
 
 
@@ -613,6 +611,27 @@
     )(slots, solved, own, from_sub, from_grp, blocks, basis, aux_sub, aux_grp, iterate, direction, curve, product)
 
 
+def finish_body(made_ref, direction_ref, sum_ref, product_ref, direction_out, sum_out):
+    width = sum_ref.shape[1]
+    scale = per_row(sum_ref[...] / product_ref[...], width)
+    sum_out[...] = sum_ref[0:1]
+    for b in range(made_ref.shape[1] // width):
+        cols = slice(b * width, (b + 1) * width)
+        direction_out[:, cols] = made_ref[:, cols] + scale * direction_ref[:, cols]
+
+
+def finish(made, direction, total_sum, product):
+    return call(
+        finish_body,
+        (jax.ShapeDtypeStruct(made.shape, F32), jax.ShapeDtypeStruct(product.shape, F32)),
+        flops=made.size * 2,
+        moved=made.size * 12,
+        in_specs=[VMEM] * 4,
+        out_specs=(VMEM, VMEM),
+        limit=4 * 1024 * 1024,
+    )(made, direction, total_sum, product)
+
+
 def shards(
     solution,
     residual,
@@ -687,10 +706,8 @@
         )
 
     new_product, (preconditioned, new_solution) = total_with(partial, "sub", late)
-    new_product = new_product[0]
-    step_ratio = new_product / residual_product
-    new_direction = preconditioned[None] + step_ratio[None, :, None] * own[None]
-    return (new_solution[None], fresh[None], new_direction, new_product)
+    new_direction, new_product = finish(preconditioned, own, new_product, product)
+    return (new_solution[None], fresh[None], new_direction[None], new_product[0])
 
 
 def solution(mesh):

time: 112 us -> 110 us (0.982)
  other arithmetic: 1.7 us -> 0.04 us
    pallas_call x0 -> x1, Pallas kernels: none -> 1.19 us  [finish(): call(finish_body, (jax.ShapeDtypeStruct(made.shape, F32), jax.ShapeDtypeS...]
    add x1 -> x0, other arithmetic: 1.14 us -> none  [shards(): new_direction = preconditioned[None] + step_ratio[None, :, None] * own[None]]
  transfers between devices with their start and end apart: 26 -> 26, of which waited for: 15 -> 16; matrix products, arithmetic and copies ran while one was open for 0% -> 0% of each run, Pallas kernels for 19% -> 19%
where the time goes in v5:
time: 110 us
  waiting for transfers between devices  49.7 us (45%)
  Pallas kernels  29.6 us (27%)
  starting transfers between devices  28.6 us (26%)
  local copies, waits for them, and re-layouts  1.41 us (1%)
    ppermute x11, waiting for transfers between devices, shifted(): return lax.ppermute(value, axis, pairs)  19.2 us
    ppermute x7, waiting for transfers between devices, total(): lax.ppermute(value, axis, [(i, i ^ bit) for i in range(count)])  16.4 us
    ppermute x11, starting transfers between devices, shifted(): return lax.ppermute(value, axis, pairs)  12 us
    ppermute x7, starting transfers between devices, total(): lax.ppermute(value, axis, [(i, i ^ bit) for i in range(count)])  8.64 us
    pallas_call x1, Pallas kernels, prepare(): call(functools.partial(prepare_body, len(keep)), (jax.ShapeDtypeStruct(co...  7.84 us
    ppermute x3, waiting for transfers between devices, total_with(): lax.ppermute(value, axis, [(i, i ^ bit) for i in range(count)])  7.8 us
    ppermute x4, waiting for transfers between devices, sub_window(): pieces.append(lax.ppermute(group, 'sub', list(zip(everyone, target))))  6.3 us
    ppermute x4, starting transfers between devices, sub_window(): pieces.append(lax.ppermute(group, 'sub', list(zip(everyone, target))))  6.15 us
  transfers between devices with their start and end apart: 26, of which 16 were waited for; matrix products, arithmetic and copies ran while one was open for 0% of the time, Pallas kernels for 19%

profile of v5, /device:TPU:0, one launch (start us, length us, event | category | flops | bytes accessed | tf_op | source)
XLA Modules:
  0.0 110.1 jit_solution(1815296030988776900)
XLA Ops:
  2.0 3.0 %collective-permute-start = (f32[128,1024]{1,0:T(8,128)S(1)}, f32[128,1024]{1,0:T(8,128)S(1)}, u32[]{:S(2)}, u32[]{:S(2)}) collective-permute-start(f32[128,1024]{1,0:T(8,128)S(1)} %get-tuple-element.93), channel_id=1, source_target_pairs={{0,4},{4,8},{8,12},{12,16},{16,20},{20,24},{24,28},{28,0},{1,5},{5... | collective-permute-start | bytes 1572872 | tf_op jit(solution)/shard_map/ppermute | solution.py:23
  5.0 7.8 %shard_map.165 = (bf16[96,256,128]{2,1,0:T(8,128)(2,1)S(1)}, bf16[96,256,256]{2,1,0:T(8,128)(2,1)S(1)}, bf16[32,128,128]{2,1,0:T(8,128)(2,1)S(1)}, bf16[32,128,1...) custom-call(bf16[96,256,128]{2,1,0:T(8,128)(2,1)} %bitcast.26, ...), custom_call_target="tpu_custom_call" | custom-call | flops 2415919104 | bytes 9437184 | tf_op jit(solution)/shard_map/pallas_call | solution.py:194
  13.5 5.8 %shard_map.167 = (bf16[16,8,128,256]{3,2,1,0:T(8,128)(2,1)S(1)}, bf16[16,8,128,256]{3,2,1,0:T(8,128)(2,1)S(1)}, f32[128,2048]{1,0:T(8,128)S(1)}, f32[128,2048]{1...) custom-call(bf16[96,256,128]{2,1,0:T(8,128)(2,1)S(1)} %get-tuple-element.47.couple_ref,, ...), custom_call_target="tpu_custom_call" | custom-call | flops 2415919104 | bytes 9437184 | tf_op jit(solution)/shard_map/pallas_call | solution.py:285
  19.9 4.8 %shard_map.168 = (f32[4,128,1024]{2,1,0:T(8,128)S(1)}, f32[8,128]{1,0:T(8,128)S(1)}) custom-call(s32[1,4]{1,0:T(1,128)S(1)} %copy-done, f32[128,2048]{1,0:T(8,128)S(1)} %get-tuple-element.56.own_ref.direction_ref, f32[128,1024]{1,0:T(8,128)S(1)} %collective-permute-done.from_sub_ref, f32[128,1024]{1,0:T(8,128)S(1)} %collective-permute-done.1.from_grp_ref, ...), custom_call_target="tpu_custom_call" | custom-call | flops 3221225472 | bytes 16777216 | tf_op jit(solution)/shard_map/pallas_call | solution.py:343
  25.7 3.2 %collective-permute-start.6 = (f32[1160,128]{1,0:T(8,128)S(1)}, f32[1160,128]{1,0:T(8,128)S(1)}, u32[]{:S(2)}, u32[]{:S(2)}) collective-permute-start(f32[1160,128]{1,0:T(8,128)S(1)} %get-tuple-element.63), channel_id=1, source_target_pairs={{0,28},{4,0},{8,4},{12,8},{16,12},{20,16},{24,20},{28,24},{1,29},{... | collective-permute-start | bytes 1781768 | tf_op jit(solution)/shard_map/ppermute | solution.py:23
  30.4 1.9 %collective-permute-start.2 = (f32[128,1024]{1,0:T(8,128)S(1)}, f32[128,1024]{1,0:T(8,128)S(1)}, u32[]{:S(2)}, u32[]{:S(2)}) collective-permute-start(f32[128,1024]{1,0:T(8,128)S(1)} %get-tuple-element.91), channel_id=1, source_target_pairs={{0,28},{4,0},{8,4},{12,8},{16,12},{20,16},{24,20},{28,24},{1,29},{... | collective-permute-start | bytes 1572872 | tf_op jit(solution)/shard_map/ppermute | solution.py:23
  32.3 6.0 %collective-permute-done.4 = f32[8,128]{1,0:T(8,128)S(1)} collective-permute-done((f32[8,128]{1,0:T(8,128)S(1)}, f32[8,128]{1,0:T(8,128)S(1)}, u32[]{:S(2)}, u32[]{:S(2)}) %collective-permute-start.4) | collective-permute-done | bytes 4128 | tf_op jit(solution)/shard_map/ppermute | solution.py:32
  38.3 4.4 %collective-permute-done.6.aux_sub_ref = f32[1160,128]{1,0:T(8,128)S(1)} collective-permute-done((f32[1160,128]{1,0:T(8,128)S(1)}, f32[1160,128]{1,0:T(8,128)S(1)}, u32[]{:S(2)}, u32[]{:S(2)}) %collective-permute-start.6) | collective-permute-done | bytes 593952 | tf_op jit(solution)/shard_map/ppermute | solution.py:23
  42.7 10.3 %collective-permute-done.2.back_sub_ref = f32[128,1024]{1,0:T(8,128)S(1)} collective-permute-done((f32[128,1024]{1,0:T(8,128)S(1)}, f32[128,1024]{1,0:T(8,128)S(1)}, u32[]{:S(2)}, u32[]{:S(2)}) %collective-permute-start.2) | collective-permute-done | bytes 524320 | tf_op jit(solution)/shard_map/ppermute | solution.py:23
  54.4 1.7 %collective-permute-start.11 = (f32[2,128,128]{2,1,0:T(8,128)S(1)}, f32[2,128,128]{2,1,0:T(8,128)S(1)}, u32[]{:S(2)}, u32[]{:S(2)}) collective-permute-start(f32[2,128,128]{2,1,0:T(8,128)S(1)} %get-tuple-element.70), channel_id=1, source_target_pairs={{0,4},{4,8},{8,12},{12,16},{16,20},{20,24},{24,28},{28,0},{1,5},{5... | collective-permute-start | bytes 393224 | tf_op jit(solution)/shard_map/ppermute | solution.py:23
  56.2 2.6 %collective-permute-start.8 = (f32[8,128]{1,0:T(8,128)S(1)}, f32[8,128]{1,0:T(8,128)S(1)}, u32[]{:S(2)}, u32[]{:S(2)}) collective-permute-start(f32[8,128]{1,0:T(8,128)S(1)} %add.31), channel_id=1, source_target_pairs={{0,16},{4,20},{8,24},{12,28},{16,0},{20,4},{24,8},{28,12},{1,17},{... | collective-permute-start | bytes 12296 | tf_op jit(solution)/shard_map/ppermute | solution.py:32
  58.7 1.9 %collective-permute-done.8 = f32[8,128]{1,0:T(8,128)S(1)} collective-permute-done((f32[8,128]{1,0:T(8,128)S(1)}, f32[8,128]{1,0:T(8,128)S(1)}, u32[]{:S(2)}, u32[]{:S(2)}) %collective-permute-start.8) | collective-permute-done | bytes 4128 | tf_op jit(solution)/shard_map/ppermute | solution.py:32
  62.4 1.9 %collective-permute-done.9 = f32[8,128]{1,0:T(8,128)S(1)} collective-permute-done((f32[8,128]{1,0:T(8,128)S(1)}, f32[8,128]{1,0:T(8,128)S(1)}, u32[]{:S(2)}, u32[]{:S(2)}) %collective-permute-start.9) | collective-permute-done | bytes 4128 | tf_op jit(solution)/shard_map/ppermute | solution.py:32
  65.4 2.5 %collective-permute-done.10 = f32[8,128]{1,0:T(8,128)S(1)} collective-permute-done((f32[8,128]{1,0:T(8,128)S(1)}, f32[8,128]{1,0:T(8,128)S(1)}, u32[]{:S(2)}, u32[]{:S(2)}) %collective-permute-start.10) | collective-permute-done | bytes 4128 | tf_op jit(solution)/shard_map/ppermute | solution.py:32
  68.7 3.7 %collective-permute-done.13 = f32[128,128]{1,0:T(8,128)S(1)} collective-permute-done((f32[128,128]{1,0:T(8,128)S(1)}, f32[128,128]{1,0:T(8,128)S(1)}, u32[]{:S(2)}, u32[]{:S(2)}) %collective-permute-start.13) | collective-permute-done | bytes 65568 | tf_op jit(solution)/shard_map/ppermute | solution.py:23
  73.7 4.4 %collective-permute-start.15 = (f32[2,128,128]{2,1,0:T(8,128)S(1)}, f32[2,128,128]{2,1,0:T(8,128)S(1)}, u32[]{:S(2)}, u32[]{:S(2)}) collective-permute-start(f32[2,128,128]{2,1,0:T(8,128)S(1)} %pad_maximum_fusion.refs_0_), channel_id=1, source_target_pairs={{0,28},{4,8},{8,4},{12,16},{16,12},{20,24},{24,20},{28,0},{1,29},{... | collective-permute-start | bytes 393224 | tf_op jit(solution)/shard_map/ppermute | solution.py:69
  78.7 2.8 %collective-permute-done.15.refs_2_ = f32[2,128,128]{2,1,0:T(8,128)S(1)} collective-permute-done((f32[2,128,128]{2,1,0:T(8,128)S(1)}, f32[2,128,128]{2,1,0:T(8,128)S(1)}, u32[]{:S(2)}, u32[]{:S(2)}) %collective-permute-start.15) | collective-permute-done | bytes 131104 | tf_op jit(solution)/shard_map/ppermute | solution.py:69
  83.1 1.9 %collective-permute-done.17.refs_4_ = f32[2,128,128]{2,1,0:T(8,128)S(1)} collective-permute-done((f32[2,128,128]{2,1,0:T(8,128)S(1)}, f32[2,128,128]{2,1,0:T(8,128)S(1)}, u32[]{:S(2)}, u32[]{:S(2)}) %collective-permute-start.17) | collective-permute-done | bytes 131104 | tf_op jit(solution)/shard_map/ppermute | solution.py:69
  86.3 2.8 %shard_map.171 = (f32[128,2048]{1,0:T(8,128)S(1)}, f32[8,128]{1,0:T(8,128)S(1)}) custom-call(s32[1,4]{1,0:T(1,128)S(1)} %copy-done, f32[128,2048]{1,0:T(8,128)S(1)} %get-tuple-element.67.halved_ref, bf16[32,128,128]{2,1,0:T(8,128)(2,1)S(1)} %get-tuple-element.51.factor_ref, f32[1160,128]{1,0:T(8,128)S(1)} %collective-permute-done.6.aux_sub_ref, ...), custom_call_target="tpu_custom_call" | custom-call | flops 536870912 | bytes 3145728 | tf_op jit(solution)/shard_map/pallas_call | solution.py:569
  92.3 3.2 %collective-permute-done.20 = f32[8,128]{1,0:T(8,128)S(1)} collective-permute-done((f32[8,128]{1,0:T(8,128)S(1)}, f32[8,128]{1,0:T(8,128)S(1)}, u32[]{:S(2)}, u32[]{:S(2)}) %collective-permute-start.20) | collective-permute-done | bytes 4128 | tf_op jit(solution)/shard_map/ppermute | solution.py:32
  97.6 3.1 %collective-permute-done.21 = f32[8,128]{1,0:T(8,128)S(1)} collective-permute-done((f32[8,128]{1,0:T(8,128)S(1)}, f32[8,128]{1,0:T(8,128)S(1)}, u32[]{:S(2)}, u32[]{:S(2)}) %collective-permute-start.21) | collective-permute-done | bytes 4128 | tf_op jit(solution)/shard_map/ppermute | solution.py:46
  101.4 2.9 %collective-permute-done.22 = f32[8,128]{1,0:T(8,128)S(1)} collective-permute-done((f32[8,128]{1,0:T(8,128)S(1)}, f32[8,128]{1,0:T(8,128)S(1)}, u32[]{:S(2)}, u32[]{:S(2)}) %collective-permute-start.22) | collective-permute-done | bytes 4128 | tf_op jit(solution)/shard_map/ppermute | solution.py:46
  104.8 2.3 %shard_map.175 = (f32[128,2048]{1,0:T(8,128)S(1)}, f32[128,2048]{1,0:T(8,128)}) custom-call(s32[1,4]{1,0:T(1,128)S(1)} %copy-done, f32[128,2048]{1,0:T(8,128)S(1)} %get-tuple-element.68.solved_ref, f32[128,128]{1,0:T(8,128)S(1)} %get-tuple-element.80.own_ref, f32[128,128]{1,0:T(8,128)S(1)} %collective-permute-done.23.from_sub_ref, ...), custom_call_target="tpu_custom_call" | custom-call | flops 268435456 | bytes 3145728 | tf_op jit(solution)/shard_map/pallas_call | solution.py:603
  107.1 1.8 %collective-permute-done.25 = f32[8,128]{1,0:T(8,128)S(1)} collective-permute-done((f32[8,128]{1,0:T(8,128)S(1)}, f32[8,128]{1,0:T(8,128)S(1)}, u32[]{:S(2)}, u32[]{:S(2)}) %collective-permute-start.25) | collective-permute-done | bytes 4128 | tf_op jit(solution)/shard_map/ppermute | solution.py:46
  (59 shorter events, 22.6 us)
Async XLA Ops:
  2.0 18.0 %collective-permute-start = (f32[128,1024]{1,0:T(8,128)S(1)}, f32[128,1024]{1,0:T(8,128)S(1)}, u32[]{:S(2)}, u32[]{:S(2)}) collective-permute-start(f32[128,1024]{1,0:T(8,128)S(1)} %get-tuple-element.93), channel_id=1, source_target_pairs={{0,4},{4,8},{8,12},{12,16},{16,20},{20,24},{24,28},{28,0},{1,5},{5... | collective-permute-start | bytes 1572872 | tf_op jit(solution)/shard_map/ppermute | solution.py:23
  5.0 15.0 %collective-permute-start.1 = (f32[128,1024]{1,0:T(8,128)S(1)}, f32[128,1024]{1,0:T(8,128)S(1)}, u32[]{:S(2)}, u32[]{:S(2)}) collective-permute-start(f32[128,1024]{1,0:T(8,128)S(1)} %get-tuple-element.92), channel_id=1, source_target_pairs={{0,1},{1,2},{2,3},{3,0},{4,5},{5,6},{6,7},{7,4},{8,9},{9,10},{10,1... | collective-permute-start | bytes 1572872 | tf_op jit(solution)/shard_map/ppermute | solution.py:23
  24.7 4.2 %collective-permute-start.3 = (f32[8,128]{1,0:T(8,128)S(1)}, f32[8,128]{1,0:T(8,128)S(1)}, u32[]{:S(2)}, u32[]{:S(2)}) collective-permute-start(f32[8,128]{1,0:T(8,128)S(1)} %get-tuple-element.60), channel_id=1, source_target_pairs={{0,1},{1,0},{2,3},{3,2},{4,5},{5,4},{6,7},{7,6},{8,9},{9,8},{10,11... | collective-permute-start | bytes 12296 | tf_op jit(solution)/shard_map/ppermute | solution.py:32
  25.7 17.0 %collective-permute-start.6 = (f32[1160,128]{1,0:T(8,128)S(1)}, f32[1160,128]{1,0:T(8,128)S(1)}, u32[]{:S(2)}, u32[]{:S(2)}) collective-permute-start(f32[1160,128]{1,0:T(8,128)S(1)} %get-tuple-element.63), channel_id=1, source_target_pairs={{0,28},{4,0},{8,4},{12,8},{16,12},{20,16},{24,20},{28,24},{1,29},{... | collective-permute-start | bytes 1781768 | tf_op jit(solution)/shard_map/ppermute | solution.py:23
  28.9 13.8 %collective-permute-start.7 = (f32[1160,128]{1,0:T(8,128)S(1)}, f32[1160,128]{1,0:T(8,128)S(1)}, u32[]{:S(2)}, u32[]{:S(2)}) collective-permute-start(f32[1160,128]{1,0:T(8,128)S(1)} %get-tuple-element.64), channel_id=1, source_target_pairs={{0,3},{1,0},{2,1},{3,2},{4,7},{5,4},{6,5},{7,6},{8,11},{9,8},{10,9... | collective-permute-start | bytes 1781768 | tf_op jit(solution)/shard_map/ppermute | solution.py:23
  29.0 9.3 %collective-permute-start.4 = (f32[8,128]{1,0:T(8,128)S(1)}, f32[8,128]{1,0:T(8,128)S(1)}, u32[]{:S(2)}, u32[]{:S(2)}) collective-permute-start(f32[8,128]{1,0:T(8,128)S(1)} %add.30), channel_id=1, source_target_pairs={{0,2},{1,3},{2,0},{3,1},{4,6},{5,7},{6,4},{7,5},{8,10},{9,11},{10,... | collective-permute-start | bytes 12296 | tf_op jit(solution)/shard_map/ppermute | solution.py:32
  30.4 22.6 %collective-permute-start.2 = (f32[128,1024]{1,0:T(8,128)S(1)}, f32[128,1024]{1,0:T(8,128)S(1)}, u32[]{:S(2)}, u32[]{:S(2)}) collective-permute-start(f32[128,1024]{1,0:T(8,128)S(1)} %get-tuple-element.91), channel_id=1, source_target_pairs={{0,28},{4,0},{8,4},{12,8},{16,12},{20,16},{24,20},{28,24},{1,29},{... | collective-permute-start | bytes 1572872 | tf_op jit(solution)/shard_map/ppermute | solution.py:23
  38.3 14.7 %collective-permute-start.5 = (f32[128,1024]{1,0:T(8,128)S(1)}, f32[128,1024]{1,0:T(8,128)S(1)}, u32[]{:S(2)}, u32[]{:S(2)}) collective-permute-start(f32[128,1024]{1,0:T(8,128)S(1)} %get-tuple-element.61), channel_id=1, source_target_pairs={{0,3},{1,0},{2,1},{3,2},{4,7},{5,4},{6,5},{7,6},{8,11},{9,8},{10,9... | collective-permute-start | bytes 1572872 | tf_op jit(solution)/shard_map/ppermute | solution.py:23
  54.4 13.5 %collective-permute-start.11 = (f32[2,128,128]{2,1,0:T(8,128)S(1)}, f32[2,128,128]{2,1,0:T(8,128)S(1)}, u32[]{:S(2)}, u32[]{:S(2)}) collective-permute-start(f32[2,128,128]{2,1,0:T(8,128)S(1)} %get-tuple-element.70), channel_id=1, source_target_pairs={{0,4},{4,8},{8,12},{12,16},{16,20},{20,24},{24,28},{28,0},{1,5},{5... | collective-permute-start | bytes 393224 | tf_op jit(solution)/shard_map/ppermute | solution.py:23
  56.2 11.7 %collective-permute-start.12 = (f32[2,128,128]{2,1,0:T(8,128)S(1)}, f32[2,128,128]{2,1,0:T(8,128)S(1)}, u32[]{:S(2)}, u32[]{:S(2)}) collective-permute-start(f32[2,128,128]{2,1,0:T(8,128)S(1)} %get-tuple-element.71), channel_id=1, source_target_pairs={{0,1},{1,2},{2,3},{3,0},{4,5},{5,6},{6,7},{7,4},{8,9},{9,10},{10,1... | collective-permute-start | bytes 393224 | tf_op jit(solution)/shard_map/ppermute | solution.py:23
  56.2 4.5 %collective-permute-start.8 = (f32[8,128]{1,0:T(8,128)S(1)}, f32[8,128]{1,0:T(8,128)S(1)}, u32[]{:S(2)}, u32[]{:S(2)}) collective-permute-start(f32[8,128]{1,0:T(8,128)S(1)} %add.31), channel_id=1, source_target_pairs={{0,16},{4,20},{8,24},{12,28},{16,0},{20,4},{24,8},{28,12},{1,17},{... | collective-permute-start | bytes 12296 | tf_op jit(solution)/shard_map/ppermute | solution.py:32
  60.7 3.6 %collective-permute-start.9 = (f32[8,128]{1,0:T(8,128)S(1)}, f32[8,128]{1,0:T(8,128)S(1)}, u32[]{:S(2)}, u32[]{:S(2)}) collective-permute-start(f32[8,128]{1,0:T(8,128)S(1)} %add.32), channel_id=1, source_target_pairs={{0,8},{4,12},{8,0},{12,4},{16,24},{20,28},{24,16},{28,20},{1,9},{5... | collective-permute-start | bytes 12296 | tf_op jit(solution)/shard_map/ppermute | solution.py:32
  64.3 3.6 %collective-permute-start.10 = (f32[8,128]{1,0:T(8,128)S(1)}, f32[8,128]{1,0:T(8,128)S(1)}, u32[]{:S(2)}, u32[]{:S(2)}) collective-permute-start(f32[8,128]{1,0:T(8,128)S(1)} %add.33), channel_id=1, source_target_pairs={{0,4},{4,0},{8,12},{12,8},{16,20},{20,16},{24,28},{28,24},{1,5},{5... | collective-permute-start | bytes 12296 | tf_op jit(solution)/shard_map/ppermute | solution.py:32
  68.2 4.3 %collective-permute-start.13 = (f32[128,128]{1,0:T(8,128)S(1)}, f32[128,128]{1,0:T(8,128)S(1)}, u32[]{:S(2)}, u32[]{:S(2)}) collective-permute-start(f32[128,128]{1,0:T(8,128)S(1)} %get-tuple-element.73.first_ref), channel_id=1, source_target_pairs={{0,2},{1,3},{2,0},{3,1},{4,6},{5,7},{6,4},{7,5},{8,10},{9,11},{10,... | collective-permute-start | bytes 196616 | tf_op jit(solution)/shard_map/ppermute | solution.py:23
  72.5 6.2 %collective-permute-start.14 = (f32[2,128,128]{2,1,0:T(8,128)S(1)}, f32[2,128,128]{2,1,0:T(8,128)S(1)}, u32[]{:S(2)}, u32[]{:S(2)}) collective-permute-start(f32[2,128,128]{2,1,0:T(8,128)S(1)} %pad_maximum_fusion.refs_0_), channel_id=1, source_target_pairs={{0,4},{4,0},{8,12},{12,8},{16,20},{20,16},{24,28},{28,24},{1,5},{5... | collective-permute-start | bytes 393224 | tf_op jit(solution)/shard_map/ppermute | solution.py:69
  73.7 7.8 %collective-permute-start.15 = (f32[2,128,128]{2,1,0:T(8,128)S(1)}, f32[2,128,128]{2,1,0:T(8,128)S(1)}, u32[]{:S(2)}, u32[]{:S(2)}) collective-permute-start(f32[2,128,128]{2,1,0:T(8,128)S(1)} %pad_maximum_fusion.refs_0_), channel_id=1, source_target_pairs={{0,28},{4,8},{8,4},{12,16},{16,12},{20,24},{24,20},{28,0},{1,29},{... | collective-permute-start | bytes 393224 | tf_op jit(solution)/shard_map/ppermute | solution.py:69
  78.1 5.0 %collective-permute-start.16 = (f32[2,128,128]{2,1,0:T(8,128)S(1)}, f32[2,128,128]{2,1,0:T(8,128)S(1)}, u32[]{:S(2)}, u32[]{:S(2)}) collective-permute-start(f32[2,128,128]{2,1,0:T(8,128)S(1)} %pad_maximum_fusion.refs_0_), channel_id=1, source_target_pairs={{0,8},{4,12},{8,0},{12,4},{16,24},{20,28},{24,16},{28,20},{1,9},{5... | collective-permute-start | bytes 393224 | tf_op jit(solution)/shard_map/ppermute | solution.py:69
  78.1 6.9 %collective-permute-start.17 = (f32[2,128,128]{2,1,0:T(8,128)S(1)}, f32[2,128,128]{2,1,0:T(8,128)S(1)}, u32[]{:S(2)}, u32[]{:S(2)}) collective-permute-start(f32[2,128,128]{2,1,0:T(8,128)S(1)} %pad_maximum_fusion.refs_0_), channel_id=1, source_target_pairs={{0,24},{4,28},{8,16},{12,20},{16,8},{20,12},{24,0},{28,4},{1,25},{... | collective-permute-start | bytes 393224 | tf_op jit(solution)/shard_map/ppermute | solution.py:69
  85.0 4.0 %collective-permute-start.18 = (f32[10,128,128]{2,1,0:T(8,128)S(1)}, f32[10,128,128]{2,1,0:T(8,128)S(1)}, u32[]{:S(2)}, u32[]{:S(2)}) collective-permute-start(f32[10,128,128]{2,1,0:T(8,128)S(1)} %shard_map.173.window_ref), channel_id=1, source_target_pairs={{0,1},{1,0},{2,3},{3,2},{4,5},{5,4},{6,7},{7,6},{8,9},{9,8},{10,11... | collective-permute-start | bytes 1966088 | tf_op jit(solution)/shard_map/ppermute | solution.py:694
  92.0 3.6 %collective-permute-start.20 = (f32[8,128]{1,0:T(8,128)S(1)}, f32[8,128]{1,0:T(8,128)S(1)}, u32[]{:S(2)}, u32[]{:S(2)}) collective-permute-start(f32[8,128]{1,0:T(8,128)S(1)} %add.35), channel_id=1, source_target_pairs={{0,2},{1,3},{2,0},{3,1},{4,6},{5,7},{6,4},{7,5},{8,10},{9,11},{10,... | collective-permute-start | bytes 12296 | tf_op jit(solution)/shard_map/ppermute | solution.py:32
  95.6 8.8 %collective-permute-start.23 = (f32[128,128]{1,0:T(8,128)S(1)}, f32[128,128]{1,0:T(8,128)S(1)}, u32[]{:S(2)}, u32[]{:S(2)}) collective-permute-start(f32[128,128]{1,0:T(8,128)S(1)} %get-tuple-element.80.own_ref), channel_id=1, source_target_pairs={{0,28},{4,0},{8,4},{12,8},{16,12},{20,16},{24,20},{28,24},{1,29},{... | collective-permute-start | bytes 196616 | tf_op jit(solution)/shard_map/ppermute | solution.py:23
  97.1 7.2 %collective-permute-start.24 = (f32[128,128]{1,0:T(8,128)S(1)}, f32[128,128]{1,0:T(8,128)S(1)}, u32[]{:S(2)}, u32[]{:S(2)}) collective-permute-start(f32[128,128]{1,0:T(8,128)S(1)} %get-tuple-element.80.own_ref), channel_id=1, source_target_pairs={{0,3},{1,0},{2,1},{3,2},{4,7},{5,4},{6,5},{7,6},{8,11},{9,8},{10,9... | collective-permute-start | bytes 196616 | tf_op jit(solution)/shard_map/ppermute | solution.py:23
  97.1 3.6 %collective-permute-start.21 = (f32[8,128]{1,0:T(8,128)S(1)}, f32[8,128]{1,0:T(8,128)S(1)}, u32[]{:S(2)}, u32[]{:S(2)}) collective-permute-start(f32[8,128]{1,0:T(8,128)S(1)} %add.36), channel_id=1, source_target_pairs={{0,4},{4,0},{8,12},{12,8},{16,20},{20,16},{24,28},{28,24},{1,5},{5... | collective-permute-start | bytes 12296 | tf_op jit(solution)/shard_map/ppermute | solution.py:46
  104.3 4.6 %collective-permute-start.25 = (f32[8,128]{1,0:T(8,128)S(1)}, f32[8,128]{1,0:T(8,128)S(1)}, u32[]{:S(2)}, u32[]{:S(2)}) collective-permute-start(f32[8,128]{1,0:T(8,128)S(1)} %add.38), channel_id=1, source_target_pairs={{0,16},{4,20},{8,24},{12,28},{16,0},{20,4},{24,8},{28,12},{1,17},{... | collective-permute-start | bytes 12296 | tf_op jit(solution)/shard_map/ppermute | solution.py:46
  (5 other events, 95.0 us)

commit v6 on v5

--- a/solution.py
+++ b/solution.py
@@ -298,7 +298,26 @@
     )(couple, middle, face, *(in_hbm(k) for k in keep))
 
 
-def apply_body(slots_ref, own_ref, from_sub_ref, from_grp_ref, high_ref, low_ref, out_ref, curve_ref, u_high, u_low):
+def one_face(which, slots_ref, face, base, high_ref, low_ref, u_high, u_low, out_ref, acc):
+    _, count, width, _ = high_ref.shape
+    loads, face_width = out_ref.shape
+    half_face = face_width // width // 2
+    slot = slots_ref[0, which]
+    for part in range(half_face):
+        pair = slot * half_face + part
+        high = jnp.concatenate([u_high[2 * pair + i] for i in range(count)], 1)
+        low = jnp.concatenate([u_low[2 * pair + i] for i in range(count)], 1)
+        weight = high_ref[pair].reshape(count * width, 2 * width)
+        both = mm(jnp.concatenate([high, low], 0), weight)
+        result = both[:loads] + both[loads:] + mm(high, low_ref[pair].reshape(count * width, 2 * width))
+        first = 2 * part * width
+        out_ref[:, first : first + 2 * width] = result
+        acc += face[:, base + first : base + first + width] * result[:, :width]
+        acc += face[:, base + first + width : base + first + 2 * width] * result[:, width:]
+    return acc
+
+
+def apply_body(slots_ref, own_ref, from_sub_ref, from_grp_ref, high_ref, low_ref, sub_out, grp_out, acc_out, u_high, u_low):
     pairs, count, width, _ = high_ref.shape
     reach = count // 2 - 1
     face_width = from_sub_ref.shape[1]
@@ -318,41 +337,46 @@
             ref[i] = ref[blocks + i]
         for i in range(reach + 1):
             ref[blocks + reach + i] = ref[reach + i]
-    half_face = per_face // 2
-
     acc = jnp.zeros((loads, width), F32)
-    for which, (ref, base) in enumerate(faces):
-        slot = slots_ref[0, which]
-        for part in range(half_face):
-            pair = slot * half_face + part
-            high = jnp.concatenate([u_high[2 * pair + i] for i in range(count)], 1)
-            low = jnp.concatenate([u_low[2 * pair + i] for i in range(count)], 1)
-            weight = high_ref[pair].reshape(count * width, 2 * width)
-            both = mm(jnp.concatenate([high, low], 0), weight)
-            result = both[:loads] + both[loads:] + mm(high, low_ref[pair].reshape(count * width, 2 * width))
-            first = 2 * part * width
-            out_ref[which, :, first : first + 2 * width] = result
-            acc += ref[:, base + first : base + first + width] * result[:, :width]
-            acc += ref[:, base + first + width : base + first + 2 * width] * result[:, width:]
-    curve_ref[...] = row_sums(acc)
+    acc = one_face(0, slots_ref, from_sub_ref, 0, high_ref, low_ref, u_high, u_low, sub_out, acc)
+    acc_out[...] = one_face(2, slots_ref, from_grp_ref, 0, high_ref, low_ref, u_high, u_low, grp_out, acc)
 
 
 def apply(slots, own, from_sub, from_grp, high, low):
     pairs, count, width, _ = high.shape
     loads, face_width = from_sub.shape
+    face = jax.ShapeDtypeStruct((loads, face_width), F32)
+    kept = jax.ShapeDtypeStruct((2 * pairs + count - 1, loads, width), BF16)
     return call(
         apply_body,
-        (
-            jax.ShapeDtypeStruct((4, loads, face_width), F32),
-            jax.ShapeDtypeStruct((8, loads), F32),
-        ),
-        flops=high.size * loads * 6,
+        (face, face, jax.ShapeDtypeStruct((loads, width), F32), kept, kept),
+        flops=high.size * loads * 3,
         moved=high.size * 4,
-        scratch=[pltpu.VMEM((2 * pairs + count - 1, loads, width), BF16)] * 2,
         in_specs=[SMEM] + [VMEM] * 5,
-        out_specs=(VMEM, VMEM),
+        out_specs=(VMEM,) * 5,
         limit=6 * 1024 * 1024,
     )(slots, own, from_sub, from_grp, high, low)
+
+
+def rest_body(slots_ref, own_ref, acc_ref, u_high, u_low, high_ref, low_ref, sub_out, grp_out, curve_ref):
+    face_width = sub_out.shape[1]
+    acc = one_face(1, slots_ref, own_ref, 0, high_ref, low_ref, u_high, u_low, sub_out, acc_ref[...])
+    acc = one_face(3, slots_ref, own_ref, face_width, high_ref, low_ref, u_high, u_low, grp_out, acc)
+    curve_ref[...] = row_sums(acc)
+
+
+def apply_rest(slots, own, acc, u_high, u_low, high, low):
+    loads = own.shape[0]
+    face = jax.ShapeDtypeStruct((loads, own.shape[1] // 2), F32)
+    return call(
+        rest_body,
+        (face, face, jax.ShapeDtypeStruct((8, loads), F32)),
+        flops=high.size * loads * 3,
+        moved=high.size * 4,
+        in_specs=[SMEM] + [VMEM] * 6,
+        out_specs=(VMEM,) * 3,
+        limit=6 * 1024 * 1024,
+    )(slots, own, acc, u_high, u_low, high, low)
 
 
 def pack_body(per_face, slots_ref, block_ref, basis_ref, factor_ref, sub_ref, grp_ref):
@@ -381,7 +405,7 @@
     )(slots, blocks, basis, factor)
 
 
-def image_body(slots_ref, y_ref, back_sub_ref, back_grp_ref, residual_ref, block_ref, basis_ref, aux_sub_ref, aux_grp_ref, image_out, own_out, sub_out, grp_out):
+def image_body(slots_ref, y_sub_ref, y_grp_ref, back_sub_ref, back_grp_ref, residual_ref, block_ref, basis_ref, aux_sub_ref, aux_grp_ref, image_out, own_out, sub_out, grp_out):
     prims, width = basis_ref.shape
     face_width = back_sub_ref.shape[1]
     per_face = face_width // width
@@ -389,9 +413,9 @@
     loads = residual_ref.shape[0]
     basis = basis_ref[...].astype(F32).T
     own_total = None
-    for which, back, aux, out in (
-        (1, back_sub_ref, aux_sub_ref, sub_out),
-        (3, back_grp_ref, aux_grp_ref, grp_out),
+    for which, y_ref, back, aux, out in (
+        (1, y_sub_ref, back_sub_ref, aux_sub_ref, sub_out),
+        (3, y_grp_ref, back_grp_ref, aux_grp_ref, grp_out),
     ):
         offset = (which // 2) * face_width
         other = aux[rows : rows + prims, :].T
@@ -401,7 +425,7 @@
         for b in range(per_face):
             cols = slice(b * width, (b + 1) * width)
             wide = slice(offset + b * width, offset + (b + 1) * width)
-            image = y_ref[which, :, cols] + back[:, cols]
+            image = y_ref[:, cols] + back[:, cols]
             image_out[:, wide] = image
             image_high, image_low = split(image)
             high, low = split(residual_ref[:, wide])
@@ -420,7 +444,7 @@
     own_out[1] = own_total[loads:] * 0.5
 
 
-def find_image(slots, y, back_sub, back_grp, residual, blocks, basis, aux_sub, aux_grp):
+def find_image(slots, y_sub, y_grp, back_sub, back_grp, residual, blocks, basis, aux_sub, aux_grp):
     loads = residual.shape[0]
     prims = basis.shape[0]
     small = jax.ShapeDtypeStruct((2, loads, prims), F32)
@@ -429,10 +453,10 @@
         (jax.ShapeDtypeStruct(residual.shape, F32), small, small, small),
         flops=residual.size * prims * 16,
         moved=residual.size * 20,
-        in_specs=[SMEM] + [VMEM] * 8,
+        in_specs=[SMEM] + [VMEM] * 9,
         out_specs=(VMEM,) * 4,
         limit=8 * 1024 * 1024,
-    )(slots, y, back_sub, back_grp, residual, blocks, basis, aux_sub, aux_grp)
+    )(slots, y_sub, y_grp, back_sub, back_grp, residual, blocks, basis, aux_sub, aux_grp)
 
 
 def advance_body(image_ref, residual_ref, curve_ref, product_ref, residual_out, half_out):
@@ -668,14 +692,14 @@
     keep = (own, residual[0], coarse_matrix[0], coarse_block_inverse[0], solution[0])
     high, low, own, old, matrix, inverse, iterate = assemble(couple, middle, face, keep)
 
-    y, curve = apply(neighbor_slots, own, from_sub, from_grp, high, low)
-    back_sub = shifted(y[0], "sub", -1)
+    y_sub, y_grp, acc, u_high, u_low = apply(neighbor_slots, own, from_sub, from_grp, high, low)
+    back_sub = shifted(y_sub, "sub", -1)
+    y_sub, kept, curve = apply_rest(neighbor_slots, own, acc, u_high, u_low, high, low)
+    back_grp = shifted(y_grp, "grp", -1)
     curve = total(curve, "grp")
-    lower, curve = lax.optimization_barrier((y[2], curve))
-    back_grp = shifted(lower, "grp", -1)
     curve = total(curve, "sub")
     image, part, part_sub, part_grp = find_image(
-        neighbor_slots, y, back_sub, back_grp, old, blocks, basis, aux_sub, aux_grp
+        neighbor_slots, y_sub, kept, back_sub, back_grp, old, blocks, basis, aux_sub, aux_grp
     )
     part_sub = shifted(part_sub, "sub", 1)
     part_grp = shifted(part_grp, "grp", 1)

time: 110 us -> 107 us (0.973)
  starting transfers between devices: 28.6 us -> 25.8 us
  waiting for transfers between devices: 49.7 us -> 48.2 us
    ppermute x11, waiting for transfers between devices: 19.2 us -> 16.4 us  [shifted(): return lax.ppermute(value, axis, pairs)]
    ppermute x7, starting transfers between devices: 8.64 us -> 6.54 us  [total(): lax.ppermute(value, axis, [(i, i ^ bit) for i in range(count)])]
    ppermute x11, starting transfers between devices: 12 us -> 13.7 us  [shifted(): return lax.ppermute(value, axis, pairs)]
    ppermute x3, starting transfers between devices: 1.73 us -> 0.08 us  [total_with(): lax.ppermute(value, axis, [(i, i ^ bit) for i in range(count)])]
    ppermute x3, waiting for transfers between devices: 7.8 us -> 9.41 us  [total_with(): lax.ppermute(value, axis, [(i, i ^ bit) for i in range(count)])]
    pallas_call x1 -> x2, Pallas kernels: 4.78 us -> 5.58 us  [the longest x1 2.8 us: apply(): call(apply_body, (face, face, jax.ShapeDtypeStruct((loads, width), F32),...]
  transfers between devices with their start and end apart: 26 -> 26, of which waited for: 16 -> 16; matrix products, arithmetic and copies ran while one was open for 0% -> 0% of each run, Pallas kernels for 19% -> 24%
where the time goes in v6:
time: 107 us
  waiting for transfers between devices  48.2 us (45%)
  Pallas kernels  30.4 us (28%)
  starting transfers between devices  25.8 us (24%)
  local copies, waits for them, and re-layouts  1.32 us (1%)
    ppermute x11, waiting for transfers between devices, shifted(): return lax.ppermute(value, axis, pairs)  16.4 us
    ppermute x7, waiting for transfers between devices, total(): lax.ppermute(value, axis, [(i, i ^ bit) for i in range(count)])  16.1 us
    ppermute x11, starting transfers between devices, shifted(): return lax.ppermute(value, axis, pairs)  13.7 us
    ppermute x3, waiting for transfers between devices, total_with(): lax.ppermute(value, axis, [(i, i ^ bit) for i in range(count)])  9.41 us
    pallas_call x1, Pallas kernels, prepare(): call(functools.partial(prepare_body, len(keep)), (jax.ShapeDtypeStruct(co...  7.81 us
    ppermute x7, starting transfers between devices, total(): lax.ppermute(value, axis, [(i, i ^ bit) for i in range(count)])  6.54 us
    ppermute x4, waiting for transfers between devices, sub_window(): pieces.append(lax.ppermute(group, 'sub', list(zip(everyone, target))))  6.3 us
    pallas_call x1, Pallas kernels, assemble(): call(functools.partial(assemble_body, blocks, len(keep)), (shape, shape)...  5.62 us
  transfers between devices with their start and end apart: 26, of which 16 were waited for; matrix products, arithmetic and copies ran while one was open for 0% of the time, Pallas kernels for 24%

profile of v6, /device:TPU:0, one launch (start us, length us, event | category | flops | bytes accessed | tf_op | source)
XLA Modules:
  0.0 106.5 jit_solution(8952591380508543829)
XLA Ops:
  2.0 3.0 %collective-permute-start = (f32[128,1024]{1,0:T(8,128)S(1)}, f32[128,1024]{1,0:T(8,128)S(1)}, u32[]{:S(2)}, u32[]{:S(2)}) collective-permute-start(f32[128,1024]{1,0:T(8,128)S(1)} %get-tuple-element.99), channel_id=1, source_target_pairs={{0,4},{4,8},{8,12},{12,16},{16,20},{20,24},{24,28},{28,0},{1,5},{5... | collective-permute-start | bytes 1572872 | tf_op jit(solution)/shard_map/ppermute | solution.py:23
  5.0 7.8 %shard_map.165 = (bf16[96,256,128]{2,1,0:T(8,128)(2,1)S(1)}, bf16[96,256,256]{2,1,0:T(8,128)(2,1)S(1)}, bf16[32,128,128]{2,1,0:T(8,128)(2,1)S(1)}, bf16[32,128,1...) custom-call(bf16[96,256,128]{2,1,0:T(8,128)(2,1)} %bitcast.22, ...), custom_call_target="tpu_custom_call" | custom-call | flops 2415919104 | bytes 9437184 | tf_op jit(solution)/shard_map/pallas_call | solution.py:194
  13.4 3.2 %collective-permute-start.4 = (f32[1160,128]{1,0:T(8,128)S(1)}, f32[1160,128]{1,0:T(8,128)S(1)}, u32[]{:S(2)}, u32[]{:S(2)}) collective-permute-start(f32[1160,128]{1,0:T(8,128)S(1)} %get-tuple-element.71), channel_id=1, source_target_pairs={{0,28},{4,0},{8,4},{12,8},{16,12},{20,16},{24,20},{28,24},{1,29},{... | collective-permute-start | bytes 1781768 | tf_op jit(solution)/shard_map/ppermute | solution.py:23
  18.0 5.6 %shard_map.167 = (bf16[16,8,128,256]{3,2,1,0:T(8,128)(2,1)S(1)}, bf16[16,8,128,256]{3,2,1,0:T(8,128)(2,1)S(1)}, f32[128,2048]{1,0:T(8,128)S(1)}, f32[128,2048]{1...) custom-call(bf16[96,256,128]{2,1,0:T(8,128)(2,1)S(1)} %get-tuple-element.51.couple_ref,, ...), custom_call_target="tpu_custom_call" | custom-call | flops 2415919104 | bytes 9437184 | tf_op jit(solution)/shard_map/pallas_call | solution.py:285
  23.7 2.8 %shard_map.168 = (f32[128,1024]{1,0:T(8,128)S(1)}, f32[128,1024]{1,0:T(8,128)S(1)}, f32[128,128]{1,0:T(8,128)S(1)}, bf16[39,128,128]{2,1,0:T(8,128)(2,1)S(1)}, bf16[39,128,128]{2,1,0:T(8,128)(2,1)S(1)}) custom-call(s32[1,4]{1,0:T(1,128)S(1)} %copy-done, f32[128,2048]{1,0:T(8,128)S(1)} %get-tuple-element.60.own_ref.direction_ref, ...), custom_call_target="tpu_custom_call" | custom-call | flops 1610612736 | bytes 16777216 | tf_op jit(solution)/shard_map/pallas_call | solution.py:350
  26.5 2.0 %collective-permute-start.2 = (f32[128,1024]{1,0:T(8,128)S(1)}, f32[128,1024]{1,0:T(8,128)S(1)}, u32[]{:S(2)}, u32[]{:S(2)}) collective-permute-start(f32[128,1024]{1,0:T(8,128)S(1)} %get-tuple-element.68), channel_id=1, source_target_pairs={{0,28},{4,0},{8,4},{12,8},{16,12},{20,16},{24,20},{28,24},{1,29},{... | collective-permute-start | bytes 1572872 | tf_op jit(solution)/shard_map/ppermute | solution.py:23
  28.5 2.8 %shard_map.169 = (f32[128,1024]{1,0:T(8,128)S(1)}, f32[128,1024]{1,0:T(8,128)S(1)}, f32[8,128]{1,0:T(8,128)S(1)}) custom-call(s32[1,4]{1,0:T(1,128)S(1)} %copy-done, f32[128,2048]{1,0:T(8,128)S(1)} %get-tuple-element.60.own_ref.direction_ref, f32[128,128]{1,0:T(8,128)S(1)} %get-tuple-element.63.acc_ref, bf16[39,128,128]{2,1,0:T(8,128)(2,1)S(1)} %get-tuple-element.64.u_high, ...), custom_call_target="tpu_custom_call" | custom-call | flops 1610612736 | bytes 16777216 | tf_op jit(solution)/shard_map/pallas_call | solution.py:371
  32.6 11.2 %collective-permute-done.2.back_sub_ref = f32[128,1024]{1,0:T(8,128)S(1)} collective-permute-done((f32[128,1024]{1,0:T(8,128)S(1)}, f32[128,1024]{1,0:T(8,128)S(1)}, u32[]{:S(2)}, u32[]{:S(2)}) %collective-permute-start.2) | collective-permute-done | bytes 524320 | tf_op jit(solution)/shard_map/ppermute | solution.py:23
  48.4 3.2 %collective-permute-done.7 = f32[8,128]{1,0:T(8,128)S(1)} collective-permute-done((f32[8,128]{1,0:T(8,128)S(1)}, f32[8,128]{1,0:T(8,128)S(1)}, u32[]{:S(2)}, u32[]{:S(2)}) %collective-permute-start.7) | collective-permute-done | bytes 4128 | tf_op jit(solution)/shard_map/ppermute | solution.py:32
  51.5 1.7 %collective-permute-start.8 = (f32[8,128]{1,0:T(8,128)S(1)}, f32[8,128]{1,0:T(8,128)S(1)}, u32[]{:S(2)}, u32[]{:S(2)}) collective-permute-start(f32[8,128]{1,0:T(8,128)S(1)} %add.31), channel_id=1, source_target_pairs={{0,16},{4,20},{8,24},{12,28},{16,0},{20,4},{24,8},{28,12},{1,17},{... | collective-permute-start | bytes 12296 | tf_op jit(solution)/shard_map/ppermute | solution.py:32
  53.3 2.8 %collective-permute-done.8 = f32[8,128]{1,0:T(8,128)S(1)} collective-permute-done((f32[8,128]{1,0:T(8,128)S(1)}, f32[8,128]{1,0:T(8,128)S(1)}, u32[]{:S(2)}, u32[]{:S(2)}) %collective-permute-start.8) | collective-permute-done | bytes 4128 | tf_op jit(solution)/shard_map/ppermute | solution.py:32
  56.8 2.9 %collective-permute-done.9 = f32[8,128]{1,0:T(8,128)S(1)} collective-permute-done((f32[8,128]{1,0:T(8,128)S(1)}, f32[8,128]{1,0:T(8,128)S(1)}, u32[]{:S(2)}, u32[]{:S(2)}) %collective-permute-start.9) | collective-permute-done | bytes 4128 | tf_op jit(solution)/shard_map/ppermute | solution.py:32
  60.7 2.5 %collective-permute-done.10 = f32[8,128]{1,0:T(8,128)S(1)} collective-permute-done((f32[8,128]{1,0:T(8,128)S(1)}, f32[8,128]{1,0:T(8,128)S(1)}, u32[]{:S(2)}, u32[]{:S(2)}) %collective-permute-start.10) | collective-permute-done | bytes 4128 | tf_op jit(solution)/shard_map/ppermute | solution.py:32
  64.1 3.8 %collective-permute-done.13 = f32[128,128]{1,0:T(8,128)S(1)} collective-permute-done((f32[128,128]{1,0:T(8,128)S(1)}, f32[128,128]{1,0:T(8,128)S(1)}, u32[]{:S(2)}, u32[]{:S(2)}) %collective-permute-start.13) | collective-permute-done | bytes 65568 | tf_op jit(solution)/shard_map/ppermute | solution.py:23
  69.0 3.6 %collective-permute-start.15 = (f32[2,128,128]{2,1,0:T(8,128)S(1)}, f32[2,128,128]{2,1,0:T(8,128)S(1)}, u32[]{:S(2)}, u32[]{:S(2)}) collective-permute-start(f32[2,128,128]{2,1,0:T(8,128)S(1)} %pad_maximum_fusion.refs_0_), channel_id=1, source_target_pairs={{0,28},{4,8},{8,4},{12,16},{16,12},{20,24},{24,20},{28,0},{1,29},{... | collective-permute-start | bytes 393224 | tf_op jit(solution)/shard_map/ppermute | solution.py:69
  73.3 3.5 %collective-permute-done.15.refs_2_ = f32[2,128,128]{2,1,0:T(8,128)S(1)} collective-permute-done((f32[2,128,128]{2,1,0:T(8,128)S(1)}, f32[2,128,128]{2,1,0:T(8,128)S(1)}, u32[]{:S(2)}, u32[]{:S(2)}) %collective-permute-start.15) | collective-permute-done | bytes 131104 | tf_op jit(solution)/shard_map/ppermute | solution.py:69
  77.7 1.9 %collective-permute-done.17.refs_4_ = f32[2,128,128]{2,1,0:T(8,128)S(1)} collective-permute-done((f32[2,128,128]{2,1,0:T(8,128)S(1)}, f32[2,128,128]{2,1,0:T(8,128)S(1)}, u32[]{:S(2)}, u32[]{:S(2)}) %collective-permute-start.17) | collective-permute-done | bytes 131104 | tf_op jit(solution)/shard_map/ppermute | solution.py:69
  80.9 2.8 %shard_map.172 = (f32[128,2048]{1,0:T(8,128)S(1)}, f32[8,128]{1,0:T(8,128)S(1)}) custom-call(s32[1,4]{1,0:T(1,128)S(1)} %copy-done, f32[128,2048]{1,0:T(8,128)S(1)} %get-tuple-element.75.halved_ref, bf16[32,128,128]{2,1,0:T(8,128)(2,1)S(1)} %get-tuple-element.55.factor_ref, f32[1160,128]{1,0:T(8,128)S(1)} %collective-permute-done.4.aux_sub_ref, ...), custom_call_target="tpu_custom_call" | custom-call | flops 536870912 | bytes 3145728 | tf_op jit(solution)/shard_map/pallas_call | solution.py:593
  87.0 3.2 %collective-permute-done.20 = f32[8,128]{1,0:T(8,128)S(1)} collective-permute-done((f32[8,128]{1,0:T(8,128)S(1)}, f32[8,128]{1,0:T(8,128)S(1)}, u32[]{:S(2)}, u32[]{:S(2)}) %collective-permute-start.20) | collective-permute-done | bytes 4128 | tf_op jit(solution)/shard_map/ppermute | solution.py:32
  90.2 3.3 %collective-permute-start.23 = (f32[128,128]{1,0:T(8,128)S(1)}, f32[128,128]{1,0:T(8,128)S(1)}, u32[]{:S(2)}, u32[]{:S(2)}) collective-permute-start(f32[128,128]{1,0:T(8,128)S(1)} %get-tuple-element.88.own_ref), channel_id=1, source_target_pairs={{0,28},{4,0},{8,4},{12,8},{16,12},{20,16},{24,20},{28,24},{1,29},{... | collective-permute-start | bytes 196616 | tf_op jit(solution)/shard_map/ppermute | solution.py:23
  93.5 3.6 %collective-permute-done.21 = f32[8,128]{1,0:T(8,128)S(1)} collective-permute-done((f32[8,128]{1,0:T(8,128)S(1)}, f32[8,128]{1,0:T(8,128)S(1)}, u32[]{:S(2)}, u32[]{:S(2)}) %collective-permute-start.21) | collective-permute-done | bytes 4128 | tf_op jit(solution)/shard_map/ppermute | solution.py:46
  97.1 3.6 %collective-permute-done.22 = f32[8,128]{1,0:T(8,128)S(1)} collective-permute-done((f32[8,128]{1,0:T(8,128)S(1)}, f32[8,128]{1,0:T(8,128)S(1)}, u32[]{:S(2)}, u32[]{:S(2)}) %collective-permute-start.22) | collective-permute-done | bytes 4128 | tf_op jit(solution)/shard_map/ppermute | solution.py:46
  100.8 2.3 %shard_map.176 = (f32[128,2048]{1,0:T(8,128)S(1)}, f32[128,2048]{1,0:T(8,128)}) custom-call(s32[1,4]{1,0:T(1,128)S(1)} %copy-done, f32[128,2048]{1,0:T(8,128)S(1)} %get-tuple-element.76.solved_ref, f32[128,128]{1,0:T(8,128)S(1)} %get-tuple-element.88.own_ref, f32[128,128]{1,0:T(8,128)S(1)} %collective-permute-done.23.from_sub_ref, ...), custom_call_target="tpu_custom_call" | custom-call | flops 268435456 | bytes 3145728 | tf_op jit(solution)/shard_map/pallas_call | solution.py:627
  103.1 2.2 %collective-permute-done.25 = f32[8,128]{1,0:T(8,128)S(1)} collective-permute-done((f32[8,128]{1,0:T(8,128)S(1)}, f32[8,128]{1,0:T(8,128)S(1)}, u32[]{:S(2)}, u32[]{:S(2)}) %collective-permute-start.25) | collective-permute-done | bytes 4128 | tf_op jit(solution)/shard_map/ppermute | solution.py:46
  (59 shorter events, 20.3 us)
Async XLA Ops:
  2.0 21.7 %collective-permute-start = (f32[128,1024]{1,0:T(8,128)S(1)}, f32[128,1024]{1,0:T(8,128)S(1)}, u32[]{:S(2)}, u32[]{:S(2)}) collective-permute-start(f32[128,1024]{1,0:T(8,128)S(1)} %get-tuple-element.99), channel_id=1, source_target_pairs={{0,4},{4,8},{8,12},{12,16},{16,20},{20,24},{24,28},{28,0},{1,5},{5... | collective-permute-start | bytes 1572872 | tf_op jit(solution)/shard_map/ppermute | solution.py:23
  5.0 18.7 %collective-permute-start.1 = (f32[128,1024]{1,0:T(8,128)S(1)}, f32[128,1024]{1,0:T(8,128)S(1)}, u32[]{:S(2)}, u32[]{:S(2)}) collective-permute-start(f32[128,1024]{1,0:T(8,128)S(1)} %get-tuple-element.98), channel_id=1, source_target_pairs={{0,1},{1,2},{2,3},{3,0},{4,5},{5,6},{6,7},{7,4},{8,9},{9,10},{10,1... | collective-permute-start | bytes 1572872 | tf_op jit(solution)/shard_map/ppermute | solution.py:23
  13.4 19.2 %collective-permute-start.4 = (f32[1160,128]{1,0:T(8,128)S(1)}, f32[1160,128]{1,0:T(8,128)S(1)}, u32[]{:S(2)}, u32[]{:S(2)}) collective-permute-start(f32[1160,128]{1,0:T(8,128)S(1)} %get-tuple-element.71), channel_id=1, source_target_pairs={{0,28},{4,0},{8,4},{12,8},{16,12},{20,16},{24,20},{28,24},{1,29},{... | collective-permute-start | bytes 1781768 | tf_op jit(solution)/shard_map/ppermute | solution.py:23
  16.6 16.0 %collective-permute-start.5 = (f32[1160,128]{1,0:T(8,128)S(1)}, f32[1160,128]{1,0:T(8,128)S(1)}, u32[]{:S(2)}, u32[]{:S(2)}) collective-permute-start(f32[1160,128]{1,0:T(8,128)S(1)} %get-tuple-element.72), channel_id=1, source_target_pairs={{0,3},{1,0},{2,1},{3,2},{4,7},{5,4},{6,5},{7,6},{8,11},{9,8},{10,9... | collective-permute-start | bytes 1781768 | tf_op jit(solution)/shard_map/ppermute | solution.py:23
  26.5 17.3 %collective-permute-start.2 = (f32[128,1024]{1,0:T(8,128)S(1)}, f32[128,1024]{1,0:T(8,128)S(1)}, u32[]{:S(2)}, u32[]{:S(2)}) collective-permute-start(f32[128,1024]{1,0:T(8,128)S(1)} %get-tuple-element.68), channel_id=1, source_target_pairs={{0,28},{4,0},{8,4},{12,8},{16,12},{20,16},{24,20},{28,24},{1,29},{... | collective-permute-start | bytes 1572872 | tf_op jit(solution)/shard_map/ppermute | solution.py:23
  28.5 15.3 %collective-permute-start.3 = (f32[128,1024]{1,0:T(8,128)S(1)}, f32[128,1024]{1,0:T(8,128)S(1)}, u32[]{:S(2)}, u32[]{:S(2)}) collective-permute-start(f32[128,1024]{1,0:T(8,128)S(1)} %get-tuple-element.69), channel_id=1, source_target_pairs={{0,3},{1,0},{2,1},{3,2},{4,7},{5,4},{6,5},{7,6},{8,11},{9,8},{10,9... | collective-permute-start | bytes 1572872 | tf_op jit(solution)/shard_map/ppermute | solution.py:23
  45.3 18.0 %collective-permute-start.11 = (f32[2,128,128]{2,1,0:T(8,128)S(1)}, f32[2,128,128]{2,1,0:T(8,128)S(1)}, u32[]{:S(2)}, u32[]{:S(2)}) collective-permute-start(f32[2,128,128]{2,1,0:T(8,128)S(1)} %get-tuple-element.78), channel_id=1, source_target_pairs={{0,4},{4,8},{8,12},{12,16},{16,20},{20,24},{24,28},{28,0},{1,5},{5... | collective-permute-start | bytes 393224 | tf_op jit(solution)/shard_map/ppermute | solution.py:23
  45.3 17.9 %collective-permute-start.12 = (f32[2,128,128]{2,1,0:T(8,128)S(1)}, f32[2,128,128]{2,1,0:T(8,128)S(1)}, u32[]{:S(2)}, u32[]{:S(2)}) collective-permute-start(f32[2,128,128]{2,1,0:T(8,128)S(1)} %get-tuple-element.79), channel_id=1, source_target_pairs={{0,1},{1,2},{2,3},{3,0},{4,5},{5,6},{6,7},{7,4},{8,9},{9,10},{10,1... | collective-permute-start | bytes 393224 | tf_op jit(solution)/shard_map/ppermute | solution.py:23
  47.9 3.6 %collective-permute-start.7 = (f32[8,128]{1,0:T(8,128)S(1)}, f32[8,128]{1,0:T(8,128)S(1)}, u32[]{:S(2)}, u32[]{:S(2)}) collective-permute-start(f32[8,128]{1,0:T(8,128)S(1)} %add.30), channel_id=1, source_target_pairs={{0,2},{1,3},{2,0},{3,1},{4,6},{5,7},{6,4},{7,5},{8,10},{9,11},{10,... | collective-permute-start | bytes 12296 | tf_op jit(solution)/shard_map/ppermute | solution.py:32
  51.5 4.5 %collective-permute-start.8 = (f32[8,128]{1,0:T(8,128)S(1)}, f32[8,128]{1,0:T(8,128)S(1)}, u32[]{:S(2)}, u32[]{:S(2)}) collective-permute-start(f32[8,128]{1,0:T(8,128)S(1)} %add.31), channel_id=1, source_target_pairs={{0,16},{4,20},{8,24},{12,28},{16,0},{20,4},{24,8},{28,12},{1,17},{... | collective-permute-start | bytes 12296 | tf_op jit(solution)/shard_map/ppermute | solution.py:32
  56.0 3.6 %collective-permute-start.9 = (f32[8,128]{1,0:T(8,128)S(1)}, f32[8,128]{1,0:T(8,128)S(1)}, u32[]{:S(2)}, u32[]{:S(2)}) collective-permute-start(f32[8,128]{1,0:T(8,128)S(1)} %add.32), channel_id=1, source_target_pairs={{0,8},{4,12},{8,0},{12,4},{16,24},{20,28},{24,16},{28,20},{1,9},{5... | collective-permute-start | bytes 12296 | tf_op jit(solution)/shard_map/ppermute | solution.py:32
  59.7 3.6 %collective-permute-start.10 = (f32[8,128]{1,0:T(8,128)S(1)}, f32[8,128]{1,0:T(8,128)S(1)}, u32[]{:S(2)}, u32[]{:S(2)}) collective-permute-start(f32[8,128]{1,0:T(8,128)S(1)} %add.33), channel_id=1, source_target_pairs={{0,4},{4,0},{8,12},{12,8},{16,20},{20,16},{24,28},{28,24},{1,5},{5... | collective-permute-start | bytes 12296 | tf_op jit(solution)/shard_map/ppermute | solution.py:32
  63.5 4.3 %collective-permute-start.13 = (f32[128,128]{1,0:T(8,128)S(1)}, f32[128,128]{1,0:T(8,128)S(1)}, u32[]{:S(2)}, u32[]{:S(2)}) collective-permute-start(f32[128,128]{1,0:T(8,128)S(1)} %get-tuple-element.81.first_ref), channel_id=1, source_target_pairs={{0,2},{1,3},{2,0},{3,1},{4,6},{5,7},{6,4},{7,5},{8,10},{9,11},{10,... | collective-permute-start | bytes 196616 | tf_op jit(solution)/shard_map/ppermute | solution.py:23
  67.9 5.4 %collective-permute-start.14 = (f32[2,128,128]{2,1,0:T(8,128)S(1)}, f32[2,128,128]{2,1,0:T(8,128)S(1)}, u32[]{:S(2)}, u32[]{:S(2)}) collective-permute-start(f32[2,128,128]{2,1,0:T(8,128)S(1)} %pad_maximum_fusion.refs_0_), channel_id=1, source_target_pairs={{0,4},{4,0},{8,12},{12,8},{16,20},{20,16},{24,28},{28,24},{1,5},{5... | collective-permute-start | bytes 393224 | tf_op jit(solution)/shard_map/ppermute | solution.py:69
  69.0 7.8 %collective-permute-start.15 = (f32[2,128,128]{2,1,0:T(8,128)S(1)}, f32[2,128,128]{2,1,0:T(8,128)S(1)}, u32[]{:S(2)}, u32[]{:S(2)}) collective-permute-start(f32[2,128,128]{2,1,0:T(8,128)S(1)} %pad_maximum_fusion.refs_0_), channel_id=1, source_target_pairs={{0,28},{4,8},{8,4},{12,16},{16,12},{20,24},{24,20},{28,0},{1,29},{... | collective-permute-start | bytes 393224 | tf_op jit(solution)/shard_map/ppermute | solution.py:69
  72.7 5.0 %collective-permute-start.16 = (f32[2,128,128]{2,1,0:T(8,128)S(1)}, f32[2,128,128]{2,1,0:T(8,128)S(1)}, u32[]{:S(2)}, u32[]{:S(2)}) collective-permute-start(f32[2,128,128]{2,1,0:T(8,128)S(1)} %pad_maximum_fusion.refs_0_), channel_id=1, source_target_pairs={{0,8},{4,12},{8,0},{12,4},{16,24},{20,28},{24,16},{28,20},{1,9},{5... | collective-permute-start | bytes 393224 | tf_op jit(solution)/shard_map/ppermute | solution.py:69
  72.7 6.9 %collective-permute-start.17 = (f32[2,128,128]{2,1,0:T(8,128)S(1)}, f32[2,128,128]{2,1,0:T(8,128)S(1)}, u32[]{:S(2)}, u32[]{:S(2)}) collective-permute-start(f32[2,128,128]{2,1,0:T(8,128)S(1)} %pad_maximum_fusion.refs_0_), channel_id=1, source_target_pairs={{0,24},{4,28},{8,16},{12,20},{16,8},{20,12},{24,0},{28,4},{1,25},{... | collective-permute-start | bytes 393224 | tf_op jit(solution)/shard_map/ppermute | solution.py:69
  79.6 4.0 %collective-permute-start.18 = (f32[10,128,128]{2,1,0:T(8,128)S(1)}, f32[10,128,128]{2,1,0:T(8,128)S(1)}, u32[]{:S(2)}, u32[]{:S(2)}) collective-permute-start(f32[10,128,128]{2,1,0:T(8,128)S(1)} %shard_map.174.window_ref), channel_id=1, source_target_pairs={{0,1},{1,0},{2,3},{3,2},{4,5},{5,4},{6,7},{7,6},{8,9},{9,8},{10,11... | collective-permute-start | bytes 1966088 | tf_op jit(solution)/shard_map/ppermute | solution.py:718
  86.6 3.6 %collective-permute-start.20 = (f32[8,128]{1,0:T(8,128)S(1)}, f32[8,128]{1,0:T(8,128)S(1)}, u32[]{:S(2)}, u32[]{:S(2)}) collective-permute-start(f32[8,128]{1,0:T(8,128)S(1)} %add.35), channel_id=1, source_target_pairs={{0,2},{1,3},{2,0},{3,1},{4,6},{5,7},{6,4},{7,5},{8,10},{9,11},{10,... | collective-permute-start | bytes 12296 | tf_op jit(solution)/shard_map/ppermute | solution.py:32
  90.2 10.5 %collective-permute-start.23 = (f32[128,128]{1,0:T(8,128)S(1)}, f32[128,128]{1,0:T(8,128)S(1)}, u32[]{:S(2)}, u32[]{:S(2)}) collective-permute-start(f32[128,128]{1,0:T(8,128)S(1)} %get-tuple-element.88.own_ref), channel_id=1, source_target_pairs={{0,28},{4,0},{8,4},{12,8},{16,12},{20,16},{24,20},{28,24},{1,29},{... | collective-permute-start | bytes 196616 | tf_op jit(solution)/shard_map/ppermute | solution.py:23
  93.5 7.2 %collective-permute-start.24 = (f32[128,128]{1,0:T(8,128)S(1)}, f32[128,128]{1,0:T(8,128)S(1)}, u32[]{:S(2)}, u32[]{:S(2)}) collective-permute-start(f32[128,128]{1,0:T(8,128)S(1)} %get-tuple-element.88.own_ref), channel_id=1, source_target_pairs={{0,3},{1,0},{2,1},{3,2},{4,7},{5,4},{6,5},{7,6},{8,11},{9,8},{10,9... | collective-permute-start | bytes 196616 | tf_op jit(solution)/shard_map/ppermute | solution.py:23
  93.5 3.6 %collective-permute-start.21 = (f32[8,128]{1,0:T(8,128)S(1)}, f32[8,128]{1,0:T(8,128)S(1)}, u32[]{:S(2)}, u32[]{:S(2)}) collective-permute-start(f32[8,128]{1,0:T(8,128)S(1)} %add.36), channel_id=1, source_target_pairs={{0,4},{4,0},{8,12},{12,8},{16,20},{20,16},{24,28},{28,24},{1,5},{5... | collective-permute-start | bytes 12296 | tf_op jit(solution)/shard_map/ppermute | solution.py:46
  97.1 3.6 %collective-permute-start.22 = (f32[8,128]{1,0:T(8,128)S(1)}, f32[8,128]{1,0:T(8,128)S(1)}, u32[]{:S(2)}, u32[]{:S(2)}) collective-permute-start(f32[8,128]{1,0:T(8,128)S(1)} %add.37), channel_id=1, source_target_pairs={{0,8},{4,12},{8,0},{12,4},{16,24},{20,28},{24,16},{28,20},{1,9},{5... | collective-permute-start | bytes 12296 | tf_op jit(solution)/shard_map/ppermute | solution.py:46
  100.7 4.6 %collective-permute-start.25 = (f32[8,128]{1,0:T(8,128)S(1)}, f32[8,128]{1,0:T(8,128)S(1)}, u32[]{:S(2)}, u32[]{:S(2)}) collective-permute-start(f32[8,128]{1,0:T(8,128)S(1)} %add.38), channel_id=1, source_target_pairs={{0,16},{4,20},{8,24},{12,28},{16,0},{20,4},{24,8},{28,12},{1,17},{... | collective-permute-start | bytes 12296 | tf_op jit(solution)/shard_map/ppermute | solution.py:46
  (5 other events, 101.7 us)
